TPU v7x, 128 devices: a whole 4x4x4 slice. The times are simulated.
128 devices in a mesh: slab: 4 (over y_hi, core), pencil: 32 (over y_lo, x, z).
Axes of the slice: x: 4, y: 4 (y_hi: 2, y_lo: 2; y = y_hi * 2 + y_lo), z: 4, core: 2. Of those that a mesh axis runs over, the one named last changes fastest.
Arguments:
- density: float32 [512, 768, 512], P('pencil', None, 'slab'), may hold values from -6 to 6
- source: float32 [512, 768, 512], P('pencil', None, 'slab'), may hold values from -6 to 8
- coupling: float32 [3], replicated, may hold values from 0.25 to 2, as said below
- width_inverse: float32 [6, 128, 128], replicated, as said below
- height_inverse: float32 [4, 128, 128], replicated, as said below
- depth_inverse: float32 [4, 128, 128], replicated, as said below
Outputs:
- stepped: float32 [512, 768, 512], P('pencil', None, 'slab')
Inputs may be any that keep to these rules, and one draw needn't show every extreme that they name: coupling holds three positive coefficients. `width_inverse`: block i is the inverse of the i-th pivot block of the block LU factorization of the tridiagonal line matrix with diagonal 1 + 2 s and off-diagonals -s, s the matching coupling. `height_inverse`: as for width_inverse, for the height lines. `depth_inverse`: as for width_inverse, for the depth lines.
All inputs are finite; a program needn't handle non-finite values.
Results may differ from a plain program's by a relative error of at most 0.00027.
Values sent between devices are 32-bit elements; how exact they have to be, the bound alone decides.
No kernel may reach another device: no remote copies, remote signals or barrier semaphores. Data moves between devices by JAX's collectives and lax.ppermute only.
A program may use at most 128 MiB of HBM per device.

v0:
```python
import jax
import jax.numpy as jnp
from jax import lax
from jax.sharding import PartitionSpec as P


def extended(value, sides, width):
    edges = {}
    for axis, dim in sides:
        count, length = (lax.axis_size(axis), value.shape[dim])
        up = [(i, (i + 1) % count) for i in range(count - 1)]
        last = lax.slice_in_dim(value, length - width, length, axis=dim)
        leading = lax.slice_in_dim(value, 0, width, axis=dim)
        edges[dim] = (
            lax.ppermute(last, axis, up),
            lax.ppermute(leading, axis, [(b, a) for a, b in up]),
        )
    done = []
    for _, dim in sides:
        low, high = edges[dim]
        around = [(width, width) if d in done else (0, 0) for d in range(value.ndim)]
        value = jnp.concatenate([jnp.pad(low, around), value, jnp.pad(high, around)], axis=dim)
        done.append(dim)
    return value


def from_everyone(value, axis):
    count = lax.axis_size(axis)
    return lax.all_to_all(
        jnp.broadcast_to(value[None], (count, *value.shape)), axis, 0, 0, tiled=True
    )


def collected_together(value, axis):
    leaves = jax.tree.leaves(value)
    turns = sorted(range(len(leaves)), key=lambda k: -leaves[k].size)
    width = (1, *leaves[turns[0]].shape)[-1]
    lines = [
        jnp.pad(leaves[k].reshape(-1), (0, -leaves[k].size % width)).reshape(-1, width)
        for k in turns
    ]
    both, at, found = (from_everyone(jnp.concatenate(lines), axis), 0, {})
    for k, line in zip(turns, lines):
        share = both[:, at : at + len(line)].reshape(len(both), -1)
        found[k] = share[:, : leaves[k].size].reshape(-1, *leaves[k].shape)
        at += len(line)
    numbers = iter(range(len(leaves)))
    return jax.tree.map(lambda _: found[next(numbers)], value)


def combined_pairwise(pieces, combine):
    while len(jax.tree.leaves(pieces)[0]) > 1:
        pieces = jax.vmap(combine)(
            *(jax.tree.map(lambda part: part[side::2], pieces) for side in (0, 1))
        )
    return jax.tree.map(lambda part: part[0], pieces)


def entering(value, axis, combine, identity):
    count, place = (lax.axis_size(axis), lax.axis_index(axis))
    passed = jnp.arange(count) < place

    def kept(part, zero, own):
        part = jnp.where(
            passed.reshape(-1, *(1 for _ in own.shape)), part, jnp.asarray(zero, own.dtype)
        )
        return part

    pieces = collected_together(value, axis)
    return combined_pairwise(jax.tree.map(kept, pieces, identity, value), combine)


def once_a_type(value, axis):
    leaves, found = (jax.tree.leaves(value), {})
    for leading, a in enumerate(leaves):
        if leading not in found:
            alike = [k for k, b in enumerate(leaves) if b.dtype == a.dtype]
            got = (
                collected_together([leaves[k] for k in alike], axis)
                if len(alike) > 1
                else [from_everyone(a, axis)]
            )
            for k, b in zip(alike, got):
                found[k] = b
    numbers = iter(range(len(leaves)))
    return jax.tree.map(lambda _: found[next(numbers)], value)


def entering_2(value, axis, combine, identity):
    count, place = (lax.axis_size(axis), lax.axis_index(axis))
    passed = jnp.arange(count) > place

    def kept(part, zero, own):
        part = jnp.where(
            passed.reshape(-1, *(1 for _ in own.shape)), part, jnp.asarray(zero, own.dtype)
        )
        return part[::-1]

    pieces = once_a_type(value, axis)
    return combined_pairwise(jax.tree.map(kept, pieces, identity, value), combine)


def solve_inner(rhs, inverses, strength):
    outer, length, inner = rhs.shape
    size = inverses.shape[1]
    count = length // size
    blocked = rhs.reshape(outer, count, size, inner)

    def forward(current, state):
        result, carry = state
        piece = lax.dynamic_index_in_dim(blocked, current, 1, keepdims=False)
        matrix = lax.dynamic_index_in_dim(inverses, current, 0, keepdims=False)
        value = jnp.einsum("pkq,jk->pjq", piece, matrix, precision=lax.Precision.HIGHEST)
        value = value + strength * matrix[:, 0][None, :, None] * carry[:, None, :]
        result = lax.dynamic_update_index_in_dim(result, value, current, 1)
        return (result, value[:, size - 1, :])

    start = (jnp.zeros_like(blocked), jnp.zeros((outer, inner), blocked.dtype))
    halfway, unused = lax.fori_loop(0, count, forward, start)

    def backward(step, state):
        result, carry = state
        current = count - 1 - step
        value = lax.dynamic_index_in_dim(result, current, 1, keepdims=False)
        matrix = lax.dynamic_index_in_dim(inverses, current, 0, keepdims=False)
        value = value + strength * matrix[:, size - 1][None, :, None] * carry[:, None, :]
        result = lax.dynamic_update_index_in_dim(result, value, current, 1)
        return (result, value[:, 0, :])

    final, unused = lax.fori_loop(
        0, count, backward, (halfway, jnp.zeros((outer, inner), blocked.dtype))
    )
    return final.reshape(outer, length, inner)


def affine_combine(earlier, later):
    return (later[0] * earlier[0], later[0] * earlier[1] + later[1])


def per_device(density, source, coupling, width_inverse, height_inverse, depth_inverse):
    padded = extended(density, (("slab", 2), ("pencil", 0)), 1)
    center = padded[1:-1, :, 1:-1]
    along_height = padded[2:, :, 1:-1] + padded[:-2, :, 1:-1] - 2.0 * center
    along_depth = padded[1:-1, :, 2:] + padded[1:-1, :, :-2] - 2.0 * center
    width_padded = jnp.pad(density, ((0, 0), (1, 1), (0, 0)))
    along_width = width_padded[:, 2:, :] + width_padded[:, :-2, :] - 2.0 * density
    explicit = (
        2.0 * (coupling[0] * along_width + coupling[1] * along_height + coupling[2] * along_depth)
        + source
    )
    width_step = solve_inner(explicit, width_inverse, coupling[0])
    piece = lax.all_to_all(width_step, "pencil", split_axis=1, concat_axis=0, tiled=True)
    height_step = solve_inner(
        piece.reshape(1, piece.shape[0], -1), height_inverse, coupling[1]
    ).reshape(piece.shape)
    size = depth_inverse.shape[1]
    strength = coupling[2]
    matrix = lax.dynamic_index_in_dim(depth_inverse, lax.axis_index("slab"), 0, keepdims=False)
    local_value = jnp.einsum("yxk,jk->yxj", height_step, matrix, precision=lax.Precision.HIGHEST)
    forward_factor = jnp.reshape(strength * matrix[size - 1, 0], (1, 1))
    unit = jnp.ones((1, 1), local_value.dtype)
    zero_rows = jnp.zeros(local_value.shape[:2], local_value.dtype)
    unused, carry_in = entering(
        (forward_factor, local_value[:, :, size - 1]), "slab", affine_combine, (unit, zero_rows)
    )
    forward_value = local_value + strength * matrix[:, 0][None, None, :] * carry_in[:, :, None]
    backward_factor = jnp.reshape(strength * matrix[0, size - 1], (1, 1))
    unused, carry_next = entering_2(
        (backward_factor, forward_value[:, :, 0]), "slab", affine_combine, (unit, zero_rows)
    )
    depth_step = (
        forward_value + strength * matrix[:, size - 1][None, None, :] * carry_next[:, :, None]
    )
    increment = lax.all_to_all(depth_step, "pencil", split_axis=0, concat_axis=1, tiled=True)
    return density + increment


def solution(mesh):
    in_specs = (P("pencil", None, "slab"), P("pencil", None, "slab"), P(), P(), P(), P())
    out_specs = P("pencil", None, "slab")
    return jax.shard_map(
        per_device, mesh=mesh, in_specs=in_specs, out_specs=out_specs, check_vma=False
    )
```

profile of v0, /device:TPU:1, one launch (start us, length us, event | category | flops | bytes accessed | tf_op | source)
XLA Modules:
  0.0 415.8 jit_solution(17377647225624506018)
XLA Ops:
  2.5 5.0 %collective-permute-start.3 = (f32[1,768,128]{2,1,0:T(8,128)S(1)}, f32[1,768,128]{2,1,0:T(8,128)S(1)}, u32[]{:S(2)}, u32[]{:S(2)}) collective-permute-start(f32[1,768,128]{2,1,0:T(8,128)S(1)} %get-tuple-element.650), channel_id=1, source_target_pairs={{0,1},{1,2},{2,3},{3,4},{4,5},{5,6},{6,7},{7,8},{8,9},{9,10},{10,1... | collective-permute-start | bytes 1179656 | tf_op jit(solution)/shard_map/ppermute | solution.py:15
  7.5 11.1 %fusion.38 = (f32[16,768,1]{2,1,0:T(8,128)}, f32[16,768,1]{2,1,0:T(8,128)}) fusion(f32[16,768,128]{2,1,0:T(8,128)} %param.14), kind=kLoop, calls=%fused_computation.97 | loop fusion | bytes 196608 | tf_op jit(solution)/shard_map/slice | solution.py:13
  18.7 4.4 %copy.97 = f32[16,768,1]{1,0,2:T(8,128)S(1)} copy(f32[16,768,1]{2,1,0:T(8,128)} %get-tuple-element.652) | data formatting | bytes 98304
  23.1 5.8 %collective-permute-start = (f32[16,768,1]{1,0,2:T(8,128)S(1)}, f32[16,768,1]{1,0,2:T(8,128)S(1)}, u32[]{:S(2)}, u32[]{:S(2)}) collective-permute-start(f32[16,768,1]{1,0,2:T(8,128)S(1)} %copy.97), channel_id=1, source_target_pairs={{0,32},{32,64},{64,96},{1,33},{33,65},{65,97},{2,34},{34,66},{66,9... | collective-permute-start | bytes 147464 | tf_op jit(solution)/shard_map/ppermute | solution.py:15
  28.9 4.4 %copy.98 = f32[16,768,1]{1,0,2:T(8,128)S(1)} copy(f32[16,768,1]{2,1,0:T(8,128)} %get-tuple-element.651) | data formatting | bytes 98304
  36.1 4.0 copy.73
  40.2 3.9 copy.74
  44.1 30.6 %fusion.20 = f32[16,768,128]{2,1,0:T(8,128)} fusion(f32[16,768,128]{2,1,0:T(8,128)} %param.15, f32[16,768,128]{2,1,0:T(8,128)} %param.14, f32[16,768,1]{2,1,0:T(8,128)} %copy.73, f32[16,768,1]{2,1,0:T(8,128)} %copy.74, f32[1,768,128]{2,1,0:T(8,128)S(1)} %collective-permute-done.3, f32[1,768,128]{2,1,0:T(8,128)S(1)} %collective-permute-done.2, f32[]{:T(128)} %bitcast.24, ...), kind=kLoop, calls=%fused_computation.41 | loop fusion | flops 44040192 | bytes 19759116 | tf_op jit(solution)/shard_map/add | solution.py:148
  74.8 24.1 %while.64 = (s32[]{:T(128)}, f32[16,6,128,128]{3,2,1,0:T(8,128)}, f32[16,128]{1,0:T(8,128)S(1)}, f32[6,128,128]{2,1,0:T(8,128)S(1)}, f32[16,6,128,128]{3,2,1,0:T(8,128)}, /*index=5*/f32[]{:T(128)}, s32[]{:T(128)}) while((s32[]{:T(128)}, f32[16,6,128,128]{3,2,1,0:T(8,128)}, f32[16,128]{1,0:T(8,128)S(1)}, f32[6,128,128]{2,1,0:T(8,128)S(1)}, ...), condition=%wide.region_1.2_spmd, body=%wide.region_0.1_spmd.sunk | while | flops 403177600 | bytes 3370069 | solution.py:119
  75.5 3.2 bitcast_dynamic-update-slice_fusion.4
  79.6 3.2 bitcast_dynamic-update-slice_fusion.4
  83.6 3.2 bitcast_dynamic-update-slice_fusion.4
  87.6 3.2 bitcast_dynamic-update-slice_fusion.4
  91.6 3.2 bitcast_dynamic-update-slice_fusion.4
  95.7 3.2 bitcast_dynamic-update-slice_fusion.4
  98.9 23.1 %while.65 = (s32[]{:T(128)}, f32[16,6,128,128]{3,2,1,0:T(8,128)}, f32[16,128]{1,0:T(8,128)S(1)}, f32[]{:T(128)}, f32[6,128,128]{2,1,0:T(8,128)S(1)}, /*index=5*/s32[]{:T(128)}, s32[]{:T(128)}, s32[]{:T(128)}, s32[]{:T(128)}) while((s32[]{:T(128)}, f32[16,6,128,128]{3,2,1,0:T(8,128)}, f32[16,128]{1,0:T(8,128)S(1)}, f32[]{:T(128)}, ...), condition=%wide.region_3.4_spmd, body=%wide.region_2.3_spmd.sunk | while | flops 528518 | bytes 5555867 | solution.py:130
  99.7 2.4 constant_dynamic-slice_fusion.5
  103.6 2.4 constant_dynamic-slice_fusion.5
  107.4 2.4 constant_dynamic-slice_fusion.5
  111.3 2.4 constant_dynamic-slice_fusion.5
  115.1 2.4 constant_dynamic-slice_fusion.5
  122.0 9.0 %copy.80 = f32[16,6,128,128]{3,0,2,1:T(8,128)} copy(f32[16,6,128,128]{3,2,1,0:T(8,128)} %get-tuple-element.488) | data formatting | bytes 12582912 | tf_op jit(solution)/shard_map/while | solution.py:130
  131.0 12.3 %all-to-all-start = ((f32[16,768,128]{2,0,1:T(8,128)}), f32[16,768,128]{2,0,1:T(8,128)}, u32[]{:S(2)}, u32[]{:S(2)}) async-start(f32[16,768,128]{2,0,1:T(8,128)} %bitcast.163), calls=%async_computation | async-start | bytes 12582912 | tf_op jit(solution)/shard_map/all_to_all | solution.py:152
  147.0 76.9 %all-to-all-done = f32[16,768,128]{2,0,1:T(8,128)} async-done(((f32[16,768,128]{2,0,1:T(8,128)}), f32[16,768,128]{2,0,1:T(8,128)}, u32[]{:S(2)}, u32[]{:S(2)}) %all-to-all-start) | async-done | bytes 6291488 | tf_op jit(solution)/shard_map/all_to_all | solution.py:152
  223.8 8.0 %copy.82 = f32[32,16,24,128]{3,2,1,0:T(8,128)} copy(f32[32,16,24,128]{3,1,2,0:T(8,128)} %bitcast.29) | data formatting | bytes 12582912 | tf_op jit(solution)/shard_map/all_to_all | solution.py:152
  231.9 7.2 %reshape_reshape.12 = f32[1,4,128,3072]{3,2,1,0:T(8,128)} reshape(f32[32,16,24,128]{3,2,1,0:T(8,128)} %copy.82) | data formatting | bytes 12582912 | tf_op jit(solution)/shard_map/reshape;reshape | solution.py:107
  239.0 19.0 %while.66 = (s32[]{:T(128)}, f32[1,4,128,3072]{3,2,1,0:T(8,128)}, f32[1,3072]{1,0:T(1,128)S(1)}, f32[4,128,128]{1,2,0:T(8,128)S(1)}, f32[1,4,128,3072]{3,2,1,0:T(8,128)}, /*index=5*/f32[]{:T(128)}, s32[]{:T(128)}) while((s32[]{:T(128)}, f32[1,4,128,3072]{3,2,1,0:T(8,128)}, f32[1,3072]{1,0:T(1,128)S(1)}, f32[4,128,128]{1,2,0:T(8,128)S(1)}, ...), condition=%wide.region_5.6_spmd, body=%wide.region_4.5_spmd.sunk | while | flops 604766336 | bytes 4955221 | solution.py:119
  239.7 4.1 bitcast_dynamic-update-slice_fusion.5
  244.4 4.1 bitcast_dynamic-update-slice_fusion.5
  249.2 4.1 bitcast_dynamic-update-slice_fusion.5
  253.9 4.1 bitcast_dynamic-update-slice_fusion.5
  258.0 14.3 %while.67 = (s32[]{:T(128)}, f32[1,4,128,3072]{3,2,1,0:T(8,128)}, f32[1,3072]{1,0:T(1,128)S(1)}, f32[]{:T(128)}, f32[4,128,128]{1,2,0:T(8,128)S(1)}, /*index=5*/s32[]{:T(128)}, s32[]{:T(128)}, s32[]{:T(128)}, s32[]{:T(128)}) while((s32[]{:T(128)}, f32[1,4,128,3072]{3,2,1,0:T(8,128)}, f32[1,3072]{1,0:T(1,128)S(1)}, f32[]{:T(128)}, ...), condition=%wide.region_7.8_spmd, body=%wide.region_6.7_spmd.sunk | while | flops 792710 | bytes 4925083 | solution.py:130
  258.7 2.8 dynamic-slice_bitcast_fusion.13
  262.3 2.8 dynamic-slice_bitcast_fusion.13
  265.9 2.8 dynamic-slice_bitcast_fusion.13
  269.5 2.8 dynamic-slice_bitcast_fusion.13
  272.4 4.2 %copy.104 = f32[64,8,24,128]{3,2,1,0:T(8,128)S(1)} copy(f32[64,8,24,128]{3,1,2,0:T(8,128)} %bitcast.161) | data formatting | bytes 12582912
  276.5 6.5 %fusion.28 = f32[512,24,128]{0,2,1:T(8,128)S(1)} fusion(f32[512,24,128]{2,1,0:T(8,128)S(1)} %bitcast.164, f32[4,128,128]{2,1,0:T(8,128)S(1)} %copy-done, s32[]{:T(128)S(6)} %select_n.84), kind=kOutput, calls=%fused_computation.60 | convolution fusion | flops 2415919104 | bytes 12648452 | tf_op jit(solution)/shard_map/yxk,jk->yxj/dot_general | solution.py:159
  283.0 2.7 copy-done.1
  286.5 7.8 %all-to-all-start.1 = ((f32[4,513,24]{1,2,0:T(8,128)}), f32[4,513,24]{1,2,0:T(8,128)S(1)}, u32[]{:S(2)}, u32[]{:S(2)}) async-start(f32[4,513,24]{1,2,0:T(8,128)} %broadcast_in_dim.80), calls=%async_computation.1 | async-start | bytes 491520 | tf_op jit(solution)/shard_map/all_to_all | solution.py:29
  295.3 5.4 %all-to-all-done.1 = f32[4,513,24]{1,2,0:T(8,128)S(1)} async-done(((f32[4,513,24]{1,2,0:T(8,128)}), f32[4,513,24]{1,2,0:T(8,128)S(1)}, u32[]{:S(2)}, u32[]{:S(2)}) %all-to-all-start.1) | async-done | bytes 197024 | tf_op jit(solution)/shard_map/all_to_all | solution.py:29
  302.6 3.7 multiply_add_fusion.1
  307.1 4.3 %all-to-all-start.2 = ((f32[4,513,24]{1,2,0:T(8,128)}), f32[4,513,24]{1,2,0:T(8,128)S(1)}, u32[]{:S(2)}, u32[]{:S(2)}) async-start(f32[4,513,24]{1,2,0:T(8,128)} %broadcast_in_dim.84), calls=%async_computation.2 | async-start | bytes 491520 | tf_op jit(solution)/shard_map/all_to_all | solution.py:29
  311.4 6.4 %all-to-all-done.2 = f32[4,513,24]{1,2,0:T(8,128)S(1)} async-done(((f32[4,513,24]{1,2,0:T(8,128)}), f32[4,513,24]{1,2,0:T(8,128)S(1)}, u32[]{:S(2)}, u32[]{:S(2)}) %all-to-all-start.2) | async-done | bytes 197024 | tf_op jit(solution)/shard_map/all_to_all | solution.py:29
  319.8 6.8 %multiply_add_fusion = f32[512,24,128]{0,2,1:T(8,128)} fusion(f32[512,24]{0,1:T(8,128)S(1)} %fusion.34, f32[128]{0:T(128)S(1)} %get-tuple-element.595, f32[512,24,128]{0,2,1:T(8,128)} %copy-done.1, f32[512,24]{0,1:T(8,128)S(1)} %fusion.35, f32[128]{0:T(128)S(1)} %get-tuple-element.596), kind=kLoop, calls=%fused_computation.62 | loop fusion | flops 6291456 | bytes 12682240 | tf_op jit(solution)/shard_map/add | solution.py:172
  326.7 6.6 %copy.88 = f32[512,24,128]{2,1,0:T(8,128)} copy(f32[512,24,128]{0,2,1:T(8,128)} %multiply_add_fusion) | data formatting | bytes 12582912 | tf_op jit(solution)/shard_map/add | solution.py:172
  333.2 77.6 %all_to_all.43 = f32[512,24,128]{2,1,0:T(8,128)S(1)} all-to-all(f32[512,24,128]{2,1,0:T(8,128)} %copy.88), channel_id=1, replica_groups=mesh['slab'=4,'pencil'=32] {'pencil'}, dimensions={0} | all-to-all | bytes 12582912 | tf_op jit(solution)/shard_map/all_to_all | solution.py:174
  412.4 3.4 bitcast_add_fusion
  (153 shorter events, 34.8 us)
Async XLA Ops:
  0.0 143.5 %copy-start = (f32[4,128,128]{2,1,0:T(8,128)S(1)}, f32[4,128,128]{2,1,0:T(8,128)}, u32[]{:S(2)}) copy-start(f32[4,128,128]{2,1,0:T(8,128)} %param.19) | copy-start | bytes 786436
  1.2 42.9 %collective-permute-start.2 = (f32[1,768,128]{2,1,0:T(8,128)S(1)}, f32[1,768,128]{2,1,0:T(8,128)S(1)}, u32[]{:S(2)}, u32[]{:S(2)}) collective-permute-start(f32[1,768,128]{2,1,0:T(8,128)S(1)} %get-tuple-element.649), channel_id=1, source_target_pairs={{1,0},{2,1},{3,2},{4,3},{5,4},{6,5},{7,6},{8,7},{9,8},{10,9},{11,1... | collective-permute-start | bytes 1179656 | tf_op jit(solution)/shard_map/ppermute | solution.py:16
  2.5 41.6 %collective-permute-start.3 = (f32[1,768,128]{2,1,0:T(8,128)S(1)}, f32[1,768,128]{2,1,0:T(8,128)S(1)}, u32[]{:S(2)}, u32[]{:S(2)}) collective-permute-start(f32[1,768,128]{2,1,0:T(8,128)S(1)} %get-tuple-element.650), channel_id=1, source_target_pairs={{0,1},{1,2},{2,3},{3,4},{4,5},{5,6},{6,7},{7,8},{8,9},{9,10},{10,1... | collective-permute-start | bytes 1179656 | tf_op jit(solution)/shard_map/ppermute | solution.py:15
  18.7 16.7 %copy-start.4 = (f32[3]{0:T(128)S(1)}, f32[3]{0:T(128)}, u32[]{:S(2)}) copy-start(f32[3]{0:T(128)} %param.16) | copy-start | bytes 40
  23.1 13.0 %collective-permute-start = (f32[16,768,1]{1,0,2:T(8,128)S(1)}, f32[16,768,1]{1,0,2:T(8,128)S(1)}, u32[]{:S(2)}, u32[]{:S(2)}) collective-permute-start(f32[16,768,1]{1,0,2:T(8,128)S(1)} %copy.97), channel_id=1, source_target_pairs={{0,32},{32,64},{64,96},{1,33},{33,65},{65,97},{2,34},{34,66},{66,9... | collective-permute-start | bytes 147464 | tf_op jit(solution)/shard_map/ppermute | solution.py:15
  33.3 6.9 %collective-permute-start.1 = (f32[16,768,1]{1,0,2:T(8,128)S(1)}, f32[16,768,1]{1,0,2:T(8,128)S(1)}, u32[]{:S(2)}, u32[]{:S(2)}) collective-permute-start(f32[16,768,1]{1,0,2:T(8,128)S(1)} %copy.98), channel_id=1, source_target_pairs={{32,0},{64,32},{96,64},{33,1},{65,33},{97,65},{34,2},{66,34},{98,6... | collective-permute-start | bytes 147464 | tf_op jit(solution)/shard_map/ppermute | solution.py:16
  44.1 30.6 %copy-start.2 = (f32[6,128,128]{2,1,0:T(8,128)S(1)}, f32[6,128,128]{2,1,0:T(8,128)}, u32[]{:S(2)}) copy-start(f32[6,128,128]{2,1,0:T(8,128)} %param.17) | copy-start | bytes 1179652
  131.0 12.3 %copy-start.3 = (f32[4,128,128]{2,1,0:T(8,128)S(1)}, f32[4,128,128]{2,1,0:T(8,128)}, u32[]{:S(2)}) copy-start(f32[4,128,128]{2,1,0:T(8,128)} %param.18) | copy-start | bytes 786436
  131.0 92.8 %all-to-all-start = ((f32[16,768,128]{2,0,1:T(8,128)}), f32[16,768,128]{2,0,1:T(8,128)}, u32[]{:S(2)}, u32[]{:S(2)}) async-start(f32[16,768,128]{2,0,1:T(8,128)} %bitcast.163), calls=%async_computation | async-start | bytes 12582912 | tf_op jit(solution)/shard_map/all_to_all | solution.py:152
  283.0 2.7 copy-start.1
  286.5 14.2 %all-to-all-start.1 = ((f32[4,513,24]{1,2,0:T(8,128)}), f32[4,513,24]{1,2,0:T(8,128)S(1)}, u32[]{:S(2)}, u32[]{:S(2)}) async-start(f32[4,513,24]{1,2,0:T(8,128)} %broadcast_in_dim.80), calls=%async_computation.1 | async-start | bytes 491520 | tf_op jit(solution)/shard_map/all_to_all | solution.py:29
  307.1 10.7 %all-to-all-start.2 = ((f32[4,513,24]{1,2,0:T(8,128)}), f32[4,513,24]{1,2,0:T(8,128)S(1)}, u32[]{:S(2)}, u32[]{:S(2)}) async-start(f32[4,513,24]{1,2,0:T(8,128)} %broadcast_in_dim.84), calls=%async_computation.2 | async-start | bytes 491520 | tf_op jit(solution)/shard_map/all_to_all | solution.py:29
  333.2 78.2 %slice-start = ((s8[6291456]{0:T(1024)(128)(4,1)}), s8[4194304]{0:T(1024)(128)(4,1)S(1)}, s32[]{:S(2)}) async-start(s8[6291456]{0:T(1024)(128)(4,1)} %bitcast.158), calls=%async_computation.4 | async-start | bytes 8388608
  410.8 1.6 slice-start.1
where the time goes:
time: 419 us; the launch traced here: 416 us
  waiting for transfers between devices  88.8 us (21%)
  other arithmetic  86.4 us (21%)
  local copies, waits for them, and re-layouts  78.2 us (19%)
  blocking collectives  77.6 us (19%)
  matrix products  42.2 us (10%)
  starting transfers between devices  38.6 us (9%)
    all_to_all x1, blocking collectives, per_device(): lax.all_to_all(depth_step, 'pencil', split_axis=0, concat_axis=1, tiled=T...  77.6 us
    all_to_all x1, waiting for transfers between devices, per_device(): lax.all_to_all(width_step, 'pencil', split_axis=1, concat_axis=0, tiled=T...  76.9 us
    dot_general x10, matrix products, forward(): jnp.einsum('pkq,jk->pjq', piece, matrix, precision=lax.Precision.HIGHEST)  35.8 us
    add x1, other arithmetic, per_device(): 2.0 * (coupling[0] * along_width + coupling[1] * along_height + coupling[...  30.6 us
    unnamed x19, local copies, waits for them, and re-layouts  16.7 us
    dynamic_slice x6, other arithmetic, backward(): value = lax.dynamic_index_in_dim(result, current, 1, keepdims=False)  14.4 us
    slice x2, local copies, waits for them, and re-layouts, extended(): leading = lax.slice_in_dim(value, 0, width, axis=dim)  12.3 us
    all_to_all x1, starting transfers between devices, per_device(): lax.all_to_all(width_step, 'pencil', split_axis=1, concat_axis=0, tiled=T...  12.3 us
  transfers between devices with their start and end apart: 7, of which 4 were waited for; matrix products, arithmetic and copies ran while one was open for 7% of the time, Pallas kernels for 0%

commit v1 on v0

v1 whole, which is shorter than its diff:
```python
import jax
import jax.numpy as jnp
from jax import lax
from jax.experimental import pallas as pl
from jax.experimental.pallas import tpu as pltpu
from jax.sharding import PartitionSpec as P

H, W, D = 16, 768, 128
B = 128
NB = W // B
NP = 32
S = W // NP
f32 = jnp.float32
bf16 = jnp.bfloat16
HIGHEST = lax.Precision.HIGHEST


def log_decay(s):
    return jnp.log(2.0 * s / (1.0 + 2.0 * s + jnp.sqrt(1.0 + 4.0 * s)))


def pivots(log_r, length):
    return (
        jnp.exp(log_r)
        * (1.0 - jnp.exp(log_r * (2.0 * length)))
        / (1.0 - jnp.exp(log_r * (2.0 * length + 2.0)))
    )


def influence(log_r, m, i):
    return (
        jnp.exp(log_r * (i + 1.0))
        * (1.0 - jnp.exp(log_r * (2.0 * (m - i))))
        / (1.0 - jnp.exp(log_r * (2.0 * m + 2.0)))
    )


def green(s, log_r, n, i, j):
    low, high = jnp.minimum(i, j), jnp.maximum(i, j)
    return (
        jnp.exp(log_r * (high - low))
        * (1.0 - jnp.exp(log_r * (2.0 * low + 2.0)))
        * (1.0 - jnp.exp(log_r * (2.0 * (n - high))))
        / (jnp.sqrt(1.0 + 4.0 * s) * (1.0 - jnp.exp(log_r * (2.0 * n + 2.0))))
    )


def split(x):
    hi = x.astype(bf16)
    return hi, (x - hi.astype(f32)).astype(bf16)


def dot(a, b):
    return lax.dot_general(a, b, (((1,), (0,)), ((), ())), preferred_element_type=f32)


def iota(shape, dim):
    return lax.broadcasted_iota(jnp.int32, shape, dim)


HEAD, BEFORE_H, BEFORE_W, AH, CH, MH, FROM = 0, 1, 5, 9, 10, 11, 12


def tables_kernel(cpl, slab, wi, di, par, cols, rows, gw3, gd4, spread, hmat, hcol):
    row = (1, 128)
    sw, sh, sd = (jnp.full(row, cpl[k], f32) for k in range(3))
    lw, lh, ld = log_decay(sw), log_decay(sh), log_decay(sd)
    lane = iota(row, 1)
    k = lane.astype(f32)
    heads = [2.0 - 4.0 * sw - 4.0 * sd, 2.0 * sw, 2.0 * sd]
    for log_r, m in ((lw, float(B)), (lh, float(H)), (ld, float(D))):
        heads += [influence(log_r, m, 0.0), influence(log_r, m, m - 1.0)]
    head = jnp.zeros(row, f32)
    for at, v in enumerate(heads):
        head = jnp.where(lane == at, v, head)
    par[HEAD : HEAD + 1] = head
    for at, log_r, m, p, q in ((BEFORE_H, lh, float(H), heads[5], heads[6]), (BEFORE_W, lw, float(B), heads[3], heads[4])):
        before = pivots(log_r, m * k)
        inv = 1.0 / (1.0 - p * before)
        w = q * before * inv
        for n, v in enumerate((before, inv, w, q + w * p)):
            par[at + n : at + n + 1] = v
    kc = jnp.minimum(k, H - 1.0)
    ch = pivots(lh, kc + 1.0)
    par[AH : AH + 1] = influence(lh, float(H), kc)
    par[CH : CH + 1] = ch
    par[MH : MH + 1] = ch / sh
    me = slab[0]
    other = lax.bitwise_and(me - lane, 3)
    of, mf = other.astype(f32), jnp.full(row, me, jnp.int32).astype(f32)
    n = float(4 * D)
    for side, (where, beside, inside) in enumerate(
        ((D * mf - 1.0, me - 1, me > 0), (D * mf + D, me + 1, me < 3))
    ):
        spot = jnp.clip(where, 0.0, n - 1.0)
        first = jnp.where(other >= 1, sd * green(sd, ld, n, spot, jnp.maximum(D * of - 1.0, 0.0)), 0.0)
        last = jnp.where(other <= 2, sd * green(sd, ld, n, spot, jnp.minimum(D * of + D, n - 1.0)), 0.0)
        same = jnp.where(other == beside, 1.0, 0.0)
        if side == 0:
            last = last + same
        else:
            first = first + same
        par[FROM + 2 * side : FROM + 2 * side + 1] = jnp.where(inside, first, 0.0)
        par[FROM + 2 * side + 1 : FROM + 2 * side + 2] = jnp.where(inside, last, 0.0)
    tall = iota((B, D), 0).astype(f32)
    lww = jnp.broadcast_to(lw, (B, D))
    cols[0] = influence(lww, float(B), tall)
    cols[1] = influence(lww, float(B), B - 1.0 - tall)
    rows[0:1] = influence(lw, float(B), k)
    rows[1:2] = influence(lw, float(B), B - 1.0 - k)
    hi, lo = split(wi[0])
    gw3[:, :B] = hi
    gw3[:, B : 2 * B] = hi
    gw3[:, 2 * B :] = lo
    hi, lo = split(di[0].T)
    gd4[:D, :D] = hi
    gd4[:D, D:] = lo
    gd4[D:, :D] = hi
    gd4[D:, D:] = jnp.zeros((D, D), bf16)
    ad, bd = influence(ld, float(D), k), influence(ld, float(D), D - 1.0 - k)
    line = iota((2 * H, D), 0)
    for h in range(H):
        v = jnp.where(line == h, ad, jnp.where(line == H + h, bd, 0.0))
        hi, lo = split(v)
        at = slice(h * D, (h + 1) * D)
        spread[: 2 * H, at] = hi
        spread[2 * H : 4 * H, at] = hi
        spread[4 * H :, at] = lo
    a = iota((2 * H, 128), 0)
    b = iota((2 * H, 128), 1)
    af = lax.bitwise_and(a, H - 1).astype(f32)
    bfl = lax.bitwise_and(b, H - 1).astype(f32)
    wide_h = jnp.broadcast_to(lh, (2 * H, 128))
    g = green(jnp.broadcast_to(sh, (2 * H, 128)), wide_h, float(H), af, bfl)
    hmat[...] = jnp.where((b < 2 * H) & (lax.shift_right_logical(a, 4) == lax.shift_right_logical(b, 4)), g, 0.0)
    c = iota((H, 128), 0).astype(f32)
    ln = iota((H, 128), 1)
    hcol[...] = influence(jnp.broadcast_to(lh, (H, 128)), float(H), jnp.where(ln == 0, c, H - 1.0 - c))


def sums_kernel(cpl, rho, sig, cr, cs, own, comb, coef, packed):
    i = pl.program_id(0)

    @pl.when(i == 0)
    def _():
        sh = jnp.full((8, 128), cpl[1], f32)
        lh = log_decay(sh)
        for h in range(H):
            coef[h] = influence(lh, float(H), float(h)) / sh

    T = 32
    lane = iota((T, D), 1)
    packs, combs = [], []
    for t in range(B // T):
        at = slice(t * T, (t + 1) * T)
        fr = jnp.zeros((T, D), f32)
        tr, fs, ts, pack = fr, fr, fr, fr
        for h in range(H):
            x, y = rho[h, at, :], sig[h, at, :]
            cf = jnp.broadcast_to(coef[h, 0:1, :], (T, D))
            ct = jnp.broadcast_to(coef[H - 1 - h, 0:1, :], (T, D))
            fr, tr, fs, ts = fr + cf * x, tr + ct * x, fs + cf * y, ts + ct * y
            pack = jnp.where((lane == 2 * h) | (lane == 2 * h + 1), pltpu.roll(x, 2 * h + 1, 1), pack)
        cr[0, at], cr[1, at], cs[0, at], cs[1, at] = fr, tr, fs, ts
        packs.append(pack)
        combs.append(jnp.where(lane < 2, pltpu.roll(fr, 1, 1), pltpu.roll(tr, 3, 1)))
    packed[...] = jnp.concatenate(packs, axis=0).T[: 2 * H]
    own[:H] = packed[pl.ds(1, H, stride=2), :]
    own[H:] = packed[pl.ds(0, H, stride=2), :]
    comb[...] = jnp.concatenate(combs, axis=0).T[:8]


def chain_w(yf, yt, par):
    p, q = par[HEAD, 3], par[HEAD, 4]
    before, inv, w, qw = (BEFORE_W + k for k in range(4))
    us = []
    for k in range(NB):
        u = yt[k] + par[w, k] * yf[k]
        us.append(u if k == 0 else u + par[qw, k] * us[-1])
    fs = [None] * NB
    for k in reversed(range(NB)):
        g = yf[k]
        if k > 0:
            g = g + p * us[k - 1]
        if k < NB - 1:
            g = g + q * fs[k + 1]
        fs[k] = g * par[inv, k]
    zero = jnp.zeros_like(yf[0])
    ls = [zero] + [us[k - 1] + par[before, k] * fs[k] for k in range(1, NB)]
    return ls, fs[1:] + [zero]


def solve_wd(x, gw3, gd4):
    hi, lo = split(x)
    z = dot(gw3[:, : 2 * B], jnp.concatenate([hi, lo], axis=0)) + dot(gw3[:, 2 * B :], hi)
    z = jnp.concatenate([z[:, :D], z[:, D:]], axis=0)
    hi, lo = split(z)
    y = dot(jnp.concatenate([hi, lo], axis=1), gd4[...])
    return y[:, :D] + y[:, D:]


def edges_kernel(par, cr, cs, from_left, from_right, gw3, gd4, cols, out, e):
    c0, c1, c2 = par[HEAD, 0], par[HEAD, 1], par[HEAD, 2]
    row = iota((B, D), 0)
    lane = iota((B, D), 1)
    blank = jnp.zeros((B - 8, B), f32)
    for k in range(NB):
        spot = slice(k * B, (k + 1) * B)
        lc = jnp.concatenate([from_left[:, spot], blank], axis=0).T
        rc = jnp.concatenate([from_right[:, spot], blank], axis=0).T
        xs = []
        for j in range(2):
            x = cr[j, spot]
            up = pltpu.roll(x, 1, 0)
            up = jnp.where(row == 0, cr[j, k * B - 1 : k * B] if k > 0 else 0.0, up)
            down = pltpu.roll(x, B - 1, 0)
            down = jnp.where(row == B - 1, cr[j, (k + 1) * B : (k + 1) * B + 1] if k < NB - 1 else 0.0, down)
            lcol = lc if j == 0 else pltpu.roll(lc, D - 2, 1)
            left = jnp.where(lane == 0, lcol, pltpu.roll(x, 1, 1))
            right = jnp.where(lane == D - 1, pltpu.roll(rc, D - 2 if j == 0 else D - 4, 1), pltpu.roll(x, D - 1, 1))
            xs.append(cs[j, spot] + c0 * x + c1 * (up + down) + c2 * (left + right))
        y = solve_wd(jnp.concatenate(xs, axis=1), gw3, gd4)
        e[0, spot] = y[:B]
        e[1, spot] = y[B:]
    for j in range(2):
        ls, rs = chain_w(
            [e[j, k * B : k * B + 1] for k in range(NB)], [e[j, k * B + B - 1 : k * B + B] for k in range(NB)], par
        )
        for k in range(NB):
            spot = slice(k * B, (k + 1) * B)
            e[j, spot] = e[j, spot] + cols[0] * ls[k] + cols[1] * rs[k]
        for p in range(NP):
            out[p, j] = e[j, S * p : S * (p + 1)]


def field_kernel(par, rho, prev, nxt, sig, gw3, gd4, out, ew, e):
    i = pl.program_id(0)
    c0, c1, c2 = par[HEAD, 0], par[HEAD, 1], par[HEAD, 2]
    row = iota((B, D), 0)
    for h in range(H):
        x = rho[h]
        up = jnp.where(row == 0, jnp.where(i > 0, prev[h, 7:8, :], 0.0), pltpu.roll(x, 1, 0))
        down = jnp.where(row == B - 1, jnp.where(i < NB - 1, nxt[h, 0:1, :], 0.0), pltpu.roll(x, B - 1, 0))
        e[h] = sig[h] + c0 * x + c1 * (up + down) + c2 * (pltpu.roll(x, 1, 1) + pltpu.roll(x, D - 1, 1))

    def tile(j, _):
        at = pl.ds(pl.multiple_of(8 * j, 8), 8)
        z = []
        for h in range(H):
            v = par[MH, h] * e[h, at, :]
            z.append(v if h == 0 else v + par[CH, h] * z[-1])
        x = z[H - 1]
        e[H - 1, at, :] = x - 2.0 * rho[H - 1, at, :]
        for h in reversed(range(H - 1)):
            x = z[h] + par[CH, h] * x
            e[h, at, :] = x - 2.0 * rho[h, at, :]
        return 0

    lax.fori_loop(0, B // 8, tile, 0)
    for g in range(H // 2):
        y = solve_wd(jnp.concatenate([e[2 * g], e[2 * g + 1]], axis=1), gw3, gd4)
        for side in range(2):
            h = 2 * g + side
            part = y[side * B : (side + 1) * B]
            ew[0, 0, h : h + 1, :] = part[0:1]
            ew[0, 1, h : h + 1, :] = part[B - 1 : B]
            out[h] = part + rho[h]


def mend_kernel(par, base, ew, cols, out, qp, fix, packed):
    i = pl.program_id(0)

    @pl.when(i == 0)
    def _():
        ls, rs = chain_w([ew[k, 0] for k in range(NB)], [ew[k, 1] for k in range(NB)], par)
        for k in range(NB):
            fix[k, 0] = ls[k]
            fix[k, 1] = rs[k]

    lane = iota((B, D), 1)
    pack = jnp.zeros((B, D), f32)
    for h in range(H):
        v = base[h] + cols[0] * fix[i, 0, h : h + 1, :] + cols[1] * fix[i, 1, h : h + 1, :]
        out[h] = v
        pack = jnp.where((lane == 2 * h) | (lane == 2 * h + 1), pltpu.roll(v, 2 * h + 1, 1), pack)
    packed[...] = pack.T[: 2 * H]
    qp[:H] = packed[pl.ds(1, H, stride=2), :]
    qp[H:] = packed[pl.ds(0, H, stride=2), :]


def planes_kernel(par, qp, own, from_left, from_right, hmat, rows, wi, out, u):
    v = jnp.concatenate([from_left[H:] - own[H:], from_right[:H] - own[:H]], axis=0)
    v = jnp.dot(hmat[:, : 2 * H], v, precision=HIGHEST, preferred_element_type=f32)
    parts = []
    for k in range(NB):
        parts.append(
            lax.dot_general(
                v[:, k * B : (k + 1) * B], wi[0], (((1,), (1,)), ((), ())), precision=HIGHEST, preferred_element_type=f32
            )
        )
    ls, rs = chain_w([a[:, 0:1] for a in parts], [a[:, B - 1 : B] for a in parts], par)
    for k in range(NB):
        spot = slice(k * B, (k + 1) * B)
        u[:, spot] = 2.0 * (parts[k] + ls[k] * rows[0:1] + rs[k] * rows[1:2])
    p, q = par[HEAD, 7], par[HEAD, 8]
    ul, ur = u[:H], u[H:]
    out[:H] = qp[:H] - own[:H] + p * ul + q * ur
    out[H:] = qp[H:] - own[H:] + q * ul + p * ur


def solver_kernel(par, y, out, us):
    p, q = par[HEAD, 5], par[HEAD, 6]
    before, inv, w, qw = (BEFORE_H + k for k in range(4))
    u = y[0, 1] + par[w, 0] * y[0, 0]
    us[0] = u
    for k in range(1, NP):
        u = y[k, 1] + par[w, k] * y[k, 0] + par[qw, k] * u
        us[k] = u
    zero = jnp.zeros_like(u)
    out[NP - 1, 1] = zero
    f = zero
    for k in reversed(range(NP)):
        g = y[k, 0]
        if k > 0:
            g = g + p * us[k - 1]
        f = (g + q * f) * par[inv, k]
        if k > 0:
            out[k, 0] = us[k - 1] + par[before, k] * f
            out[k - 1, 1] = f
    out[0, 0] = zero


def corner_kernel(a, out, wide):
    lane = iota((S, D), 1)
    for p in range(NP):
        wide[S * p : S * (p + 1)] = jnp.where(lane < 2, pltpu.roll(a[p, 0], 1, 1), pltpu.roll(a[p, 1], 3, 1))
    for k in range(NB):
        out[:, k * B : (k + 1) * B] = wide[k * B : (k + 1) * B].T[:8]


def final_kernel(par, base, a, d0, d1, d2, d3, c0, c1, c2, c3, u, hcol, spread, out, tall):
    i = pl.program_id(0)

    @pl.when(i == 0)
    def _():
        ds, cs = (d0, d1, d2, d3), (c0, c1, c2, c3)
        sides = []
        for side in range(2):
            first, last = FROM + 2 * side, FROM + 2 * side + 1
            own = u[H * side : H * (side + 1)]
            for k in range(4):
                own = own + par[first, k] * ds[k][:H] + par[last, k] * ds[k][H:]
            gam = []
            for plane in range(2):
                g = 0.0
                for k in range(4):
                    t, f = cs[k][2 * plane : 2 * plane + 1], cs[k][2 * plane + 1 : 2 * plane + 2]
                    g = g + par[first, k] * f + par[last, k] * t
                gam.append(g)
            sides.append(own + hcol[:, 0:1] * gam[0] + hcol[:, 1:2] * gam[1])
        both = jnp.concatenate(sides + [jnp.zeros((D - 2 * H, W), f32)], axis=0)
        for k in range(NB):
            tall[k * B : (k + 1) * B] = both[:, k * B : (k + 1) * B].T

    at = pl.ds(pl.multiple_of(i * 4 * S, 4 * S), 4 * S)
    hi, lo = split(tall[at, : 2 * H])
    wide = dot(jnp.concatenate([hi, lo, hi], axis=1), spread[...])
    l = jnp.concatenate([a[p, 0] for p in range(4)], axis=0)
    r = jnp.concatenate([a[p, 1] for p in range(4)], axis=0)
    for h in range(H):
        out[h] = base[h] + wide[:, h * D : (h + 1) * D] + par[AH, h] * l + par[AH, H - 1 - h] * r


SMEM = pl.BlockSpec(memory_space=pltpu.SMEM)


def whole(*shape):
    return pl.BlockSpec(shape, lambda *_: (0,) * len(shape))


def shaped(*shape, dtype=f32):
    return jax.ShapeDtypeStruct(shape, dtype)


def cost(flops, bytes_accessed):
    return pl.CostEstimate(flops=flops, bytes_accessed=bytes_accessed, transcendentals=0)


def per_device(density, source, coupling, width_inverse, height_inverse, depth_inverse):
    slab = lax.axis_index("slab")
    slabs = lax.axis_size("slab")
    up = [(k, k + 1) for k in range(slabs - 1)]
    down = [(k + 1, k) for k in range(slabs - 1)]

    block = pl.BlockSpec((H, B, D), lambda i: (0, i, 0))
    pair = pl.BlockSpec((2, B, D), lambda i: (0, i, 0))
    line = pl.BlockSpec((2 * H, B), lambda i: (0, i))
    cr, cs, own, comb = pl.pallas_call(
        sums_kernel,
        grid=(NB,),
        in_specs=[SMEM, block, block],
        out_specs=[pair, pair, line, pl.BlockSpec((8, B), lambda i: (0, i))],
        out_shape=[shaped(2, W, D), shaped(2, W, D), shaped(2 * H, W), shaped(8, W)],
        scratch_shapes=[pltpu.VMEM((H, 8, 128), f32), pltpu.VMEM((2 * H, B), f32)],
        name="sums",
        cost_estimate=cost(10**7, 14 * 10**6),
    )(coupling, density, source)
    comb_left = lax.ppermute(comb, "slab", up)
    comb_right = lax.ppermute(comb, "slab", down)

    first_block = pl.BlockSpec((1, B, B), lambda *_: (0, 0, 0))
    par, cols, rows, gw3, gd4, spread, hmat, hcol = pl.pallas_call(
        tables_kernel,
        grid=(1,),
        in_specs=[SMEM, SMEM, first_block, first_block],
        out_specs=[
            whole(16, 128),
            whole(2, B, D),
            whole(8, 128),
            whole(B, 3 * B),
            whole(2 * D, 2 * D),
            whole(6 * H, H * D),
            whole(2 * H, 128),
            whole(H, 128),
        ],
        out_shape=[
            shaped(16, 128),
            shaped(2, B, D),
            shaped(8, 128),
            shaped(B, 3 * B, dtype=bf16),
            shaped(2 * D, 2 * D, dtype=bf16),
            shaped(6 * H, H * D, dtype=bf16),
            shaped(2 * H, 128),
            shaped(H, 128),
        ],
        name="tables",
        cost_estimate=cost(10**7, 10**6),
    )(coupling, slab.reshape(1), width_inverse, depth_inverse)

    edges = pl.pallas_call(
        edges_kernel,
        grid=(1,),
        in_specs=[SMEM, whole(2, W, D), whole(2, W, D), whole(8, W), whole(8, W), whole(B, 3 * B), whole(2 * D, 2 * D), whole(2, B, D)],
        out_specs=whole(NP, 2, S, D),
        out_shape=shaped(NP, 2, S, D),
        scratch_shapes=[pltpu.VMEM((2, W, D), f32)],
        name="edges",
        cost_estimate=cost(10**8, 3 * 10**6),
    )(par, cr, cs, comb_left, comb_right, gw3, gd4, cols)
    arrived = lax.all_to_all(edges, "pencil", 0, 0, tiled=True)

    own_left = lax.ppermute(own, "slab", up)
    own_right = lax.ppermute(own, "slab", down)
    raw, ew = pl.pallas_call(
        field_kernel,
        grid=(NB,),
        in_specs=[
            SMEM,
            block,
            pl.BlockSpec((H, 8, D), lambda i: (0, jnp.maximum(i * (B // 8) - 1, 0), 0)),
            pl.BlockSpec((H, 8, D), lambda i: (0, jnp.minimum((i + 1) * (B // 8), W // 8 - 1), 0)),
            block,
            whole(B, 3 * B),
            whole(2 * D, 2 * D),
        ],
        out_specs=[block, pl.BlockSpec((1, 2, H, D), lambda i: (i, 0, 0, 0))],
        out_shape=[shaped(H, W, D), shaped(NB, 2, H, D)],
        scratch_shapes=[pltpu.VMEM((H, B, D), f32)],
        name="field",
        cost_estimate=cost(4 * 10**9, 19 * 10**6),
    )(par, density, density, density, source, gw3, gd4)

    arrived, ew = lax.optimization_barrier((arrived, ew))
    solved = pl.pallas_call(
        solver_kernel,
        grid=(1,),
        in_specs=[SMEM, whole(NP, 2, S, D)],
        out_specs=whole(NP, 2, S, D),
        out_shape=shaped(NP, 2, S, D),
        scratch_shapes=[pltpu.VMEM((NP, S, D), f32)],
        name="solver",
        cost_estimate=cost(10**6, 2 * 10**6),
    )(par, arrived)
    outside = lax.all_to_all(solved, "pencil", 0, 0, tiled=True)

    base, qp = pl.pallas_call(
        mend_kernel,
        grid=(NB,),
        in_specs=[SMEM, block, whole(NB, 2, H, D), whole(2, B, D)],
        out_specs=[block, line],
        out_shape=[shaped(H, W, D), shaped(2 * H, W)],
        scratch_shapes=[pltpu.VMEM((NB, 2, H, D), f32), pltpu.VMEM((2 * H, B), f32)],
        input_output_aliases={1: 0},
        name="mend",
        cost_estimate=cost(10**9, 13 * 10**6),
    )(par, raw, ew, cols)
    planes, u = pl.pallas_call(
        planes_kernel,
        grid=(1,),
        in_specs=[SMEM, *[whole(2 * H, W)] * 4, whole(2 * H, 128), whole(8, 128), first_block],
        out_specs=[whole(2 * H, W)] * 2,
        out_shape=[shaped(2 * H, W)] * 2,
        name="planes",
        cost_estimate=cost(10**8, 10**6),
    )(par, qp, own, own_left, own_right, hmat, rows, width_inverse)

    def turned(value):
        return [value] + [
            lax.ppermute(value, "slab", [(k, (k + d) % slabs) for k in range(slabs)]) for d in range(1, slabs)
        ]

    planes_all = turned(planes)
    corners = pl.pallas_call(
        corner_kernel,
        grid=(1,),
        in_specs=[whole(NP, 2, S, D)],
        out_specs=whole(8, W),
        out_shape=shaped(8, W),
        scratch_shapes=[pltpu.VMEM((W, D), f32)],
        name="corner",
        cost_estimate=cost(10**6, 10**6),
    )(outside)
    corners_all = turned(corners)
    return pl.pallas_call(
        final_kernel,
        grid=(NP // 4,),
        in_specs=[
            SMEM,
            pl.BlockSpec((H, 4 * S, D), lambda i: (0, i, 0)),
            pl.BlockSpec((4, 2, S, D), lambda i: (i, 0, 0, 0)),
            *[whole(2 * H, W)] * 4,
            *[whole(8, W)] * 4,
            whole(2 * H, W),
            whole(H, 128),
            whole(6 * H, H * D),
        ],
        out_specs=pl.BlockSpec((H, 4 * S, D), lambda i: (0, i, 0)),
        out_shape=shaped(H, W, D),
        scratch_shapes=[pltpu.VMEM((W, D), f32)],
        name="final",
        cost_estimate=cost(10**9, 13 * 10**6),
    )(par, base, outside, *planes_all, *corners_all, u, hcol, spread)


def solution(mesh):
    in_specs = (P("pencil", None, "slab"), P("pencil", None, "slab"), P(), P(), P(), P())
    out_specs = P("pencil", None, "slab")
    return jax.shard_map(per_device, mesh=mesh, in_specs=in_specs, out_specs=out_specs, check_vma=False)
```

time: 419 us -> 109 us (0.26)
  other arithmetic: 86.4 us -> 0 us
  waiting for transfers between devices: 88.8 us -> 7.91 us
  blocking collectives: 77.6 us -> 0 us
  local copies, waits for them, and re-layouts: 78.2 us -> 3.63 us
  Pallas kernels: 0 us -> 57.1 us
  matrix products: 42.2 us -> 0 us
    all_to_all x3 -> x2, waiting for transfers between devices: 88.6 us -> 0.01 us  [the longest x1 0.01 us: per_device(): arrived = lax.all_to_all(edges, 'pencil', 0, 0, tiled=True)]
    all_to_all x1 -> x0, blocking collectives: 77.6 us -> none  [per_device(): lax.all_to_all(depth_step, 'pencil', split_axis=0, concat_axis=1, tiled=T...]
    pallas_call x0 -> x9, Pallas kernels: none -> 57.1 us  [the longest x1 18.3 us: per_device(): pl.pallas_call(field_kernel, grid=(NB,), in_specs=[SMEM, block, pl.BlockS...]
    add x6 -> x0, other arithmetic: 44.7 us -> none  [the longest x1 30.6 us: per_device(): 2.0 * (coupling[0] * along_width + coupling[1] * along_height + coupling[...]
    dot_general x11 -> x0, matrix products: 42.2 us -> none  [the longest x10 35.8 us: forward(): jnp.einsum('pkq,jk->pjq', piece, matrix, precision=lax.Precision.HIGHEST)]
    slice x25 -> x0, local copies, waits for them, and re-layouts: 16 us -> none  [the longest x2 12.3 us: extended(): leading = lax.slice_in_dim(value, 0, width, axis=dim)]
    mul x25 -> x0, other arithmetic: 15.3 us -> none  [the longest x10 6.84 us: forward(): value = value + strength * matrix[:, 0][None, :, None] * carry[:, None, :]]
    dynamic_slice x6 -> x0, other arithmetic: 14.4 us -> none  [backward(): value = lax.dynamic_index_in_dim(result, current, 1, keepdims=False)]
  transfers between devices with their start and end apart: 7 -> 12, of which waited for: 4 -> 3; matrix products, arithmetic and copies ran while one was open for 7% -> 0% of each run, Pallas kernels for 0% -> 31%
where the time goes in v1:
time: 109 us; the launch traced here: 108 us
  Pallas kernels  57.1 us (52%)
  starting transfers between devices  38.9 us (36%)
  waiting for transfers between devices  7.91 us (7%)
  local copies, waits for them, and re-layouts  3.63 us (3%)
    pallas_call x1, Pallas kernels, per_device(): pl.pallas_call(field_kernel, grid=(NB,), in_specs=[SMEM, block, pl.BlockS...  18.3 us
    pallas_call x1, Pallas kernels, per_device(): pl.pallas_call(final_kernel, grid=(NP // 4,), in_specs=[SMEM, pl.BlockSpe...  9.7 us
    ppermute x6, starting transfers between devices, turned(): lax.ppermute(value, 'slab', [(k, (k + d) % slabs) for k in range(slabs)])  9.46 us
    pallas_call x1, Pallas kernels, per_device(): pl.pallas_call(sums_kernel, grid=(NB,), in_specs=[SMEM, block, block], ou...  8.08 us
    all_to_all x1, starting transfers between devices, per_device(): arrived = lax.all_to_all(edges, 'pencil', 0, 0, tiled=True)  7.99 us
    pallas_call x1, Pallas kernels, per_device(): pl.pallas_call(mend_kernel, grid=(NB,), in_specs=[SMEM, block, whole(NB,...  7.95 us
    all_to_all x1, starting transfers between devices, per_device(): outside = lax.all_to_all(solved, 'pencil', 0, 0, tiled=True)  7.76 us
    ppermute x1, starting transfers between devices, per_device(): comb_left = lax.ppermute(comb, 'slab', up)  6.19 us
  transfers between devices with their start and end apart: 12, of which 3 were waited for; matrix products, arithmetic and copies ran while one was open for 0% of the time, Pallas kernels for 31%

profile of v1, /device:TPU:1, one launch (start us, length us, event | category | flops | bytes accessed | tf_op | source)
XLA Modules:
  0.0 107.7 jit_solution(15023771946630174725)
XLA Ops:
  0.0 8.1 %sums.1 = (f32[2,768,128]{2,1,0:T(8,128)}, f32[2,768,128]{2,1,0:T(8,128)}, f32[32,768]{1,0:T(8,128)}, f32[8,768]{1,0:T(8,128)}) custom-call(f32[3]{0:T(128)} %cpl.3, f32[16,768,128]{2,1,0:T(8,128)} %rho.3, f32[16,768,128]{2,1,0:T(8,128)} %sig.3), custom_call_target="tpu_custom_call" | custom-call | flops 10000000 | bytes 14000000 | tf_op jit(solution)/shard_map/sums/pallas_call | solution.py:398
  8.1 6.2 %collective-permute-start = (f32[8,768]{1,0:T(8,128)}, f32[8,768]{1,0:T(8,128)S(1)}, u32[]{:S(2)}, u32[]{:S(2)}) collective-permute-start(f32[8,768]{1,0:T(8,128)} %get-tuple-element.31), channel_id=1, source_target_pairs={{0,32},{32,64},{64,96},{1,33},{33,65},{65,97},{2,34},{34,66},{66,9... | collective-permute-start | bytes 73736 | tf_op jit(solution)/shard_map/ppermute | solution.py:408
  14.3 1.9 %collective-permute-start.1 = (f32[8,768]{1,0:T(8,128)}, f32[8,768]{1,0:T(8,128)S(1)}, u32[]{:S(2)}, u32[]{:S(2)}) collective-permute-start(f32[8,768]{1,0:T(8,128)} %get-tuple-element.31), channel_id=1, source_target_pairs={{32,0},{64,32},{96,64},{33,1},{65,33},{97,65},{34,2},{66,34},{98,6... | collective-permute-start | bytes 73736 | tf_op jit(solution)/shard_map/ppermute | solution.py:409
  16.2 1.9 %tables.1 = (f32[16,128]{1,0:T(8,128)}, f32[2,128,128]{2,1,0:T(8,128)}, f32[8,128]{1,0:T(8,128)}, bf16[128,384]{1,0:T(8,128)(2,1)}, bf16[256,256]{1,0:T(8,128)(2...) custom-call(f32[3]{0:T(128)} %cpl.3, s32[1]{0:T(128)} %bitcast.slab, f32[6,128,128]{2,1,0:T(8,128)} %wi.3, ...), custom_call_target="tpu_custom_call" | custom-call | flops 10000000 | bytes 1000000 | tf_op jit(solution)/shard_map/tables/pallas_call | solution.py:412
  18.1 0.0 collective-permute-done.from_left
  18.1 3.0 %collective-permute-done.1.from_right = f32[8,768]{1,0:T(8,128)S(1)} collective-permute-done((f32[8,768]{1,0:T(8,128)}, f32[8,768]{1,0:T(8,128)S(1)}, u32[]{:S(2)}, u32[]{:S(2)}) %collective-permute-start.1) | collective-permute-done | bytes 24608 | tf_op jit(solution)/shard_map/ppermute | solution.py:409
  21.1 0.0 copy-done.10
  21.1 0.6 copy-done.12
  21.7 3.9 %edges.1 = f32[32,2,24,128]{3,2,1,0:T(8,128)} custom-call(f32[16,128]{1,0:T(8,128)} %get-tuple-element.25.par, f32[2,768,128]{2,1,0:T(8,128)} %get-tuple-element.29.cr, f32[2,768,128]{2,1,0:T(8,128)} %get-tuple-element.30.cs, f32[8,768]{1,0:T(8,128)} %copy-done.10, f32[8,768]{1,0:T(8,128)} %copy-done.12, bf16[128,384]{1,0:T(8,128)(2,1)} %get-tuple-element.26.gw3, ...), custom_call_target="tpu_custom_call" | custom-call | flops 100000000 | bytes 3000000 | tf_op jit(solution)/shard_map/edges/pallas_call | solution.py:440
  25.6 8.0 %all-to-all-start = ((f32[32,2,24,128]{3,2,1,0:T(8,128)}), f32[32,2,24,128]{3,2,1,0:T(8,128)S(1)}, u32[]{:S(2)}, u32[]{:S(2)}) async-start(f32[32,2,24,128]{3,2,1,0:T(8,128)} %edges.1), calls=%async_computation | async-start | bytes 1572864 | tf_op jit(solution)/shard_map/all_to_all | solution.py:450
  33.6 0.0 copy-start.5
  33.7 18.3 %field.1 = (f32[16,768,128]{2,1,0:T(8,128)}, f32[6,2,16,128]{3,2,1,0:T(8,128)}) custom-call(f32[16,128]{1,0:T(8,128)} %get-tuple-element.25.par, f32[16,768,128]{2,1,0:T(8,128)} %rho.3, f32[16,768,128]{2,1,0:T(8,128)} %rho.3, f32[16,768,128]{2,1,0:T(8,128)} %rho.3, f32[16,768,128]{2,1,0:T(8,128)} %sig.3, bf16[128,384]{1,0:T(8,128)(2,1)} %get-tuple-element.26.gw3, ...), custom_call_target="tpu_custom_call" | custom-call | flops 4000000000 | bytes 19000000 | tf_op jit(solution)/shard_map/field/pallas_call | solution.py:454
  51.9 0.0 all-to-all-done.y
  51.9 0.0 copy-start.1
  52.0 0.9 copy-done.1
  52.8 2.2 %solver.1 = f32[32,2,24,128]{3,2,1,0:T(8,128)} custom-call(f32[16,128]{1,0:T(8,128)} %get-tuple-element.25.par, f32[32,2,24,128]{3,2,1,0:T(8,128)} %copy-done.1), custom_call_target="tpu_custom_call" | custom-call | flops 1000000 | bytes 2000000 | tf_op jit(solution)/shard_map/solver/pallas_call | solution.py:474
  55.1 7.8 %all-to-all-start.1 = ((f32[32,2,24,128]{3,2,1,0:T(8,128)}), f32[32,2,24,128]{3,2,1,0:T(8,128)S(1)}, u32[]{:S(2)}, u32[]{:S(2)}) async-start(f32[32,2,24,128]{3,2,1,0:T(8,128)} %solver.1), calls=%async_computation.1 | async-start | bytes 1572864 | tf_op jit(solution)/shard_map/all_to_all | solution.py:484
  62.8 0.0 copy-done.5
  62.8 3.6 %collective-permute-start.2 = (f32[32,768]{1,0:T(8,128)S(1)}, f32[32,768]{1,0:T(8,128)S(1)}, u32[]{:S(2)}, u32[]{:S(2)}) collective-permute-start(f32[32,768]{1,0:T(8,128)S(1)} %copy-done.5), channel_id=1, source_target_pairs={{0,32},{32,64},{64,96},{1,33},{33,65},{65,97},{2,34},{34,66},{66,9... | collective-permute-start | bytes 294920 | tf_op jit(solution)/shard_map/ppermute | solution.py:452
  66.5 1.9 %collective-permute-start.3 = (f32[32,768]{1,0:T(8,128)S(1)}, f32[32,768]{1,0:T(8,128)S(1)}, u32[]{:S(2)}, u32[]{:S(2)}) collective-permute-start(f32[32,768]{1,0:T(8,128)S(1)} %copy-done.5), channel_id=1, source_target_pairs={{32,0},{64,32},{96,64},{33,1},{65,33},{97,65},{34,2},{66,34},{98,6... | collective-permute-start | bytes 294920 | tf_op jit(solution)/shard_map/ppermute | solution.py:453
  68.4 7.9 %mend.1 = (f32[16,768,128]{2,1,0:T(8,128)}, f32[32,768]{1,0:T(8,128)}) custom-call(f32[16,128]{1,0:T(8,128)} %get-tuple-element.25.par, f32[16,768,128]{2,1,0:T(8,128)} %get-tuple-element.28.base, f32[6,2,16,128]{3,2,1,0:T(8,128)} %get-tuple-element.34.ew, f32[2,128,128]{2,1,0:T(8,128)} %get-tuple-element.32.cols), custom_call_target="tpu_custom_call", output_to_operand_aliasing={{0}: (1, {})} | custom-call | flops 1000000000 | bytes 13000000 | tf_op jit(solution)/shard_map/mend/pallas_call | solution.py:486
  76.3 0.0 collective-permute-done.2.from_left
  76.3 0.0 copy-start.6
  76.4 0.0 collective-permute-done.3.from_right
  76.4 0.0 copy-start.7
  76.4 0.6 copy-done.6
  77.0 0.0 copy-done.7
  77.0 3.0 %planes.1 = (f32[32,768]{1,0:T(8,128)}, f32[32,768]{1,0:T(8,128)}) custom-call(f32[16,128]{1,0:T(8,128)} %get-tuple-element.25.par, f32[32,768]{1,0:T(8,128)} %get-tuple-element.37.qp, f32[32,768]{1,0:T(8,128)} %get-tuple-element.38.own, f32[32,768]{1,0:T(8,128)} %copy-done.6, f32[32,768]{1,0:T(8,128)} %copy-done.7, f32[32,128]{1,0:T(8,128)} %get-tuple-element.39.hmat, ...), custom_call_target="tpu_custom_call" | custom-call | flops 100000000 | bytes 1000000 | tf_op jit(solution)/shard_map/planes/pallas_call | solution.py:497
  80.0 3.2 %collective-permute-start.4 = (f32[32,768]{1,0:T(8,128)}, f32[32,768]{1,0:T(8,128)S(1)}, u32[]{:S(2)}, u32[]{:S(2)}) collective-permute-start(f32[32,768]{1,0:T(8,128)} %get-tuple-element.41.d0), channel_id=1, source_target_pairs={{0,32},{32,64},{64,96},{96,0},{1,33},{33,65},{65,97},{97,1},{2,34}... | collective-permute-start | bytes 294920 | tf_op jit(solution)/shard_map/ppermute | solution.py:509
  83.2 0.0 collective-permute-start.5
  83.2 0.4 collective-permute-start.6
  83.6 0.0 all-to-all-done.1.a
  83.6 0.9 copy-done
  84.5 2.1 %corner.1.c0 = f32[8,768]{1,0:T(8,128)} custom-call(f32[32,2,24,128]{3,2,1,0:T(8,128)} %copy-done), custom_call_target="tpu_custom_call" | custom-call | flops 1000000 | bytes 1000000 | tf_op jit(solution)/shard_map/corner/pallas_call | solution.py:513
  86.6 2.9 %collective-permute-start.7 = (f32[8,768]{1,0:T(8,128)}, f32[8,768]{1,0:T(8,128)S(1)}, u32[]{:S(2)}, u32[]{:S(2)}) collective-permute-start(f32[8,768]{1,0:T(8,128)} %corner.1.c0), channel_id=1, source_target_pairs={{0,32},{32,64},{64,96},{96,0},{1,33},{33,65},{65,97},{97,1},{2,34}... | collective-permute-start | bytes 73736 | tf_op jit(solution)/shard_map/ppermute | solution.py:509
  89.5 3.0 %collective-permute-start.8 = (f32[8,768]{1,0:T(8,128)}, f32[8,768]{1,0:T(8,128)S(1)}, u32[]{:S(2)}, u32[]{:S(2)}) collective-permute-start(f32[8,768]{1,0:T(8,128)} %corner.1.c0), channel_id=1, source_target_pairs={{0,64},{32,96},{64,0},{96,32},{1,65},{33,97},{65,1},{97,33},{2,66}... | collective-permute-start | bytes 73736 | tf_op jit(solution)/shard_map/ppermute | solution.py:509
  92.5 0.0 collective-permute-done.4.d1
  92.5 0.0 collective-permute-start.9
  92.5 0.0 collective-permute-done.5.d2
  92.5 0.0 copy-start.3
  92.5 0.0 collective-permute-done.6.d3
  92.5 0.0 collective-permute-done.7.c1
  92.5 0.0 copy-start.8
  92.5 1.6 %collective-permute-done.8.c2 = f32[8,768]{1,0:T(8,128)S(1)} collective-permute-done((f32[8,768]{1,0:T(8,128)}, f32[8,768]{1,0:T(8,128)S(1)}, u32[]{:S(2)}, u32[]{:S(2)}) %collective-permute-start.8) | collective-permute-done | bytes 24608 | tf_op jit(solution)/shard_map/ppermute | solution.py:509
  94.2 3.3 %collective-permute-done.9.c3 = f32[8,768]{1,0:T(8,128)S(1)} collective-permute-done((f32[8,768]{1,0:T(8,128)}, f32[8,768]{1,0:T(8,128)S(1)}, u32[]{:S(2)}, u32[]{:S(2)}) %collective-permute-start.9) | collective-permute-done | bytes 24608 | tf_op jit(solution)/shard_map/ppermute | solution.py:509
  97.4 0.0 copy-done.3
  97.5 0.6 copy-done.11
  98.0 9.7 %final.1 = f32[16,768,128]{2,1,0:T(8,128)} custom-call(f32[16,128]{1,0:T(8,128)} %get-tuple-element.25.par, f32[16,768,128]{2,1,0:T(8,128)} %get-tuple-element.35.base, f32[32,2,24,128]{3,2,1,0:T(8,128)} %copy-done, f32[32,768]{1,0:T(8,128)} %get-tuple-element.41.d0, f32[32,768]{1,0:T(8,128)} %copy-done.2, f32[32,768]{1,0:T(8,128)} %copy-done.3, ...), custom_call_target="tpu_custom_call" | custom-call | flops 1000000000 | bytes 13000000 | tf_op jit(solution)/shard_map/final/pallas_call | solution.py:524
  (11 shorter events, 0.0 us)
Async XLA Ops:
  8.1 10.1 %collective-permute-start = (f32[8,768]{1,0:T(8,128)}, f32[8,768]{1,0:T(8,128)S(1)}, u32[]{:S(2)}, u32[]{:S(2)}) collective-permute-start(f32[8,768]{1,0:T(8,128)} %get-tuple-element.31), channel_id=1, source_target_pairs={{0,32},{32,64},{64,96},{1,33},{33,65},{65,97},{2,34},{34,66},{66,9... | collective-permute-start | bytes 73736 | tf_op jit(solution)/shard_map/ppermute | solution.py:408
  14.3 6.9 %collective-permute-start.1 = (f32[8,768]{1,0:T(8,128)}, f32[8,768]{1,0:T(8,128)S(1)}, u32[]{:S(2)}, u32[]{:S(2)}) collective-permute-start(f32[8,768]{1,0:T(8,128)} %get-tuple-element.31), channel_id=1, source_target_pairs={{32,0},{64,32},{96,64},{33,1},{65,33},{97,65},{34,2},{66,34},{98,6... | collective-permute-start | bytes 73736 | tf_op jit(solution)/shard_map/ppermute | solution.py:409
  18.1 3.0 %copy-start.10 = (f32[8,768]{1,0:T(8,128)}, f32[8,768]{1,0:T(8,128)S(1)}, u32[]{:S(2)}) copy-start(f32[8,768]{1,0:T(8,128)S(1)} %collective-permute-done.from_left) | copy-start | bytes 73732
  21.1 0.6 copy-start.12
  25.6 26.3 %all-to-all-start = ((f32[32,2,24,128]{3,2,1,0:T(8,128)}), f32[32,2,24,128]{3,2,1,0:T(8,128)S(1)}, u32[]{:S(2)}, u32[]{:S(2)}) async-start(f32[32,2,24,128]{3,2,1,0:T(8,128)} %edges.1), calls=%async_computation | async-start | bytes 1572864 | tf_op jit(solution)/shard_map/all_to_all | solution.py:450
  33.6 29.2 %copy-start.5 = (f32[32,768]{1,0:T(8,128)S(1)}, f32[32,768]{1,0:T(8,128)}, u32[]{:S(2)}) copy-start(f32[32,768]{1,0:T(8,128)} %get-tuple-element.38.own) | copy-start | bytes 294916
  51.9 0.9 copy-start.1
  55.1 28.6 %all-to-all-start.1 = ((f32[32,2,24,128]{3,2,1,0:T(8,128)}), f32[32,2,24,128]{3,2,1,0:T(8,128)S(1)}, u32[]{:S(2)}, u32[]{:S(2)}) async-start(f32[32,2,24,128]{3,2,1,0:T(8,128)} %solver.1), calls=%async_computation.1 | async-start | bytes 1572864 | tf_op jit(solution)/shard_map/all_to_all | solution.py:484
  62.8 13.5 %collective-permute-start.2 = (f32[32,768]{1,0:T(8,128)S(1)}, f32[32,768]{1,0:T(8,128)S(1)}, u32[]{:S(2)}, u32[]{:S(2)}) collective-permute-start(f32[32,768]{1,0:T(8,128)S(1)} %copy-done.5), channel_id=1, source_target_pairs={{0,32},{32,64},{64,96},{1,33},{33,65},{65,97},{2,34},{34,66},{66,9... | collective-permute-start | bytes 294920 | tf_op jit(solution)/shard_map/ppermute | solution.py:452
  66.5 9.9 %collective-permute-start.3 = (f32[32,768]{1,0:T(8,128)S(1)}, f32[32,768]{1,0:T(8,128)S(1)}, u32[]{:S(2)}, u32[]{:S(2)}) collective-permute-start(f32[32,768]{1,0:T(8,128)S(1)} %copy-done.5), channel_id=1, source_target_pairs={{32,0},{64,32},{96,64},{33,1},{65,33},{97,65},{34,2},{66,34},{98,6... | collective-permute-start | bytes 294920 | tf_op jit(solution)/shard_map/ppermute | solution.py:453
  76.3 0.7 copy-start.6
  76.4 0.7 copy-start.7
  80.0 12.5 %collective-permute-start.4 = (f32[32,768]{1,0:T(8,128)}, f32[32,768]{1,0:T(8,128)S(1)}, u32[]{:S(2)}, u32[]{:S(2)}) collective-permute-start(f32[32,768]{1,0:T(8,128)} %get-tuple-element.41.d0), channel_id=1, source_target_pairs={{0,32},{32,64},{64,96},{96,0},{1,33},{33,65},{65,97},{97,1},{2,34}... | collective-permute-start | bytes 294920 | tf_op jit(solution)/shard_map/ppermute | solution.py:509
  83.2 9.2 %collective-permute-start.5 = (f32[32,768]{1,0:T(8,128)}, f32[32,768]{1,0:T(8,128)S(1)}, u32[]{:S(2)}, u32[]{:S(2)}) collective-permute-start(f32[32,768]{1,0:T(8,128)} %get-tuple-element.41.d0), channel_id=1, source_target_pairs={{0,64},{32,96},{64,0},{96,32},{1,65},{33,97},{65,1},{97,33},{2,66}... | collective-permute-start | bytes 294920 | tf_op jit(solution)/shard_map/ppermute | solution.py:509
  83.2 9.2 %collective-permute-start.6 = (f32[32,768]{1,0:T(8,128)}, f32[32,768]{1,0:T(8,128)S(1)}, u32[]{:S(2)}, u32[]{:S(2)}) collective-permute-start(f32[32,768]{1,0:T(8,128)} %get-tuple-element.41.d0), channel_id=1, source_target_pairs={{0,96},{32,0},{64,32},{96,64},{1,97},{33,1},{65,33},{97,65},{2,98}... | collective-permute-start | bytes 294920 | tf_op jit(solution)/shard_map/ppermute | solution.py:509
  83.6 0.9 copy-start
  86.6 5.9 %collective-permute-start.7 = (f32[8,768]{1,0:T(8,128)}, f32[8,768]{1,0:T(8,128)S(1)}, u32[]{:S(2)}, u32[]{:S(2)}) collective-permute-start(f32[8,768]{1,0:T(8,128)} %corner.1.c0), channel_id=1, source_target_pairs={{0,32},{32,64},{64,96},{96,0},{1,33},{33,65},{65,97},{97,1},{2,34}... | collective-permute-start | bytes 73736 | tf_op jit(solution)/shard_map/ppermute | solution.py:509
  89.5 4.7 %collective-permute-start.8 = (f32[8,768]{1,0:T(8,128)}, f32[8,768]{1,0:T(8,128)S(1)}, u32[]{:S(2)}, u32[]{:S(2)}) collective-permute-start(f32[8,768]{1,0:T(8,128)} %corner.1.c0), channel_id=1, source_target_pairs={{0,64},{32,96},{64,0},{96,32},{1,65},{33,97},{65,1},{97,33},{2,66}... | collective-permute-start | bytes 73736 | tf_op jit(solution)/shard_map/ppermute | solution.py:509
  92.5 5.0 %copy-start.2 = (f32[32,768]{1,0:T(8,128)}, f32[32,768]{1,0:T(8,128)S(1)}, u32[]{:S(2)}) copy-start(f32[32,768]{1,0:T(8,128)S(1)} %collective-permute-done.4.d1) | copy-start | bytes 294916
  92.5 5.0 %collective-permute-start.9 = (f32[8,768]{1,0:T(8,128)}, f32[8,768]{1,0:T(8,128)S(1)}, u32[]{:S(2)}, u32[]{:S(2)}) collective-permute-start(f32[8,768]{1,0:T(8,128)} %corner.1.c0), channel_id=1, source_target_pairs={{0,96},{32,0},{64,32},{96,64},{1,97},{33,1},{65,33},{97,65},{2,98}... | collective-permute-start | bytes 73736 | tf_op jit(solution)/shard_map/ppermute | solution.py:509
  92.5 5.0 %copy-start.3 = (f32[32,768]{1,0:T(8,128)}, f32[32,768]{1,0:T(8,128)S(1)}, u32[]{:S(2)}) copy-start(f32[32,768]{1,0:T(8,128)S(1)} %collective-permute-done.5.d2) | copy-start | bytes 294916
  92.5 4.9 %copy-start.4 = (f32[32,768]{1,0:T(8,128)}, f32[32,768]{1,0:T(8,128)S(1)}, u32[]{:S(2)}) copy-start(f32[32,768]{1,0:T(8,128)S(1)} %collective-permute-done.6.d3) | copy-start | bytes 294916
  92.5 4.9 %copy-start.8 = (f32[8,768]{1,0:T(8,128)}, f32[8,768]{1,0:T(8,128)S(1)}, u32[]{:S(2)}) copy-start(f32[8,768]{1,0:T(8,128)S(1)} %collective-permute-done.7.c1) | copy-start | bytes 73732
  94.2 3.3 %copy-start.9 = (f32[8,768]{1,0:T(8,128)}, f32[8,768]{1,0:T(8,128)S(1)}, u32[]{:S(2)}) copy-start(f32[8,768]{1,0:T(8,128)S(1)} %collective-permute-done.8.c2) | copy-start | bytes 73732
  97.4 0.6 copy-start.11

commit v2 on v1

v2 whole, which is shorter than its diff:
```python
import jax
import jax.numpy as jnp
from jax import lax
from jax.experimental import pallas as pl
from jax.experimental.pallas import tpu as pltpu
from jax.sharding import PartitionSpec as P

H, W, D = 16, 768, 128
B = 128
NB = W // B
NP = 32
S = W // NP
T = 16
f32 = jnp.float32
bf16 = jnp.bfloat16
HIGHEST = lax.Precision.HIGHEST


def log_decay(s):
    return jnp.log(2.0 * s / (1.0 + 2.0 * s + jnp.sqrt(1.0 + 4.0 * s)))


def pivots(log_r, length):
    return (
        jnp.exp(log_r)
        * (1.0 - jnp.exp(log_r * (2.0 * length)))
        / (1.0 - jnp.exp(log_r * (2.0 * length + 2.0)))
    )


def influence(log_r, m, i):
    return (
        jnp.exp(log_r * (i + 1.0))
        * (1.0 - jnp.exp(log_r * (2.0 * (m - i))))
        / (1.0 - jnp.exp(log_r * (2.0 * m + 2.0)))
    )


def green(s, log_r, n, i, j):
    low, high = jnp.minimum(i, j), jnp.maximum(i, j)
    return (
        jnp.exp(log_r * (high - low))
        * (1.0 - jnp.exp(log_r * (2.0 * low + 2.0)))
        * (1.0 - jnp.exp(log_r * (2.0 * (n - high))))
        / (jnp.sqrt(1.0 + 4.0 * s) * (1.0 - jnp.exp(log_r * (2.0 * n + 2.0))))
    )


def split(x):
    hi = x.astype(bf16)
    return hi, (x - hi.astype(f32)).astype(bf16)


def dot(a, b):
    return lax.dot_general(a, b, (((1,), (0,)), ((), ())), preferred_element_type=f32)


def iota(shape, dim):
    return lax.broadcasted_iota(jnp.int32, shape, dim)


HEAD, BEFORE_H, BEFORE_W, AH, CH, MH, FROM = 0, 1, 5, 9, 10, 11, 12


def tables_kernel(cpl, slab, wi, di, par, cols, rows, gw3, gd4, spread, hmat, hcol, gwf):
    row = (1, 128)
    sw, sh, sd = (jnp.full(row, cpl[k], f32) for k in range(3))
    lw, lh, ld = log_decay(sw), log_decay(sh), log_decay(sd)
    lane = iota(row, 1)
    k = lane.astype(f32)
    heads = [2.0 - 4.0 * sw - 4.0 * sd, 2.0 * sw, 2.0 * sd]
    for log_r, m in ((lw, float(B)), (lh, float(H)), (ld, float(D))):
        heads += [influence(log_r, m, 0.0), influence(log_r, m, m - 1.0)]
    middle = pivots(lh, float(H // 2))
    heads.append(1.0 / (1.0 - middle * middle))
    head = jnp.zeros(row, f32)
    for at, v in enumerate(heads):
        head = jnp.where(lane == at, v, head)
    par[HEAD : HEAD + 1] = head
    for at, log_r, m, p, q in ((BEFORE_H, lh, float(H), heads[5], heads[6]), (BEFORE_W, lw, float(B), heads[3], heads[4])):
        before = pivots(log_r, m * k)
        inv = 1.0 / (1.0 - p * before)
        w = q * before * inv
        for n, v in enumerate((before, inv, w, q + w * p)):
            par[at + n : at + n + 1] = v
    kc = jnp.minimum(k, H - 1.0)
    ch = pivots(lh, kc + 1.0)
    par[AH : AH + 1] = influence(lh, float(H), kc)
    par[CH : CH + 1] = ch
    par[MH : MH + 1] = ch / sh
    me = slab[0]
    other = lax.bitwise_and(me - lane, 3)
    of, mf = other.astype(f32), jnp.full(row, me, jnp.int32).astype(f32)
    n = float(4 * D)
    for side, (where, beside, inside) in enumerate(
        ((D * mf - 1.0, me - 1, me > 0), (D * mf + D, me + 1, me < 3))
    ):
        spot = jnp.clip(where, 0.0, n - 1.0)
        first = jnp.where(other >= 1, sd * green(sd, ld, n, spot, jnp.maximum(D * of - 1.0, 0.0)), 0.0)
        last = jnp.where(other <= 2, sd * green(sd, ld, n, spot, jnp.minimum(D * of + D, n - 1.0)), 0.0)
        same = jnp.where(other == beside, 1.0, 0.0)
        if side == 0:
            last = last + same
        else:
            first = first + same
        par[FROM + 2 * side : FROM + 2 * side + 1] = jnp.where(inside, first, 0.0)
        par[FROM + 2 * side + 1 : FROM + 2 * side + 2] = jnp.where(inside, last, 0.0)
    tall = iota((B, D), 0).astype(f32)
    lww = jnp.broadcast_to(lw, (B, D))
    cols[0] = influence(lww, float(B), tall)
    cols[1] = influence(lww, float(B), B - 1.0 - tall)
    rows[0:1] = influence(lw, float(B), k)
    rows[1:2] = influence(lw, float(B), B - 1.0 - k)
    gwf[...] = wi[0]
    hi, lo = split(wi[0])
    gw3[:, :B] = hi
    gw3[:, B : 2 * B] = hi
    gw3[:, 2 * B :] = lo
    hi, lo = split(di[0].T)
    gd4[:D, :D] = hi
    gd4[:D, D:] = lo
    gd4[D:, :D] = hi
    gd4[D:, D:] = jnp.zeros((D, D), bf16)
    ad, bd = influence(ld, float(D), k), influence(ld, float(D), D - 1.0 - k)
    line = iota((2 * H, D), 0)
    for h in range(H):
        v = jnp.where(line == h, ad, jnp.where(line == H + h, bd, 0.0))
        hi, lo = split(v)
        at = slice(h * D, (h + 1) * D)
        spread[: 2 * H, at] = hi
        spread[2 * H : 4 * H, at] = hi
        spread[4 * H :, at] = lo
    a = iota((2 * H, 128), 0)
    b = iota((2 * H, 128), 1)
    af = lax.bitwise_and(a, H - 1).astype(f32)
    bfl = lax.bitwise_and(b, H - 1).astype(f32)
    wide_h = jnp.broadcast_to(lh, (2 * H, 128))
    g = green(jnp.broadcast_to(sh, (2 * H, 128)), wide_h, float(H), af, bfl)
    hmat[...] = jnp.where((b < 2 * H) & (lax.shift_right_logical(a, 4) == lax.shift_right_logical(b, 4)), g, 0.0)
    c = iota((H, 128), 0).astype(f32)
    ln = iota((H, 128), 1)
    hcol[...] = influence(jnp.broadcast_to(lh, (H, 128)), float(H), jnp.where(ln == 0, c, H - 1.0 - c))


def sums_kernel(cpl, rho, sig, cr, cs, halo, rv, sv, coef, packed, sems):
    def parts(i):
        at = pl.ds(pl.multiple_of(i * B, B), B)
        return (
            pltpu.make_async_copy(rho.at[:, at, :], rv.at[:, at, :], sems.at[0, i]),
            pltpu.make_async_copy(sig.at[:, at, :], sv.at[:, at, :], sems.at[1, i]),
        )

    for i in range(NB):
        for part in parts(i):
            part.start()
    sh = jnp.full((8, 128), cpl[1], f32)
    lh = log_decay(sh)
    for h in range(H):
        coef[h] = influence(lh, float(H), float(h)) / sh

    R = 32
    lane = iota((R, D), 1)

    def block(i, _):
        for part in parts(i):
            part.wait()
        packs, combs = [], []
        for t in range(B // R):
            at = pl.ds(pl.multiple_of(i * B + t * R, R), R)
            fr = jnp.zeros((R, D), f32)
            tr, fs, ts, pack = fr, fr, fr, fr
            for h in range(H):
                x, y = rv[h, at, :], sv[h, at, :]
                cf = jnp.broadcast_to(coef[h, 0:1, :], (R, D))
                ct = jnp.broadcast_to(coef[H - 1 - h, 0:1, :], (R, D))
                fr, tr, fs, ts = fr + cf * x, tr + ct * x, fs + cf * y, ts + ct * y
                pack = jnp.where((lane == 2 * h) | (lane == 2 * h + 1), pltpu.roll(x, 2 * h + 1, 1), pack)
            cr[0, at, :], cr[1, at, :], cs[0, at, :], cs[1, at, :] = fr, tr, fs, ts
            packs.append(pack)
            combs.append(jnp.where(lane < 2, pltpu.roll(fr, 1, 1), pltpu.roll(tr, 3, 1)))
        at = pl.ds(pl.multiple_of(i * B, B), B)
        packed[...] = jnp.concatenate(packs, axis=0).T[: 2 * H]
        halo[:H, at] = packed[pl.ds(1, H, stride=2), :]
        halo[H : 2 * H, at] = packed[pl.ds(0, H, stride=2), :]
        halo[2 * H :, at] = jnp.concatenate(combs, axis=0).T[:8]
        return 0

    lax.fori_loop(0, NB, block, 0)


def chain_w(yf, yt, par):
    p, q = par[HEAD, 3], par[HEAD, 4]
    before, inv, w, qw = (BEFORE_W + k for k in range(4))
    us = []
    for k in range(NB):
        u = yt[k] + par[w, k] * yf[k]
        us.append(u if k == 0 else u + par[qw, k] * us[-1])
    fs = [None] * NB
    for k in reversed(range(NB)):
        g = yf[k]
        if k > 0:
            g = g + p * us[k - 1]
        if k < NB - 1:
            g = g + q * fs[k + 1]
        fs[k] = g * par[inv, k]
    zero = jnp.zeros_like(yf[0])
    ls = [zero] + [us[k - 1] + par[before, k] * fs[k] for k in range(1, NB)]
    return ls, fs[1:] + [zero]


def solve_wd(x, gw3, gd4):
    hi, lo = split(x)
    z = dot(gw3[:, : 2 * B], jnp.concatenate([hi, lo], axis=0)) + dot(gw3[:, 2 * B :], hi)
    z = jnp.concatenate([z[:, :D], z[:, D:]], axis=0)
    hi, lo = split(z)
    y = dot(jnp.concatenate([hi, lo], axis=1), gd4[...])
    return y[:, :D] + y[:, D:]


def edges_kernel(par, cr, cs, from_left, from_right, gw3, gd4, cols, out, e):
    c0, c1, c2 = par[HEAD, 0], par[HEAD, 1], par[HEAD, 2]
    row = iota((B, D), 0)
    lane = iota((B, D), 1)
    blank = jnp.zeros((B - 8, B), f32)
    for k in range(NB):
        spot = slice(k * B, (k + 1) * B)
        lc = jnp.concatenate([from_left[2 * H :, spot], blank], axis=0).T
        rc = jnp.concatenate([from_right[2 * H :, spot], blank], axis=0).T
        xs = []
        for j in range(2):
            x = cr[j, spot]
            up = pltpu.roll(x, 1, 0)
            up = jnp.where(row == 0, cr[j, k * B - 1 : k * B] if k > 0 else 0.0, up)
            down = pltpu.roll(x, B - 1, 0)
            down = jnp.where(row == B - 1, cr[j, (k + 1) * B : (k + 1) * B + 1] if k < NB - 1 else 0.0, down)
            lcol = lc if j == 0 else pltpu.roll(lc, D - 2, 1)
            left = jnp.where(lane == 0, lcol, pltpu.roll(x, 1, 1))
            right = jnp.where(lane == D - 1, pltpu.roll(rc, D - 2 if j == 0 else D - 4, 1), pltpu.roll(x, D - 1, 1))
            xs.append(cs[j, spot] + c0 * x + c1 * (up + down) + c2 * (left + right))
        y = solve_wd(jnp.concatenate(xs, axis=1), gw3, gd4)
        e[0, spot] = y[:B]
        e[1, spot] = y[B:]
    for j in range(2):
        ls, rs = chain_w(
            [e[j, k * B : k * B + 1] for k in range(NB)], [e[j, k * B + B - 1 : k * B + B] for k in range(NB)], par
        )
        for k in range(NB):
            spot = slice(k * B, (k + 1) * B)
            e[j, spot] = e[j, spot] + cols[0] * ls[k] + cols[1] * rs[k]
        for p in range(NP):
            out[p, j] = e[j, S * p : S * (p + 1)]


def field_kernel(par, rho, sig, gw3, gd4, raw, ew, qp, rv, out, packed, sems):
    sv = out

    def parts(i):
        at = pl.ds(pl.multiple_of(i * B, B), B)
        return (
            pltpu.make_async_copy(rho.at[:, at, :], rv.at[:, at, :], sems.at[0, i]),
            pltpu.make_async_copy(sig.at[:, at, :], out.at[:, at, :], sems.at[1, i]),
        )

    def send(i):
        at = pl.ds(pl.multiple_of(i * B, B), B)
        return pltpu.make_async_copy(out.at[:, at, :], raw.at[:, at, :], sems.at[2, i])

    for i in range(NB):
        for part in parts(i):
            part.start()
    for part in parts(0):
        part.wait()
    c0, c1, c2 = par[HEAD, 0], par[HEAD, 1], par[HEAD, 2]
    row = iota((B, D), 0)
    half = H // 2
    meet = par[HEAD, 9]

    def block(i, _):
        @pl.when(i < NB - 1)
        def _():
            for part in parts(jnp.minimum(i + 1, NB - 1)):
                part.wait()

        here = pl.ds(pl.multiple_of(i * B, B), B)
        before = pl.ds(pl.multiple_of(jnp.maximum(i * B - 8, 0), 8), 8)
        after = pl.ds(pl.multiple_of(jnp.minimum(i * B + B, W - 8), 8), 8)
        for h in range(H):
            x = rv[h, here, :]
            first = jnp.where(i > 0, rv[h, before, :][7:8], 0.0)
            last = jnp.where(i < NB - 1, rv[h, after, :][0:1], 0.0)
            up = jnp.where(row == 0, first, pltpu.roll(x, 1, 0))
            down = jnp.where(row == B - 1, last, pltpu.roll(x, B - 1, 0))
            out[h, here, :] = (
                sv[h, here, :] + c0 * x + c1 * (up + down) + c2 * (pltpu.roll(x, 1, 1) + pltpu.roll(x, D - 1, 1))
            )

        def tile(j, _):
            at = pl.ds(pl.multiple_of(i * B + T * j, T), T)
            top, bottom = [None] * half, [None] * half
            for h in range(half):
                m, c = par[MH, h], par[CH, h]
                a, b = m * out[h, at, :], m * out[H - 1 - h, at, :]
                top[h] = a if h == 0 else a + c * top[h - 1]
                bottom[h] = b if h == 0 else b + c * bottom[h - 1]
            c = par[CH, half - 1]
            x = (top[half - 1] + c * bottom[half - 1]) * meet
            y = bottom[half - 1] + c * x
            for h in reversed(range(half)):
                if h < half - 1:
                    c = par[CH, h]
                    x, y = top[h] + c * x, bottom[h] + c * y
                out[h, at, :] = x - 2.0 * rv[h, at, :]
                out[H - 1 - h, at, :] = y - 2.0 * rv[H - 1 - h, at, :]
            return 0

        lax.fori_loop(0, B // T, tile, 0)
        lane = iota((B, D), 1)
        pack = jnp.zeros((B, D), f32)
        for g in range(H // 2):
            y = solve_wd(jnp.concatenate([out[2 * g, here, :], out[2 * g + 1, here, :]], axis=1), gw3, gd4)
            for side in range(2):
                h = 2 * g + side
                part = y[side * B : (side + 1) * B]
                ew[i, 0, h : h + 1, :] = part[0:1]
                ew[i, 1, h : h + 1, :] = part[B - 1 : B]
                out[h, here, :] = part + rv[h, here, :]
                pack = jnp.where((lane == 2 * h) | (lane == 2 * h + 1), pltpu.roll(part, 2 * h + 1, 1), pack)
        packed[...] = pack.T[: 2 * H]
        qp[:H, here] = packed[pl.ds(1, H, stride=2), :]
        qp[H:, here] = packed[pl.ds(0, H, stride=2), :]
        send(i).start()
        return 0

    lax.fori_loop(0, NB, block, 0)
    for i in range(NB):
        send(i).wait()


def planes_kernel(par, ew, qp, own, from_left, from_right, hmat, rows, gwf, planes, u, fix):
    ls, rs = chain_w([ew[k, 0] for k in range(NB)], [ew[k, 1] for k in range(NB)], par)
    for k in range(NB):
        fix[k, 0] = ls[k]
        fix[k, 1] = rs[k]
    v = jnp.concatenate([from_left[H : 2 * H] - own[H : 2 * H], from_right[:H] - own[:H]], axis=0)
    v = jnp.dot(hmat[:, : 2 * H], v, precision=HIGHEST, preferred_element_type=f32)
    parts = []
    for k in range(NB):
        spot = slice(k * B, (k + 1) * B)
        solved = lax.dot_general(
            v[:, spot], gwf[...], (((1,), (1,)), ((), ())), precision=HIGHEST, preferred_element_type=f32
        )
        parts.append(jnp.concatenate([2.0 * solved, qp[:, spot]], axis=0))
    ls, rs = chain_w([a[:, 0:1] for a in parts], [a[:, B - 1 : B] for a in parts], par)
    p, q = par[HEAD, 7], par[HEAD, 8]
    for k in range(NB):
        spot = slice(k * B, (k + 1) * B)
        both = parts[k] + ls[k] * rows[0:1] + rs[k] * rows[1:2]
        ul, ur = both[:H], both[H : 2 * H]
        u[:, spot] = both[: 2 * H]
        planes[:H, spot] = both[2 * H : 3 * H] + p * ul + q * ur
        planes[H:, spot] = both[3 * H :] + q * ul + p * ur


def solver_kernel(par, y, out, us):
    p, q = par[HEAD, 5], par[HEAD, 6]
    before, inv, w, qw = (BEFORE_H + k for k in range(4))
    u = y[0, 1] + par[w, 0] * y[0, 0]
    us[0] = u
    for k in range(1, NP):
        u = y[k, 1] + par[w, k] * y[k, 0] + par[qw, k] * u
        us[k] = u
    zero = jnp.zeros_like(u)
    out[NP - 1, 1] = zero
    f = zero
    for k in reversed(range(NP)):
        g = y[k, 0]
        if k > 0:
            g = g + p * us[k - 1]
        f = (g + q * f) * par[inv, k]
        if k > 0:
            out[k, 0] = us[k - 1] + par[before, k] * f
            out[k - 1, 1] = f
    out[0, 0] = zero


def corner_kernel(a, out, wide):
    lane = iota((S, D), 1)
    for p in range(NP):
        wide[S * p : S * (p + 1)] = jnp.where(lane < 2, pltpu.roll(a[p, 0], 1, 1), pltpu.roll(a[p, 1], 3, 1))
    for k in range(NB):
        out[:, k * B : (k + 1) * B] = wide[k * B : (k + 1) * B].T[:8]


def nearly_kernel(par, raw, a, fix, cols, out, lr, sems):
    def part(i):
        at = pl.ds(pl.multiple_of(i * B, B), B)
        return pltpu.make_async_copy(raw.at[:, at, :], out.at[:, at, :], sems.at[i])

    for i in range(NB):
        part(i).start()
    for p in range(NP):
        for j in range(2):
            lr[j, S * p : S * (p + 1)] = a[p, j]
    R = 32

    def block(i, _):
        part(i).wait()
        for t in range(B // R):
            at = pl.ds(pl.multiple_of(i * B + t * R, R), R)
            ca, cb = cols[0, t * R : (t + 1) * R], cols[1, t * R : (t + 1) * R]
            l, r = lr[0, at, :], lr[1, at, :]
            for h in range(H):
                v = ca * fix[i, 0, h : h + 1, :] + cb * fix[i, 1, h : h + 1, :]
                out[h, at, :] = out[h, at, :] + v + (par[AH, h] * l + par[AH, H - 1 - h] * r)
        return 0

    lax.fori_loop(0, NB, block, 0)


def final_kernel(par, base, d0, d1, d2, d3, c0, c1, c2, c3, u, hcol, spread, out, tall, buf, sems):
    ds, cs = (d0, d1, d2, d3), (c0, c1, c2, c3)
    sides = []
    for side in range(2):
        first, last = FROM + 2 * side, FROM + 2 * side + 1
        own = u[H * side : H * (side + 1)]
        for k in range(4):
            own = own + par[first, k] * ds[k][:H] + par[last, k] * ds[k][H:]
        gam = []
        for plane in range(2):
            g = 0.0
            for k in range(4):
                t, f = cs[k][2 * plane : 2 * plane + 1], cs[k][2 * plane + 1 : 2 * plane + 2]
                g = g + par[first, k] * f + par[last, k] * t
            gam.append(g)
        sides.append(own + hcol[:, 0:1] * gam[0] + hcol[:, 1:2] * gam[1])
    both = jnp.concatenate(sides + [jnp.zeros((D - 2 * H, W), f32)], axis=0)
    for k in range(NB):
        tall[k * B : (k + 1) * B] = both[:, k * B : (k + 1) * B].T

    def send(i):
        at = pl.ds(pl.multiple_of(i * B, B), B)
        return pltpu.make_async_copy(buf.at[:, at, :], out.at[:, at, :], sems.at[i])

    def block(i, _):
        at = pl.ds(pl.multiple_of(i * B, B), B)
        hi, lo = split(tall[at, : 2 * H])
        wide = dot(jnp.concatenate([hi, lo, hi], axis=1), spread[...])
        for h in range(H):
            buf[h, at, :] = base[h, at, :] + wide[:, h * D : (h + 1) * D]
        send(i).start()
        return 0

    lax.fori_loop(0, NB, block, 0)
    for i in range(NB):
        send(i).wait()


SMEM = pl.BlockSpec(memory_space=pltpu.SMEM)
VMEM = pl.BlockSpec(memory_space=pltpu.VMEM)
HBM = pl.BlockSpec(memory_space=pltpu.HBM)


def limit(mib):
    return pltpu.CompilerParams(vmem_limit_bytes=mib * 2**20)


def held(*shape, dtype=f32):
    return pltpu.VMEM(shape, dtype)


def near(x):
    return pltpu.with_memory_space_constraint(x, pltpu.VMEM)


def far(x):
    return pltpu.with_memory_space_constraint(x, pltpu.HBM)


def cost(flops, bytes_accessed):
    return pl.CostEstimate(flops=flops, bytes_accessed=bytes_accessed, transcendentals=0)


def per_device(density, source, coupling, width_inverse, height_inverse, depth_inverse):
    slab = lax.axis_index("slab")
    slabs = lax.axis_size("slab")
    up = [(k, k + 1) for k in range(slabs - 1)]
    down = [(k + 1, k) for k in range(slabs - 1)]
    grid = [pltpu.VMEM((H, W, D), f32)]

    cr, cs, halo = pl.pallas_call(
        sums_kernel,
        in_specs=[SMEM, HBM, HBM],
        out_specs=[VMEM] * 3,
        out_shape=[held(2, W, D), held(2, W, D), held(2 * H + 8, W)],
        scratch_shapes=grid * 2
        + [pltpu.VMEM((H, 8, 128), f32), pltpu.VMEM((2 * H, B), f32), pltpu.SemaphoreType.DMA((2, NB))],
        compiler_params=limit(24),
        name="sums",
        cost_estimate=cost(10**7, 14 * 10**6),
    )(coupling, far(density), far(source))
    halo_left = lax.ppermute(halo, "slab", up)
    halo_right = lax.ppermute(halo, "slab", down)

    first = pl.BlockSpec((1, B, B), lambda *_: (0, 0, 0))
    shapes = [
        ((16, 128), f32),
        ((2, B, D), f32),
        ((8, 128), f32),
        ((B, 3 * B), bf16),
        ((2 * D, 2 * D), bf16),
        ((6 * H, H * D), bf16),
        ((2 * H, 128), f32),
        ((H, 128), f32),
        ((B, B), f32),
    ]
    par, cols, rows, gw3, gd4, spread, hmat, hcol, gwf = pl.pallas_call(
        tables_kernel,
        grid=(1,),
        in_specs=[SMEM, SMEM, first, first],
        out_specs=[pl.BlockSpec(shape, lambda *_, n=len(shape): (0,) * n) for shape, _ in shapes],
        out_shape=[jax.ShapeDtypeStruct(*shapes[0])] + [held(*shape, dtype=kind) for shape, kind in shapes[1:]],
        compiler_params=limit(8),
        name="tables",
        cost_estimate=cost(10**7, 10**6),
    )(coupling, slab.reshape(1), width_inverse, depth_inverse)

    edges = pl.pallas_call(
        edges_kernel,
        in_specs=[SMEM] + [VMEM] * 7,
        out_specs=VMEM,
        out_shape=held(NP, 2, S, D),
        scratch_shapes=[pltpu.VMEM((2, W, D), f32)],
        compiler_params=limit(8),
        name="edges",
        cost_estimate=cost(10**8, 3 * 10**6),
    )(par, near(cr), near(cs), near(halo_left), near(halo_right), near(gw3), near(gd4), near(cols))
    arrived = lax.all_to_all(edges, "pencil", 0, 0, tiled=True)

    raw, ew, qp = pl.pallas_call(
        field_kernel,
        in_specs=[SMEM, HBM, HBM, VMEM, VMEM],
        out_specs=[HBM, VMEM, VMEM],
        out_shape=[pltpu.HBM((H, W, D), f32), held(NB, 2, H, D), held(2 * H, W)],
        scratch_shapes=grid * 2 + [pltpu.VMEM((2 * H, B), f32), pltpu.SemaphoreType.DMA((3, NB))],
        compiler_params=limit(24),
        name="field",
        cost_estimate=cost(4 * 10**9, 19 * 10**6),
    )(par, far(density), far(source), near(gw3), near(gd4))

    arrived, ew = lax.optimization_barrier((arrived, ew))
    solved = pl.pallas_call(
        solver_kernel,
        in_specs=[SMEM, VMEM],
        out_specs=VMEM,
        out_shape=held(NP, 2, S, D),
        scratch_shapes=[pltpu.VMEM((NP, S, D), f32)],
        compiler_params=limit(8),
        name="solver",
        cost_estimate=cost(10**6, 2 * 10**6),
    )(par, near(arrived))
    outside = lax.all_to_all(solved, "pencil", 0, 0, tiled=True)

    planes, u, fix = pl.pallas_call(
        planes_kernel,
        in_specs=[SMEM] + [VMEM] * 8,
        out_specs=[VMEM] * 3,
        out_shape=[held(2 * H, W), held(2 * H, W), held(NB, 2, H, D)],
        compiler_params=limit(8),
        name="planes",
        cost_estimate=cost(10**8, 10**6),
    )(par, near(ew), near(qp), near(halo), near(halo_left), near(halo_right), near(hmat), near(rows), near(gwf))

    def turned(value):
        return [value] + [
            lax.ppermute(value, "slab", [(k, (k + d) % slabs) for k in range(slabs)]) for d in range(1, slabs)
        ]

    planes_all = turned(planes)
    outside = near(outside)
    corners = pl.pallas_call(
        corner_kernel,
        in_specs=[VMEM],
        out_specs=VMEM,
        out_shape=held(8, W),
        scratch_shapes=[pltpu.VMEM((W, D), f32)],
        compiler_params=limit(8),
        name="corner",
        cost_estimate=cost(10**6, 10**6),
    )(outside)
    corners_all = turned(corners)
    base = pl.pallas_call(
        nearly_kernel,
        in_specs=[SMEM, HBM] + [VMEM] * 3,
        out_specs=VMEM,
        out_shape=held(H, W, D),
        scratch_shapes=[pltpu.VMEM((2, W, D), f32), pltpu.SemaphoreType.DMA((NB,))],
        compiler_params=limit(8),
        name="nearly",
        cost_estimate=cost(10**8, 7 * 10**6),
    )(par, far(raw), outside, near(fix), near(cols))
    return pl.pallas_call(
        final_kernel,
        in_specs=[SMEM] + [VMEM] * 12,
        out_specs=HBM,
        out_shape=pltpu.HBM((H, W, D), f32),
        scratch_shapes=[pltpu.VMEM((W, D), f32), *grid, pltpu.SemaphoreType.DMA((NB,))],
        compiler_params=limit(16),
        name="final",
        cost_estimate=cost(10**9, 13 * 10**6),
    )(par, near(base), *[near(v) for v in planes_all], *[near(v) for v in corners_all], near(u), near(hcol), near(spread))


def solution(mesh):
    in_specs = (P("pencil", None, "slab"), P("pencil", None, "slab"), P(), P(), P(), P())
    out_specs = P("pencil", None, "slab")
    return jax.shard_map(per_device, mesh=mesh, in_specs=in_specs, out_specs=out_specs, check_vma=False)
```

time: 109 us -> 79.1 us (0.73)
  Pallas kernels: 57.1 us -> 37.1 us
  starting transfers between devices: 38.9 us -> 34.6 us
  local copies, waits for them, and re-layouts: 3.63 us -> 0.73 us
  waiting for transfers between devices: 7.91 us -> 6.15 us
    pallas_call x9, Pallas kernels: 57.1 us -> 37.1 us  [the longest x1 15.6 us: per_device(): pl.pallas_call(field_kernel, in_specs=[SMEM, HBM, HBM, VMEM, VMEM], out_s...]
    ppermute x4 -> x2, starting transfers between devices: 13.6 us -> 8.12 us  [the longest x1 4.83 us: per_device(): halo_left = lax.ppermute(halo, 'slab', up)]
    all_to_all x1, waiting for transfers between devices: 0.01 us -> 5.11 us  [per_device(): outside = lax.all_to_all(solved, 'pencil', 0, 0, tiled=True)]
    ppermute x6, waiting for transfers between devices: 4.91 us -> 0.02 us  [turned(): lax.ppermute(value, 'slab', [(k, (k + d) % slabs) for k in range(slabs)])]
    unnamed x26 -> x8, local copies, waits for them, and re-layouts: 3.63 us -> 0.73 us
    ppermute x4 -> x2, waiting for transfers between devices: 3 us -> 1.02 us  [the longest x1 1.02 us: per_device(): halo_left = lax.ppermute(halo, 'slab', up)]
  transfers between devices with their start and end apart: 12 -> 10, of which waited for: 3 -> 2; matrix products, arithmetic and copies ran while one was open for 0% -> 0% of each run, Pallas kernels for 31% -> 29%
where the time goes in v2:
time: 79.1 us; the launch traced here: 78.7 us
  Pallas kernels  37.1 us (47%)
  starting transfers between devices  34.6 us (44%)
  waiting for transfers between devices  6.15 us (8%)
    pallas_call x1, Pallas kernels, per_device(): pl.pallas_call(field_kernel, in_specs=[SMEM, HBM, HBM, VMEM, VMEM], out_s...  15.6 us
    ppermute x6, starting transfers between devices, turned(): lax.ppermute(value, 'slab', [(k, (k + d) % slabs) for k in range(slabs)])  10 us
    all_to_all x1, starting transfers between devices, per_device(): arrived = lax.all_to_all(edges, 'pencil', 0, 0, tiled=True)  8.66 us
    all_to_all x1, starting transfers between devices, per_device(): outside = lax.all_to_all(solved, 'pencil', 0, 0, tiled=True)  7.76 us
    pallas_call x1, Pallas kernels, per_device(): pl.pallas_call(sums_kernel, in_specs=[SMEM, HBM, HBM], out_specs=[VMEM] *...  5.68 us
    all_to_all x1, waiting for transfers between devices, per_device(): outside = lax.all_to_all(solved, 'pencil', 0, 0, tiled=True)  5.11 us
    ppermute x1, starting transfers between devices, per_device(): halo_left = lax.ppermute(halo, 'slab', up)  4.83 us
    pallas_call x1, Pallas kernels, per_device(): pl.pallas_call(final_kernel, in_specs=[SMEM] + [VMEM] * 12, out_specs=HBM...  4.05 us
  transfers between devices with their start and end apart: 10, of which 2 were waited for; matrix products, arithmetic and copies ran while one was open for 0% of the time, Pallas kernels for 29%

profile of v2, /device:TPU:1, one launch (start us, length us, event | category | flops | bytes accessed | tf_op | source)
XLA Modules:
  0.0 78.7 jit_solution(1911998450491492699)
XLA Ops:
  0.0 0.0 copy-start.1
  0.0 0.0 copy-start
  0.0 0.0 copy-start.2
  0.0 0.7 copy-done.2
  0.7 0.0 copy-start.3
  0.7 5.7 %sums.1 = (f32[2,768,128]{2,1,0:T(8,128)S(1)}, f32[2,768,128]{2,1,0:T(8,128)S(1)}, f32[40,768]{1,0:T(8,128)S(1)}) custom-call(f32[3]{0:T(128)S(1)} %copy-done.2, f32[16,768,128]{2,1,0:T(8,128)} %rho.3, f32[16,768,128]{2,1,0:T(8,128)} %sig.3), custom_call_target="tpu_custom_call" | custom-call | flops 10000000 | bytes 14000000 | tf_op jit(solution)/shard_map/sums/pallas_call | solution.py:490
  6.4 3.3 %collective-permute-start.1 = (f32[40,768]{1,0:T(8,128)S(1)}, f32[40,768]{1,0:T(8,128)S(1)}, u32[]{:S(2)}, u32[]{:S(2)}) collective-permute-start(f32[40,768]{1,0:T(8,128)S(1)} %get-tuple-element.31.own), channel_id=1, source_target_pairs={{32,0},{64,32},{96,64},{33,1},{65,33},{97,65},{34,2},{66,34},{98,6... | collective-permute-start | bytes 368648 | tf_op jit(solution)/shard_map/ppermute | solution.py:502
  9.7 4.8 %collective-permute-start = (f32[40,768]{1,0:T(8,128)S(1)}, f32[40,768]{1,0:T(8,128)S(1)}, u32[]{:S(2)}, u32[]{:S(2)}) collective-permute-start(f32[40,768]{1,0:T(8,128)S(1)} %get-tuple-element.31.own), channel_id=1, source_target_pairs={{0,32},{32,64},{64,96},{1,33},{33,65},{65,97},{2,34},{34,66},{66,9... | collective-permute-start | bytes 368648 | tf_op jit(solution)/shard_map/ppermute | solution.py:501
  14.6 0.0 copy-done.1
  14.6 0.0 copy-done
  14.6 0.0 copy-done.3
  14.6 0.8 tables.1
  15.4 0.0 collective-permute-done.1.from_right
  15.4 1.0 %collective-permute-done.from_left = f32[40,768]{1,0:T(8,128)S(1)} collective-permute-done((f32[40,768]{1,0:T(8,128)S(1)}, f32[40,768]{1,0:T(8,128)S(1)}, u32[]{:S(2)}, u32[]{:S(2)}) %collective-permute-start) | collective-permute-done | bytes 122912 | tf_op jit(solution)/shard_map/ppermute | solution.py:501
  16.4 3.1 %edges.1 = f32[32,2,24,128]{3,2,1,0:T(8,128)} custom-call(f32[16,128]{1,0:T(8,128)S(1)} %get-tuple-element.25.par, f32[2,768,128]{2,1,0:T(8,128)S(1)} %get-tuple-element.29.cr, f32[2,768,128]{2,1,0:T(8,128)S(1)} %get-tuple-element.30.cs, f32[40,768]{1,0:T(8,128)S(1)} %collective-permute-done.from_left, f32[40,768]{1,0:T(8,128)S(1)} %collective-permute-done.1.from_right, ...), custom_call_target="tpu_custom_call" | custom-call | flops 100000000 | bytes 3000000 | tf_op jit(solution)/shard_map/edges/pallas_call | solution.py:527
  19.5 8.7 %all-to-all-start = ((f32[32,2,24,128]{3,2,1,0:T(8,128)}), f32[32,2,24,128]{3,2,1,0:T(8,128)S(1)}, u32[]{:S(2)}, u32[]{:S(2)}) async-start(f32[32,2,24,128]{3,2,1,0:T(8,128)} %edges.1), calls=%async_computation | async-start | bytes 1572864 | tf_op jit(solution)/shard_map/all_to_all | solution.py:537
  28.2 15.6 %field.1 = (f32[16,768,128]{2,1,0:T(8,128)}, f32[6,2,16,128]{3,2,1,0:T(8,128)S(1)}, f32[32,768]{1,0:T(8,128)S(1)}) custom-call(f32[16,128]{1,0:T(8,128)S(1)} %get-tuple-element.25.par, f32[16,768,128]{2,1,0:T(8,128)} %rho.3, f32[16,768,128]{2,1,0:T(8,128)} %sig.3, bf16[128,384]{1,0:T(8,128)(2,1)S(1)} %get-tuple-element.26.gw3, ...), custom_call_target="tpu_custom_call" | custom-call | flops 4000000000 | bytes 19000000 | tf_op jit(solution)/shard_map/field/pallas_call | solution.py:539
  43.8 0.0 all-to-all-done.y
  43.8 1.8 %solver.1 = f32[32,2,24,128]{3,2,1,0:T(8,128)} custom-call(f32[16,128]{1,0:T(8,128)S(1)} %get-tuple-element.25.par, f32[32,2,24,128]{3,2,1,0:T(8,128)S(1)} %all-to-all-done.y), custom_call_target="tpu_custom_call" | custom-call | flops 1000000 | bytes 2000000 | tf_op jit(solution)/shard_map/solver/pallas_call | solution.py:551
  45.6 7.8 %all-to-all-start.1 = ((f32[32,2,24,128]{3,2,1,0:T(8,128)}), f32[32,2,24,128]{3,2,1,0:T(8,128)S(1)}, u32[]{:S(2)}, u32[]{:S(2)}) async-start(f32[32,2,24,128]{3,2,1,0:T(8,128)} %solver.1), calls=%async_computation.1 | async-start | bytes 1572864 | tf_op jit(solution)/shard_map/all_to_all | solution.py:561
  53.3 1.9 %planes.1 = (f32[32,768]{1,0:T(8,128)S(1)}, f32[32,768]{1,0:T(8,128)S(1)}, f32[6,2,16,128]{3,2,1,0:T(8,128)S(1)}) custom-call(f32[16,128]{1,0:T(8,128)S(1)} %get-tuple-element.25.par, f32[6,2,16,128]{3,2,1,0:T(8,128)S(1)} %get-tuple-element.35.ew, f32[32,768]{1,0:T(8,128)S(1)} %get-tuple-element.36.qp, f32[40,768]{1,0:T(8,128)S(1)} %get-tuple-element.31.own, ...), custom_call_target="tpu_custom_call" | custom-call | flops 100000000 | bytes 1000000 | tf_op jit(solution)/shard_map/planes/pallas_call | solution.py:563
  55.3 0.1 collective-permute-start.4
  55.4 5.5 %collective-permute-start.3 = (f32[32,768]{1,0:T(8,128)S(1)}, f32[32,768]{1,0:T(8,128)S(1)}, u32[]{:S(2)}, u32[]{:S(2)}) collective-permute-start(f32[32,768]{1,0:T(8,128)S(1)} %get-tuple-element.41.d0), channel_id=1, source_target_pairs={{0,64},{32,96},{64,0},{96,32},{1,65},{33,97},{65,1},{97,33},{2,66}... | collective-permute-start | bytes 294920 | tf_op jit(solution)/shard_map/ppermute | solution.py:575
  60.9 0.1 collective-permute-start.2
  60.9 5.1 %all-to-all-done.1.a = f32[32,2,24,128]{3,2,1,0:T(8,128)S(1)} async-done(((f32[32,2,24,128]{3,2,1,0:T(8,128)}), f32[32,2,24,128]{3,2,1,0:T(8,128)S(1)}, u32[]{:S(2)}, u32[]{:S(2)}) %all-to-all-start.1) | async-done | bytes 786464 | tf_op jit(solution)/shard_map/all_to_all | solution.py:561
  66.0 0.3 corner.1.c0
  66.4 0.1 collective-permute-start.7
  66.4 4.3 %collective-permute-start.6 = (f32[8,768]{1,0:T(8,128)S(1)}, f32[8,768]{1,0:T(8,128)S(1)}, u32[]{:S(2)}, u32[]{:S(2)}) collective-permute-start(f32[8,768]{1,0:T(8,128)S(1)} %corner.1.c0), channel_id=1, source_target_pairs={{0,64},{32,96},{64,0},{96,32},{1,65},{33,97},{65,1},{97,33},{2,66}... | collective-permute-start | bytes 73736 | tf_op jit(solution)/shard_map/ppermute | solution.py:575
  70.7 0.0 collective-permute-done.4.d3
  70.7 0.1 collective-permute-start.5
  70.8 3.8 %nearly.1.base = f32[16,768,128]{2,1,0:T(8,128)S(1)} custom-call(f32[16,128]{1,0:T(8,128)S(1)} %get-tuple-element.25.par, f32[16,768,128]{2,1,0:T(8,128)} %get-tuple-element.28.raw, f32[32,2,24,128]{3,2,1,0:T(8,128)S(1)} %all-to-all-done.1.a, f32[6,2,16,128]{3,2,1,0:T(8,128)S(1)} %get-tuple-element.40.fix, f32[2,128,128]{2,1,0:T(8,128)S(1)} %get-tuple-element.32.cols), custom_call_target="tpu_custom_call" | custom-call | flops 100000000 | bytes 7000000 | tf_op jit(solution)/shard_map/nearly/pallas_call | solution.py:591
  74.6 0.0 collective-permute-done.3.d2
  74.6 0.0 collective-permute-done.2.d1
  74.6 0.0 collective-permute-done.7.c3
  74.7 0.0 collective-permute-done.6.c2
  74.7 0.0 collective-permute-done.5.c1
  74.7 4.0 %final.1 = f32[16,768,128]{2,1,0:T(8,128)} custom-call(f32[16,128]{1,0:T(8,128)S(1)} %get-tuple-element.25.par, f32[16,768,128]{2,1,0:T(8,128)S(1)} %nearly.1.base, f32[32,768]{1,0:T(8,128)S(1)} %get-tuple-element.41.d0, f32[32,768]{1,0:T(8,128)S(1)} %collective-permute-done.2.d1, f32[32,768]{1,0:T(8,128)S(1)} %collective-permute-done.3.d2, ...), custom_call_target="tpu_custom_call" | custom-call | flops 1000000000 | bytes 13000000 | tf_op jit(solution)/shard_map/final/pallas_call | solution.py:601
Async XLA Ops:
  0.0 14.6 %copy-start.1 = (f32[4,128,128]{2,1,0:T(8,128)S(1)}, f32[4,128,128]{2,1,0:T(8,128)}, u32[]{:S(2)}) copy-start(f32[4,128,128]{2,1,0:T(8,128)} %di.1) | copy-start | bytes 786436
  0.0 14.6 %copy-start = (f32[6,128,128]{2,1,0:T(8,128)S(1)}, f32[6,128,128]{2,1,0:T(8,128)}, u32[]{:S(2)}) copy-start(f32[6,128,128]{2,1,0:T(8,128)} %wi.1) | copy-start | bytes 1179652
  0.0 0.7 copy-start.2
  0.7 13.9 %copy-start.3 = (f32[3]{0:T(128)S(1)}, f32[3]{0:T(128)}, u32[]{:S(2)}) copy-start(f32[3]{0:T(128)} %cpl.3) | copy-start | bytes 40
  6.4 9.0 %collective-permute-start.1 = (f32[40,768]{1,0:T(8,128)S(1)}, f32[40,768]{1,0:T(8,128)S(1)}, u32[]{:S(2)}, u32[]{:S(2)}) collective-permute-start(f32[40,768]{1,0:T(8,128)S(1)} %get-tuple-element.31.own), channel_id=1, source_target_pairs={{32,0},{64,32},{96,64},{33,1},{65,33},{97,65},{34,2},{66,34},{98,6... | collective-permute-start | bytes 368648 | tf_op jit(solution)/shard_map/ppermute | solution.py:502
  9.7 6.7 %collective-permute-start = (f32[40,768]{1,0:T(8,128)S(1)}, f32[40,768]{1,0:T(8,128)S(1)}, u32[]{:S(2)}, u32[]{:S(2)}) collective-permute-start(f32[40,768]{1,0:T(8,128)S(1)} %get-tuple-element.31.own), channel_id=1, source_target_pairs={{0,32},{32,64},{64,96},{1,33},{33,65},{65,97},{2,34},{34,66},{66,9... | collective-permute-start | bytes 368648 | tf_op jit(solution)/shard_map/ppermute | solution.py:501
  19.5 24.3 %all-to-all-start = ((f32[32,2,24,128]{3,2,1,0:T(8,128)}), f32[32,2,24,128]{3,2,1,0:T(8,128)S(1)}, u32[]{:S(2)}, u32[]{:S(2)}) async-start(f32[32,2,24,128]{3,2,1,0:T(8,128)} %edges.1), calls=%async_computation | async-start | bytes 1572864 | tf_op jit(solution)/shard_map/all_to_all | solution.py:537
  45.6 20.5 %all-to-all-start.1 = ((f32[32,2,24,128]{3,2,1,0:T(8,128)}), f32[32,2,24,128]{3,2,1,0:T(8,128)S(1)}, u32[]{:S(2)}, u32[]{:S(2)}) async-start(f32[32,2,24,128]{3,2,1,0:T(8,128)} %solver.1), calls=%async_computation.1 | async-start | bytes 1572864 | tf_op jit(solution)/shard_map/all_to_all | solution.py:561
  55.3 15.5 %collective-permute-start.4 = (f32[32,768]{1,0:T(8,128)S(1)}, f32[32,768]{1,0:T(8,128)S(1)}, u32[]{:S(2)}, u32[]{:S(2)}) collective-permute-start(f32[32,768]{1,0:T(8,128)S(1)} %get-tuple-element.41.d0), channel_id=1, source_target_pairs={{0,96},{32,0},{64,32},{96,64},{1,97},{33,1},{65,33},{97,65},{2,98}... | collective-permute-start | bytes 294920 | tf_op jit(solution)/shard_map/ppermute | solution.py:575
  55.4 19.3 %collective-permute-start.3 = (f32[32,768]{1,0:T(8,128)S(1)}, f32[32,768]{1,0:T(8,128)S(1)}, u32[]{:S(2)}, u32[]{:S(2)}) collective-permute-start(f32[32,768]{1,0:T(8,128)S(1)} %get-tuple-element.41.d0), channel_id=1, source_target_pairs={{0,64},{32,96},{64,0},{96,32},{1,65},{33,97},{65,1},{97,33},{2,66}... | collective-permute-start | bytes 294920 | tf_op jit(solution)/shard_map/ppermute | solution.py:575
  60.9 13.8 %collective-permute-start.2 = (f32[32,768]{1,0:T(8,128)S(1)}, f32[32,768]{1,0:T(8,128)S(1)}, u32[]{:S(2)}, u32[]{:S(2)}) collective-permute-start(f32[32,768]{1,0:T(8,128)S(1)} %get-tuple-element.41.d0), channel_id=1, source_target_pairs={{0,32},{32,64},{64,96},{96,0},{1,33},{33,65},{65,97},{97,1},{2,34}... | collective-permute-start | bytes 294920 | tf_op jit(solution)/shard_map/ppermute | solution.py:575
  66.4 8.3 %collective-permute-start.7 = (f32[8,768]{1,0:T(8,128)S(1)}, f32[8,768]{1,0:T(8,128)S(1)}, u32[]{:S(2)}, u32[]{:S(2)}) collective-permute-start(f32[8,768]{1,0:T(8,128)S(1)} %corner.1.c0), channel_id=1, source_target_pairs={{0,96},{32,0},{64,32},{96,64},{1,97},{33,1},{65,33},{97,65},{2,98}... | collective-permute-start | bytes 73736 | tf_op jit(solution)/shard_map/ppermute | solution.py:575
  66.4 8.2 %collective-permute-start.6 = (f32[8,768]{1,0:T(8,128)S(1)}, f32[8,768]{1,0:T(8,128)S(1)}, u32[]{:S(2)}, u32[]{:S(2)}) collective-permute-start(f32[8,768]{1,0:T(8,128)S(1)} %corner.1.c0), channel_id=1, source_target_pairs={{0,64},{32,96},{64,0},{96,32},{1,65},{33,97},{65,1},{97,33},{2,66}... | collective-permute-start | bytes 73736 | tf_op jit(solution)/shard_map/ppermute | solution.py:575
  70.7 3.9 %collective-permute-start.5 = (f32[8,768]{1,0:T(8,128)S(1)}, f32[8,768]{1,0:T(8,128)S(1)}, u32[]{:S(2)}, u32[]{:S(2)}) collective-permute-start(f32[8,768]{1,0:T(8,128)S(1)} %corner.1.c0), channel_id=1, source_target_pairs={{0,32},{32,64},{64,96},{96,0},{1,33},{33,65},{65,97},{97,1},{2,34}... | collective-permute-start | bytes 73736 | tf_op jit(solution)/shard_map/ppermute | solution.py:575

commit v3 on v2

--- a/solution.py
+++ b/solution.py
@@ -1,3 +1,5 @@
+from functools import partial
+
 import jax
 import jax.numpy as jnp
 from jax import lax
@@ -11,6 +13,7 @@
 NP = 32
 S = W // NP
 T = 16
+HALF = 3
 f32 = jnp.float32
 bf16 = jnp.bfloat16
 HIGHEST = lax.Precision.HIGHEST
@@ -59,10 +62,10 @@
     return lax.broadcasted_iota(jnp.int32, shape, dim)
 
 
-HEAD, BEFORE_H, BEFORE_W, AH, CH, MH, FROM = 0, 1, 5, 9, 10, 11, 12
-
-
-def tables_kernel(cpl, slab, wi, di, par, cols, rows, gw3, gd4, spread, hmat, hcol, gwf):
+HEAD, BEFORE_H, BEFORE_W, AH, CH, MH, PAIR = 0, 1, 5, 9, 10, 11, 12
+
+
+def tables_kernel(cpl, slab, wi, di, par, cols, rows, gw3, gd4, spread, hmat, hcol, gwf, colm):
     row = (1, 128)
     sw, sh, sd = (jnp.full(row, cpl[k], f32) for k in range(3))
     lw, lh, ld = log_decay(sw), log_decay(sh), log_decay(sd)
@@ -73,6 +76,25 @@
         heads += [influence(log_r, m, 0.0), influence(log_r, m, m - 1.0)]
     middle = pivots(lh, float(H // 2))
     heads.append(1.0 / (1.0 - middle * middle))
+    p, q = heads[7], heads[8]
+    i1 = 1.0 / (1.0 - p * p)
+    v = p + p * q * q * i1
+    i2 = 1.0 / (1.0 - v * v)
+    heads += [i2, i2 * v]
+    one, none = jnp.ones(row, f32), jnp.zeros(row, f32)
+    by_slab = (
+        ((none, q * i1, q * i1 * p, one, none), (none,) * 5, (none, p * i1, i1, none, q * i1)),
+        ((q * i1 * p, one, none, q * i1, none), (p * i1, none, none, i1, p * q * i1), (none,) * 4 + (one,)),
+        ((one, q * i1 * p, q * i1, none, none), (none,) * 4 + (one,), (none, p * i1, i1, none, p * q * i1)),
+        ((q * i1, none, one, q * i1 * p, none), (p * i1, none, none, i1, q * i1), (none,) * 5),
+    )
+    mine = jnp.full(row, slab[0], jnp.int32)
+    for line in range(3):
+        total = none
+        for at in range(4):
+            for n, value in enumerate(by_slab[at][line]):
+                total = jnp.where((mine == at) & (lane == n), value, total)
+        par[PAIR + line : PAIR + line + 1] = total
     head = jnp.zeros(row, f32)
     for at, v in enumerate(heads):
         head = jnp.where(lane == at, v, head)
@@ -88,27 +110,16 @@
     par[AH : AH + 1] = influence(lh, float(H), kc)
     par[CH : CH + 1] = ch
     par[MH : MH + 1] = ch / sh
-    me = slab[0]
-    other = lax.bitwise_and(me - lane, 3)
-    of, mf = other.astype(f32), jnp.full(row, me, jnp.int32).astype(f32)
-    n = float(4 * D)
-    for side, (where, beside, inside) in enumerate(
-        ((D * mf - 1.0, me - 1, me > 0), (D * mf + D, me + 1, me < 3))
-    ):
-        spot = jnp.clip(where, 0.0, n - 1.0)
-        first = jnp.where(other >= 1, sd * green(sd, ld, n, spot, jnp.maximum(D * of - 1.0, 0.0)), 0.0)
-        last = jnp.where(other <= 2, sd * green(sd, ld, n, spot, jnp.minimum(D * of + D, n - 1.0)), 0.0)
-        same = jnp.where(other == beside, 1.0, 0.0)
-        if side == 0:
-            last = last + same
-        else:
-            first = first + same
-        par[FROM + 2 * side : FROM + 2 * side + 1] = jnp.where(inside, first, 0.0)
-        par[FROM + 2 * side + 1 : FROM + 2 * side + 2] = jnp.where(inside, last, 0.0)
     tall = iota((B, D), 0).astype(f32)
     lww = jnp.broadcast_to(lw, (B, D))
     cols[0] = influence(lww, float(B), tall)
     cols[1] = influence(lww, float(B), B - 1.0 - tall)
+    ca, cb = cols[0], cols[1]
+    ca_hi, cb_hi = ca.astype(bf16).astype(f32), cb.astype(bf16).astype(f32)
+    wide = iota((B, D), 1)
+    mixed = jnp.where((wide == 0) | (wide == 8), ca_hi, jnp.where((wide == 1) | (wide == 9), cb_hi, 0.0))
+    mixed = jnp.where(wide == 16, ca - ca_hi, jnp.where(wide == 17, cb - cb_hi, mixed))
+    colm[...] = mixed[:, :32].astype(bf16)
     rows[0:1] = influence(lw, float(B), k)
     rows[1:2] = influence(lw, float(B), B - 1.0 - k)
     gwf[...] = wi[0]
@@ -142,7 +153,9 @@
     hcol[...] = influence(jnp.broadcast_to(lh, (H, 128)), float(H), jnp.where(ln == 0, c, H - 1.0 - c))
 
 
-def sums_kernel(cpl, rho, sig, cr, cs, halo, rv, sv, coef, packed, sems):
+def sums_kernel(cpl_far, rho, sig, cr, cs, halo, rv, sv, coef, packed, cpl, sems, sem):
+    small = pltpu.make_async_copy(cpl_far, cpl, sem)
+    small.start()
     def parts(i):
         at = pl.ds(pl.multiple_of(i * B, B), B)
         return (
@@ -153,6 +166,7 @@
     for i in range(NB):
         for part in parts(i):
             part.start()
+    small.wait()
     sh = jnp.full((8, 128), cpl[1], f32)
     lh = log_decay(sh)
     for h in range(H):
@@ -248,26 +262,41 @@
             spot = slice(k * B, (k + 1) * B)
             e[j, spot] = e[j, spot] + cols[0] * ls[k] + cols[1] * rs[k]
         for p in range(NP):
-            out[p, j] = e[j, S * p : S * (p + 1)]
-
-
-def field_kernel(par, rho, sig, gw3, gd4, raw, ew, qp, rv, out, packed, sems):
+            out[p, S * j : S * (j + 1)] = e[j, S * p : S * (p + 1)]
+
+
+def field_kernel(start, count, par, rho, sig, gw3, gd4, raw, ew, qp, rv, out, packed, sems, rims):
     sv = out
 
+    def place(i, lead=0):
+        return pl.ds(pl.multiple_of(i * B + lead, 8), B)
+
     def parts(i):
-        at = pl.ds(pl.multiple_of(i * B, B), B)
+        there = place(i, start * B)
         return (
-            pltpu.make_async_copy(rho.at[:, at, :], rv.at[:, at, :], sems.at[0, i]),
-            pltpu.make_async_copy(sig.at[:, at, :], out.at[:, at, :], sems.at[1, i]),
+            pltpu.make_async_copy(rho.at[:, there, :], rv.at[:, place(i, 8), :], sems.at[0, i]),
+            pltpu.make_async_copy(sig.at[:, there, :], out.at[:, place(i), :], sems.at[1, i]),
         )
 
     def send(i):
-        at = pl.ds(pl.multiple_of(i * B, B), B)
-        return pltpu.make_async_copy(out.at[:, at, :], raw.at[:, at, :], sems.at[2, i])
-
-    for i in range(NB):
+        return pltpu.make_async_copy(out.at[:, place(i), :], raw.at[:, place(i), :], sems.at[2, i])
+
+    ends = []
+    if start > 0:
+        ends.append((start * B - 8, 0))
+    if start + count < NB:
+        ends.append(((start + count) * B, 8 + count * B))
+    ends = [
+        pltpu.make_async_copy(rho.at[:, pl.ds(there, 8), :], rv.at[:, pl.ds(here, 8), :], rims.at[n])
+        for n, (there, here) in enumerate(ends)
+    ]
+    for end in ends:
+        end.start()
+    for i in range(count):
         for part in parts(i):
             part.start()
+    for end in ends:
+        end.wait()
     for part in parts(0):
         part.wait()
     c0, c1, c2 = par[HEAD, 0], par[HEAD, 1], par[HEAD, 2]
@@ -276,18 +305,19 @@
     meet = par[HEAD, 9]
 
     def block(i, _):
-        @pl.when(i < NB - 1)
+        @pl.when(i < count - 1)
         def _():
-            for part in parts(jnp.minimum(i + 1, NB - 1)):
+            for part in parts(jnp.minimum(i + 1, count - 1)):
                 part.wait()
 
-        here = pl.ds(pl.multiple_of(i * B, B), B)
-        before = pl.ds(pl.multiple_of(jnp.maximum(i * B - 8, 0), 8), 8)
-        after = pl.ds(pl.multiple_of(jnp.minimum(i * B + B, W - 8), 8), 8)
+        here = place(i)
+        inner = place(i, 8)
+        before = pl.ds(pl.multiple_of(i * B, 8), 8)
+        after = pl.ds(pl.multiple_of(i * B + B + 8, 8), 8)
         for h in range(H):
-            x = rv[h, here, :]
-            first = jnp.where(i > 0, rv[h, before, :][7:8], 0.0)
-            last = jnp.where(i < NB - 1, rv[h, after, :][0:1], 0.0)
+            x = rv[h, inner, :]
+            first = jnp.where(i + start > 0, rv[h, before, :][7:8], 0.0)
+            last = jnp.where(i + start < NB - 1, rv[h, after, :][0:1], 0.0)
             up = jnp.where(row == 0, first, pltpu.roll(x, 1, 0))
             down = jnp.where(row == B - 1, last, pltpu.roll(x, B - 1, 0))
             out[h, here, :] = (
@@ -296,6 +326,7 @@
 
         def tile(j, _):
             at = pl.ds(pl.multiple_of(i * B + T * j, T), T)
+            beside = pl.ds(pl.multiple_of(i * B + T * j + 8, 8), T)
             top, bottom = [None] * half, [None] * half
             for h in range(half):
                 m, c = par[MH, h], par[CH, h]
@@ -309,8 +340,8 @@
                 if h < half - 1:
                     c = par[CH, h]
                     x, y = top[h] + c * x, bottom[h] + c * y
-                out[h, at, :] = x - 2.0 * rv[h, at, :]
-                out[H - 1 - h, at, :] = y - 2.0 * rv[H - 1 - h, at, :]
+                out[h, at, :] = x - 2.0 * rv[h, beside, :]
+                out[H - 1 - h, at, :] = y - 2.0 * rv[H - 1 - h, beside, :]
             return 0
 
         lax.fori_loop(0, B // T, tile, 0)
@@ -323,7 +354,7 @@
                 part = y[side * B : (side + 1) * B]
                 ew[i, 0, h : h + 1, :] = part[0:1]
                 ew[i, 1, h : h + 1, :] = part[B - 1 : B]
-                out[h, here, :] = part + rv[h, here, :]
+                out[h, here, :] = part + rv[h, inner, :]
                 pack = jnp.where((lane == 2 * h) | (lane == 2 * h + 1), pltpu.roll(part, 2 * h + 1, 1), pack)
         packed[...] = pack.T[: 2 * H]
         qp[:H, here] = packed[pl.ds(1, H, stride=2), :]
@@ -331,16 +362,22 @@
         send(i).start()
         return 0
 
-    lax.fori_loop(0, NB, block, 0)
-    for i in range(NB):
+    lax.fori_loop(0, count, block, 0)
+    for i in range(count):
         send(i).wait()
 
 
-def planes_kernel(par, ew, qp, own, from_left, from_right, hmat, rows, gwf, planes, u, fix):
-    ls, rs = chain_w([ew[k, 0] for k in range(NB)], [ew[k, 1] for k in range(NB)], par)
+def planes_kernel(par, ew0, ew1, qp0, qp1, own, from_left, from_right, hmat, rows, gwf, planes, u, fix, flat):
+    ew = [ew0[k] for k in range(HALF)] + [ew1[k] for k in range(NB - HALF)]
+    ls, rs = chain_w([a[0] for a in ew], [a[1] for a in ew], par)
+    flat[...] = jnp.zeros((8, H * D), f32)
     for k in range(NB):
-        fix[k, 0] = ls[k]
-        fix[k, 1] = rs[k]
+        for h in range(H):
+            flat[0:1, h * D : (h + 1) * D] = ls[k][h : h + 1]
+            flat[1:2, h * D : (h + 1) * D] = rs[k][h : h + 1]
+        x = flat[...]
+        hi = x.astype(bf16).astype(f32)
+        fix[k] = jnp.concatenate([hi, x - hi, hi, jnp.zeros_like(x)], axis=0).astype(bf16)
     v = jnp.concatenate([from_left[H : 2 * H] - own[H : 2 * H], from_right[:H] - own[:H]], axis=0)
     v = jnp.dot(hmat[:, : 2 * H], v, precision=HIGHEST, preferred_element_type=f32)
     parts = []
@@ -349,7 +386,8 @@
         solved = lax.dot_general(
             v[:, spot], gwf[...], (((1,), (1,)), ((), ())), precision=HIGHEST, preferred_element_type=f32
         )
-        parts.append(jnp.concatenate([2.0 * solved, qp[:, spot]], axis=0))
+        seen = qp0[:, spot] if k < HALF else qp1[:, (k - HALF) * B : (k - HALF + 1) * B]
+        parts.append(jnp.concatenate([2.0 * solved, seen], axis=0))
     ls, rs = chain_w([a[:, 0:1] for a in parts], [a[:, B - 1 : B] for a in parts], par)
     p, q = par[HEAD, 7], par[HEAD, 8]
     for k in range(NB):
@@ -361,78 +399,91 @@
         planes[H:, spot] = both[3 * H :] + q * ul + p * ur
 
 
+def pair_kernel(par, a, b, out):
+    def joined(first, last):
+        return (
+            par[PAIR, 0] * a[first, :] + par[PAIR, 1] * a[last, :] + par[PAIR, 2] * b[first, :] + par[PAIR, 3] * b[last, :]
+        )
+
+    out[:H] = joined(pl.ds(0, H), pl.ds(H, H))
+    out[H:] = jnp.zeros((8, W), f32)
+    for plane in range(2):
+        at = 2 * H + 2 * plane
+        out[H + plane : H + plane + 1] = joined(pl.ds(at + 1, 1), pl.ds(at, 1))
+
+
 def solver_kernel(par, y, out, us):
     p, q = par[HEAD, 5], par[HEAD, 6]
     before, inv, w, qw = (BEFORE_H + k for k in range(4))
-    u = y[0, 1] + par[w, 0] * y[0, 0]
+    u = y[0, S:] + par[w, 0] * y[0, :S]
     us[0] = u
     for k in range(1, NP):
-        u = y[k, 1] + par[w, k] * y[k, 0] + par[qw, k] * u
+        u = y[k, S:] + par[w, k] * y[k, :S] + par[qw, k] * u
         us[k] = u
     zero = jnp.zeros_like(u)
-    out[NP - 1, 1] = zero
+    out[NP - 1, S:] = zero
     f = zero
     for k in reversed(range(NP)):
-        g = y[k, 0]
+        g = y[k, :S]
         if k > 0:
             g = g + p * us[k - 1]
         f = (g + q * f) * par[inv, k]
         if k > 0:
-            out[k, 0] = us[k - 1] + par[before, k] * f
-            out[k - 1, 1] = f
-    out[0, 0] = zero
-
-
-def corner_kernel(a, out, wide):
+            out[k, :S] = us[k - 1] + par[before, k] * f
+            out[k - 1, S:] = f
+    out[0, :S] = zero
+
+
+def corner_kernel(a, planes, out, wide):
+    out[: 2 * H] = planes[...]
     lane = iota((S, D), 1)
     for p in range(NP):
-        wide[S * p : S * (p + 1)] = jnp.where(lane < 2, pltpu.roll(a[p, 0], 1, 1), pltpu.roll(a[p, 1], 3, 1))
+        wide[S * p : S * (p + 1)] = jnp.where(lane < 2, pltpu.roll(a[p, :S], 1, 1), pltpu.roll(a[p, S:], 3, 1))
     for k in range(NB):
-        out[:, k * B : (k + 1) * B] = wide[k * B : (k + 1) * B].T[:8]
-
-
-def nearly_kernel(par, raw, a, fix, cols, out, lr, sems):
-    def part(i):
-        at = pl.ds(pl.multiple_of(i * B, B), B)
-        return pltpu.make_async_copy(raw.at[:, at, :], out.at[:, at, :], sems.at[i])
-
+        out[2 * H :, k * B : (k + 1) * B] = wide[k * B : (k + 1) * B].T[:8]
+
+
+def nearly_kernel(par, raw0, raw1, a, out, lr, sems):
     for i in range(NB):
-        part(i).start()
+        raw, k = (raw0, i) if i < HALF else (raw1, i - HALF)
+        spot = pl.ds(i * B, B)
+        pltpu.make_async_copy(raw.at[:, pl.ds(k * B, B), :], out.at[:, spot, :], sems.at[i]).start()
     for p in range(NP):
         for j in range(2):
-            lr[j, S * p : S * (p + 1)] = a[p, j]
-    R = 32
+            lr[j, S * p : S * (p + 1)] = a[p, S * j : S * (j + 1)]
 
     def block(i, _):
-        part(i).wait()
-        for t in range(B // R):
-            at = pl.ds(pl.multiple_of(i * B + t * R, R), R)
-            ca, cb = cols[0, t * R : (t + 1) * R], cols[1, t * R : (t + 1) * R]
-            l, r = lr[0, at, :], lr[1, at, :]
-            for h in range(H):
-                v = ca * fix[i, 0, h : h + 1, :] + cb * fix[i, 1, h : h + 1, :]
-                out[h, at, :] = out[h, at, :] + v + (par[AH, h] * l + par[AH, H - 1 - h] * r)
+        at = pl.ds(pl.multiple_of(i * B, B), B)
+        pltpu.make_async_copy(raw1.at[:, pl.ds(0, B), :], out.at[:, at, :], sems.at[i]).wait()
+        l, r = lr[0, at, :], lr[1, at, :]
+        for h in range(H):
+            out[h, at, :] = out[h, at, :] + (par[AH, h] * l + par[AH, H - 1 - h] * r)
         return 0
 
     lax.fori_loop(0, NB, block, 0)
 
 
-def final_kernel(par, base, d0, d1, d2, d3, c0, c1, c2, c3, u, hcol, spread, out, tall, buf, sems):
-    ds, cs = (d0, d1, d2, d3), (c0, c1, c2, c3)
+def final_kernel(par, base, fix, colm, a, b, v0, v1, u, hcol, spread, out, tall, buf, sems):
+    beyond = par[HEAD, 10] * v1[...] + par[HEAD, 11] * v0[...]
+
+    def known(first, last, far_row):
+        return (a[first, :], a[last, :], b[first, :], b[last, :], far_row)
+
     sides = []
     for side in range(2):
-        first, last = FROM + 2 * side, FROM + 2 * side + 1
-        own = u[H * side : H * (side + 1)]
-        for k in range(4):
-            own = own + par[first, k] * ds[k][:H] + par[last, k] * ds[k][H:]
-        gam = []
+
+        def mixed(parts):
+            total = 0.0
+            for k, part in enumerate(parts):
+                total = total + par[PAIR + 1 + side, k] * part
+            return total
+
+        own = u[H * side : H * (side + 1)] + mixed(known(pl.ds(0, H), pl.ds(H, H), beyond[:H]))
         for plane in range(2):
-            g = 0.0
-            for k in range(4):
-                t, f = cs[k][2 * plane : 2 * plane + 1], cs[k][2 * plane + 1 : 2 * plane + 2]
-                g = g + par[first, k] * f + par[last, k] * t
-            gam.append(g)
-        sides.append(own + hcol[:, 0:1] * gam[0] + hcol[:, 1:2] * gam[1])
+            at = 2 * H + 2 * plane
+            row = beyond[H + plane : H + plane + 1]
+            own = own + hcol[:, plane : plane + 1] * mixed(known(pl.ds(at + 1, 1), pl.ds(at, 1), row))
+        sides.append(own)
     both = jnp.concatenate(sides + [jnp.zeros((D - 2 * H, W), f32)], axis=0)
     for k in range(NB):
         tall[k * B : (k + 1) * B] = both[:, k * B : (k + 1) * B].T
@@ -444,7 +495,9 @@
     def block(i, _):
         at = pl.ds(pl.multiple_of(i * B, B), B)
         hi, lo = split(tall[at, : 2 * H])
-        wide = dot(jnp.concatenate([hi, lo, hi], axis=1), spread[...])
+        wide = dot(
+            jnp.concatenate([hi, lo, hi, colm[...]], axis=1), jnp.concatenate([spread[...], fix[i]], axis=0)
+        )
         for h in range(H):
             buf[h, at, :] = base[h, at, :] + wide[:, h * D : (h + 1) * D]
         send(i).start()
@@ -485,19 +538,25 @@
     slabs = lax.axis_size("slab")
     up = [(k, k + 1) for k in range(slabs - 1)]
     down = [(k + 1, k) for k in range(slabs - 1)]
-    grid = [pltpu.VMEM((H, W, D), f32)]
+    grid = [pltpu.VMEM((H, W + 8, D), f32)]
 
     cr, cs, halo = pl.pallas_call(
         sums_kernel,
-        in_specs=[SMEM, HBM, HBM],
+        in_specs=[HBM, HBM, HBM],
         out_specs=[VMEM] * 3,
         out_shape=[held(2, W, D), held(2, W, D), held(2 * H + 8, W)],
         scratch_shapes=grid * 2
-        + [pltpu.VMEM((H, 8, 128), f32), pltpu.VMEM((2 * H, B), f32), pltpu.SemaphoreType.DMA((2, NB))],
+        + [
+            pltpu.VMEM((H, 8, 128), f32),
+            pltpu.VMEM((2 * H, B), f32),
+            pltpu.SMEM((3,), f32),
+            pltpu.SemaphoreType.DMA((2, NB)),
+            pltpu.SemaphoreType.DMA(()),
+        ],
         compiler_params=limit(24),
         name="sums",
         cost_estimate=cost(10**7, 14 * 10**6),
-    )(coupling, far(density), far(source))
+    )(far(coupling), far(density), far(source))
     halo_left = lax.ppermute(halo, "slab", up)
     halo_right = lax.ppermute(halo, "slab", down)
 
@@ -512,8 +571,9 @@
         ((2 * H, 128), f32),
         ((H, 128), f32),
         ((B, B), f32),
+        ((B, 32), bf16),
     ]
-    par, cols, rows, gw3, gd4, spread, hmat, hcol, gwf = pl.pallas_call(
+    par, cols, rows, gw3, gd4, spread, hmat, hcol, gwf, colm = pl.pallas_call(
         tables_kernel,
         grid=(1,),
         in_specs=[SMEM, SMEM, first, first],
@@ -528,7 +588,7 @@
         edges_kernel,
         in_specs=[SMEM] + [VMEM] * 7,
         out_specs=VMEM,
-        out_shape=held(NP, 2, S, D),
+        out_shape=held(NP, 2 * S, D),
         scratch_shapes=[pltpu.VMEM((2, W, D), f32)],
         compiler_params=limit(8),
         name="edges",
@@ -536,23 +596,32 @@
     )(par, near(cr), near(cs), near(halo_left), near(halo_right), near(gw3), near(gd4), near(cols))
     arrived = lax.all_to_all(edges, "pencil", 0, 0, tiled=True)
 
-    raw, ew, qp = pl.pallas_call(
-        field_kernel,
-        in_specs=[SMEM, HBM, HBM, VMEM, VMEM],
-        out_specs=[HBM, VMEM, VMEM],
-        out_shape=[pltpu.HBM((H, W, D), f32), held(NB, 2, H, D), held(2 * H, W)],
-        scratch_shapes=grid * 2 + [pltpu.VMEM((2 * H, B), f32), pltpu.SemaphoreType.DMA((3, NB))],
-        compiler_params=limit(24),
-        name="field",
-        cost_estimate=cost(4 * 10**9, 19 * 10**6),
-    )(par, far(density), far(source), near(gw3), near(gd4))
-
-    arrived, ew = lax.optimization_barrier((arrived, ew))
+    def field(start, count):
+        rows = count * B
+        return pl.pallas_call(
+            partial(field_kernel, start, count),
+            in_specs=[SMEM, HBM, HBM, VMEM, VMEM],
+            out_specs=[HBM, VMEM, VMEM],
+            out_shape=[pltpu.HBM((H, rows, D), f32), held(count, 2, H, D), held(2 * H, rows)],
+            scratch_shapes=[
+                pltpu.VMEM((H, rows + 16, D), f32),
+                pltpu.VMEM((H, rows, D), f32),
+                pltpu.VMEM((2 * H, B), f32),
+                pltpu.SemaphoreType.DMA((3, count)),
+                pltpu.SemaphoreType.DMA((2,)),
+            ],
+            compiler_params=limit(24),
+            name="field" + str(start),
+            cost_estimate=cost(2 * 10**9, 10**7),
+        )(par, far(density), far(source), near(gw3), near(gd4))
+
+    raw0, ew0, qp0 = field(0, HALF)
+    arrived, ew0 = lax.optimization_barrier((arrived, ew0))
     solved = pl.pallas_call(
         solver_kernel,
         in_specs=[SMEM, VMEM],
         out_specs=VMEM,
-        out_shape=held(NP, 2, S, D),
+        out_shape=held(NP, 2 * S, D),
         scratch_shapes=[pltpu.VMEM((NP, S, D), f32)],
         compiler_params=limit(8),
         name="solver",
@@ -560,54 +629,76 @@
     )(par, near(arrived))
     outside = lax.all_to_all(solved, "pencil", 0, 0, tiled=True)
 
+    raw1, ew1, qp1 = field(HALF, NB - HALF)
     planes, u, fix = pl.pallas_call(
         planes_kernel,
-        in_specs=[SMEM] + [VMEM] * 8,
+        in_specs=[SMEM] + [VMEM] * 10,
         out_specs=[VMEM] * 3,
-        out_shape=[held(2 * H, W), held(2 * H, W), held(NB, 2, H, D)],
+        out_shape=[held(2 * H, W), held(2 * H, W), held(NB, 32, H * D, dtype=bf16)],
+        scratch_shapes=[pltpu.VMEM((8, H * D), f32)],
         compiler_params=limit(8),
         name="planes",
         cost_estimate=cost(10**8, 10**6),
-    )(par, near(ew), near(qp), near(halo), near(halo_left), near(halo_right), near(hmat), near(rows), near(gwf))
-
-    def turned(value):
-        return [value] + [
-            lax.ppermute(value, "slab", [(k, (k + d) % slabs) for k in range(slabs)]) for d in range(1, slabs)
-        ]
-
-    planes_all = turned(planes)
+    )(par, *[near(v) for v in (ew0, ew1, qp0, qp1)], near(halo), near(halo_left), near(halo_right), near(hmat), near(rows), near(gwf))
+
     outside = near(outside)
     corners = pl.pallas_call(
         corner_kernel,
-        in_specs=[VMEM],
+        in_specs=[VMEM] * 2,
         out_specs=VMEM,
-        out_shape=held(8, W),
+        out_shape=held(2 * H + 8, W),
         scratch_shapes=[pltpu.VMEM((W, D), f32)],
         compiler_params=limit(8),
         name="corner",
         cost_estimate=cost(10**6, 10**6),
-    )(outside)
-    corners_all = turned(corners)
+    )(outside, near(planes))
+
+    def across(value, d):
+        return lax.ppermute(value, "slab", [(k, k ^ d) for k in range(slabs)])
+
+    beside = across(corners, 1)
+    rim = pl.pallas_call(
+        pair_kernel,
+        in_specs=[SMEM] + [VMEM] * 2,
+        out_specs=VMEM,
+        out_shape=held(H + 8, W),
+        compiler_params=limit(8),
+        name="pair",
+        cost_estimate=cost(10**5, 10**5),
+    )(par, near(corners), near(beside))
+    far_rim = across(rim, 2)
     base = pl.pallas_call(
         nearly_kernel,
-        in_specs=[SMEM, HBM] + [VMEM] * 3,
+        in_specs=[SMEM, HBM, HBM, VMEM],
         out_specs=VMEM,
         out_shape=held(H, W, D),
         scratch_shapes=[pltpu.VMEM((2, W, D), f32), pltpu.SemaphoreType.DMA((NB,))],
         compiler_params=limit(8),
         name="nearly",
         cost_estimate=cost(10**8, 7 * 10**6),
-    )(par, far(raw), outside, near(fix), near(cols))
+    )(par, far(raw0), far(raw1), outside)
     return pl.pallas_call(
         final_kernel,
-        in_specs=[SMEM] + [VMEM] * 12,
+        in_specs=[SMEM] + [VMEM] * 10,
         out_specs=HBM,
         out_shape=pltpu.HBM((H, W, D), f32),
         scratch_shapes=[pltpu.VMEM((W, D), f32), *grid, pltpu.SemaphoreType.DMA((NB,))],
         compiler_params=limit(16),
         name="final",
         cost_estimate=cost(10**9, 13 * 10**6),
-    )(par, near(base), *[near(v) for v in planes_all], *[near(v) for v in corners_all], near(u), near(hcol), near(spread))
+    )(
+        par,
+        near(base),
+        near(fix),
+        near(colm),
+        near(corners),
+        near(beside),
+        near(rim),
+        near(far_rim),
+        near(u),
+        near(hcol),
+        near(spread),
+    )
 
 
 def solution(mesh):

time: 79.1 us -> 73.7 us (0.932)
  starting transfers between devices: 34.6 us -> 25.8 us
  Pallas kernels: 37.1 us -> 41 us
    ppermute x6 -> x2, starting transfers between devices: 10 us -> 3.73 us  [across(): return lax.ppermute(value, 'slab', [(k, k ^ d) for k in range(slabs)])]
    pallas_call x6 -> x8, Pallas kernels: 31.4 us -> 35.3 us  [the longest x2 19.3 us: field(): pl.pallas_call(partial(field_kernel, start, count), in_specs=[SMEM, HBM,...]
    all_to_all x1, waiting for transfers between devices: 5.11 us -> 1.56 us  [per_device(): outside = lax.all_to_all(solved, 'pencil', 0, 0, tiled=True)]
    all_to_all x1, waiting for transfers between devices: 0.01 us -> 2.45 us  [per_device(): arrived = lax.all_to_all(edges, 'pencil', 0, 0, tiled=True)]
    all_to_all x1, starting transfers between devices: 7.76 us -> 5.32 us  [per_device(): outside = lax.all_to_all(solved, 'pencil', 0, 0, tiled=True)]
    ppermute x6 -> x2, waiting for transfers between devices: 0.02 us -> 1.33 us  [across(): return lax.ppermute(value, 'slab', [(k, k ^ d) for k in range(slabs)])]
  transfers between devices with their start and end apart: 10 -> 6, of which waited for: 2 -> 4; matrix products, arithmetic and copies ran while one was open for 0% -> 0% of each run, Pallas kernels for 29% -> 35%
where the time goes in v3:
time: 73.7 us; the launch traced here: 73.3 us
  Pallas kernels  41 us (56%)
  starting transfers between devices  25.8 us (35%)
  waiting for transfers between devices  6.34 us (9%)
    pallas_call x2, Pallas kernels, field(): pl.pallas_call(partial(field_kernel, start, count), in_specs=[SMEM, HBM,...  19.3 us
    all_to_all x1, starting transfers between devices, per_device(): arrived = lax.all_to_all(edges, 'pencil', 0, 0, tiled=True)  8.66 us
    all_to_all x1, starting transfers between devices, per_device(): outside = lax.all_to_all(solved, 'pencil', 0, 0, tiled=True)  5.32 us
    pallas_call x1, Pallas kernels, per_device(): pl.pallas_call(sums_kernel, in_specs=[HBM, HBM, HBM], out_specs=[VMEM] *...  5.21 us
    ppermute x1, starting transfers between devices, per_device(): halo_left = lax.ppermute(halo, 'slab', up)  4.84 us
    pallas_call x1, Pallas kernels, per_device(): pl.pallas_call(final_kernel, in_specs=[SMEM] + [VMEM] * 10, out_specs=HBM...  4.08 us
    ppermute x2, starting transfers between devices, across(): return lax.ppermute(value, 'slab', [(k, k ^ d) for k in range(slabs)])  3.73 us
    pallas_call x1, Pallas kernels, per_device(): pl.pallas_call(nearly_kernel, in_specs=[SMEM, HBM, HBM, VMEM], out_specs=...  3.66 us
  transfers between devices with their start and end apart: 6, of which 4 were waited for; matrix products, arithmetic and copies ran while one was open for 0% of the time, Pallas kernels for 35%

profile of v3, /device:TPU:1, one launch (start us, length us, event | category | flops | bytes accessed | tf_op | source)
XLA Modules:
  0.0 73.3 jit_solution(4936234824177281224)
XLA Ops:
  0.0 0.0 copy-start.2
  0.0 0.0 copy-start.1
  0.0 0.0 copy-start
  0.0 5.2 %sums.1 = (f32[2,768,128]{2,1,0:T(8,128)S(1)}, f32[2,768,128]{2,1,0:T(8,128)S(1)}, f32[40,768]{1,0:T(8,128)S(1)}) custom-call(f32[3]{0:T(128)} %cpl_far.1, f32[16,768,128]{2,1,0:T(8,128)} %rho.5, f32[16,768,128]{2,1,0:T(8,128)} %sig.5), custom_call_target="tpu_custom_call" | custom-call | flops 10000000 | bytes 14000000 | tf_op jit(solution)/shard_map/sums/pallas_call | solution.py:543
  5.2 3.3 %collective-permute-start.1 = (f32[40,768]{1,0:T(8,128)S(1)}, f32[40,768]{1,0:T(8,128)S(1)}, u32[]{:S(2)}, u32[]{:S(2)}) collective-permute-start(f32[40,768]{1,0:T(8,128)S(1)} %get-tuple-element.36.own), channel_id=1, source_target_pairs={{32,0},{64,32},{96,64},{33,1},{65,33},{97,65},{34,2},{66,34},{98,6... | collective-permute-start | bytes 368648 | tf_op jit(solution)/shard_map/ppermute | solution.py:561
  8.5 4.8 %collective-permute-start = (f32[40,768]{1,0:T(8,128)S(1)}, f32[40,768]{1,0:T(8,128)S(1)}, u32[]{:S(2)}, u32[]{:S(2)}) collective-permute-start(f32[40,768]{1,0:T(8,128)S(1)} %get-tuple-element.36.own), channel_id=1, source_target_pairs={{0,32},{32,64},{64,96},{1,33},{33,65},{65,97},{2,34},{34,66},{66,9... | collective-permute-start | bytes 368648 | tf_op jit(solution)/shard_map/ppermute | solution.py:560
  13.4 0.0 copy-done.2
  13.4 0.0 copy-done.1
  13.4 0.0 copy-done
  13.4 0.8 %tables.1 = (f32[16,128]{1,0:T(8,128)S(1)}, f32[2,128,128]{2,1,0:T(8,128)S(1)}, f32[8,128]{1,0:T(8,128)S(1)}, bf16[128,384]{1,0:T(8,128)(2,1)S(1)}, bf16[256,256...) custom-call(f32[3]{0:T(128)S(1)} %copy-done.2, ...), custom_call_target="tpu_custom_call" | custom-call | flops 10000000 | bytes 1000000 | tf_op jit(solution)/shard_map/tables/pallas_call | solution.py:576
  14.2 0.0 collective-permute-done.1.from_right
  14.2 1.0 %collective-permute-done.from_left = f32[40,768]{1,0:T(8,128)S(1)} collective-permute-done((f32[40,768]{1,0:T(8,128)S(1)}, f32[40,768]{1,0:T(8,128)S(1)}, u32[]{:S(2)}, u32[]{:S(2)}) %collective-permute-start) | collective-permute-done | bytes 122912 | tf_op jit(solution)/shard_map/ppermute | solution.py:560
  15.2 3.1 %edges.1 = f32[32,48,128]{2,1,0:T(8,128)} custom-call(f32[16,128]{1,0:T(8,128)S(1)} %get-tuple-element.29.par, f32[2,768,128]{2,1,0:T(8,128)S(1)} %get-tuple-element.34.cr, f32[2,768,128]{2,1,0:T(8,128)S(1)} %get-tuple-element.35.cs, f32[40,768]{1,0:T(8,128)S(1)} %collective-permute-done.from_left, f32[40,768]{1,0:T(8,128)S(1)} %collective-permute-done.1.from_right, ...), custom_call_target="tpu_custom_call" | custom-call | flops 100000000 | bytes 3000000 | tf_op jit(solution)/shard_map/edges/pallas_call | solution.py:587
  18.3 8.7 %all-to-all-start = ((f32[32,48,128]{2,1,0:T(8,128)}), f32[32,48,128]{2,1,0:T(8,128)S(1)}, u32[]{:S(2)}, u32[]{:S(2)}) async-start(f32[32,48,128]{2,1,0:T(8,128)} %edges.1), calls=%async_computation | async-start | bytes 1572864 | tf_op jit(solution)/shard_map/all_to_all | solution.py:597
  27.0 9.6 %field0.1 = (f32[16,384,128]{2,1,0:T(8,128)}, f32[3,2,16,128]{3,2,1,0:T(8,128)S(1)}, f32[32,384]{1,0:T(8,128)S(1)}) custom-call(f32[16,128]{1,0:T(8,128)S(1)} %get-tuple-element.29.par, f32[16,768,128]{2,1,0:T(8,128)} %rho.5, f32[16,768,128]{2,1,0:T(8,128)} %sig.5, bf16[128,384]{1,0:T(8,128)(2,1)S(1)} %get-tuple-element.30.gw3, ...), custom_call_target="tpu_custom_call" | custom-call | flops 2000000000 | bytes 10000000 | tf_op jit(solution)/shard_map/field0/pallas_call | solution.py:601
  36.6 2.5 %all-to-all-done.y = f32[32,48,128]{2,1,0:T(8,128)S(1)} async-done(((f32[32,48,128]{2,1,0:T(8,128)}), f32[32,48,128]{2,1,0:T(8,128)S(1)}, u32[]{:S(2)}, u32[]{:S(2)}) %all-to-all-start) | async-done | bytes 786464 | tf_op jit(solution)/shard_map/all_to_all | solution.py:597
  39.1 1.8 %solver.1 = f32[32,48,128]{2,1,0:T(8,128)} custom-call(f32[16,128]{1,0:T(8,128)S(1)} %get-tuple-element.29.par, f32[32,48,128]{2,1,0:T(8,128)S(1)} %all-to-all-done.y), custom_call_target="tpu_custom_call" | custom-call | flops 1000000 | bytes 2000000 | tf_op jit(solution)/shard_map/solver/pallas_call | solution.py:620
  40.8 5.3 %all-to-all-start.1 = ((f32[32,48,128]{2,1,0:T(8,128)}), f32[32,48,128]{2,1,0:T(8,128)S(1)}, u32[]{:S(2)}, u32[]{:S(2)}) async-start(f32[32,48,128]{2,1,0:T(8,128)} %solver.1), calls=%async_computation.1 | async-start | bytes 1572864 | tf_op jit(solution)/shard_map/all_to_all | solution.py:630
  46.2 9.7 %field3.1 = (f32[16,384,128]{2,1,0:T(8,128)}, f32[3,2,16,128]{3,2,1,0:T(8,128)S(1)}, f32[32,384]{1,0:T(8,128)S(1)}) custom-call(f32[16,128]{1,0:T(8,128)S(1)} %get-tuple-element.29.par, f32[16,768,128]{2,1,0:T(8,128)} %rho.5, f32[16,768,128]{2,1,0:T(8,128)} %sig.5, bf16[128,384]{1,0:T(8,128)(2,1)S(1)} %get-tuple-element.30.gw3, ...), custom_call_target="tpu_custom_call" | custom-call | flops 2000000000 | bytes 10000000 | tf_op jit(solution)/shard_map/field3/pallas_call | solution.py:601
  55.8 2.1 %planes.1 = (f32[32,768]{1,0:T(8,128)S(1)}, f32[32,768]{1,0:T(8,128)S(1)}, bf16[6,32,2048]{2,1,0:T(8,128)(2,1)S(1)}) custom-call(f32[16,128]{1,0:T(8,128)S(1)} %get-tuple-element.29.par, f32[3,2,16,128]{3,2,1,0:T(8,128)S(1)} %get-tuple-element.40.ew0, f32[3,2,16,128]{3,2,1,0:T(8,128)S(1)} %get-tuple-element.41.ew1, f32[32,384]{1,0:T(8,128)S(1)} %get-tuple-element.42.qp0, ...), custom_call_target="tpu_custom_call" | custom-call | flops 100000000 | bytes 1000000 | tf_op jit(solution)/shard_map/planes/pallas_call | solution.py:633
  57.9 1.6 %all-to-all-done.1.a = f32[32,48,128]{2,1,0:T(8,128)S(1)} async-done(((f32[32,48,128]{2,1,0:T(8,128)}), f32[32,48,128]{2,1,0:T(8,128)S(1)}, u32[]{:S(2)}, u32[]{:S(2)}) %all-to-all-start.1) | async-done | bytes 786464 | tf_op jit(solution)/shard_map/all_to_all | solution.py:630
  59.5 0.3 corner.1.a
  59.8 0.1 collective-permute-start.2
  59.9 1.3 %collective-permute-done.2.b = f32[40,768]{1,0:T(8,128)S(1)} collective-permute-done((f32[40,768]{1,0:T(8,128)S(1)}, f32[40,768]{1,0:T(8,128)S(1)}, u32[]{:S(2)}, u32[]{:S(2)}) %collective-permute-start.2) | collective-permute-done | bytes 122912 | tf_op jit(solution)/shard_map/ppermute | solution.py:657
  61.2 0.7 pair.1.v0
  61.9 3.7 %collective-permute-start.3 = (f32[24,768]{1,0:T(8,128)S(1)}, f32[24,768]{1,0:T(8,128)S(1)}, u32[]{:S(2)}, u32[]{:S(2)}) collective-permute-start(f32[24,768]{1,0:T(8,128)S(1)} %pair.1.v0), channel_id=1, source_target_pairs={{0,64},{32,96},{64,0},{96,32},{1,65},{33,97},{65,1},{97,33},{2,66}... | collective-permute-start | bytes 221192 | tf_op jit(solution)/shard_map/ppermute | solution.py:657
  65.6 3.7 %nearly.1.base = f32[16,768,128]{2,1,0:T(8,128)S(1)} custom-call(f32[16,128]{1,0:T(8,128)S(1)} %get-tuple-element.29.par, f32[16,384,128]{2,1,0:T(8,128)} %get-tuple-element.32.raw0, f32[16,384,128]{2,1,0:T(8,128)} %get-tuple-element.33.raw1, f32[32,48,128]{2,1,0:T(8,128)S(1)} %all-to-all-done.1.a), custom_call_target="tpu_custom_call" | custom-call | flops 100000000 | bytes 7000000 | tf_op jit(solution)/shard_map/nearly/pallas_call | solution.py:670
  69.2 0.0 collective-permute-done.3.v1
  69.2 4.1 %final.1 = f32[16,768,128]{2,1,0:T(8,128)} custom-call(f32[16,128]{1,0:T(8,128)S(1)} %get-tuple-element.29.par, f32[16,768,128]{2,1,0:T(8,128)S(1)} %nearly.1.base, bf16[6,32,2048]{2,1,0:T(8,128)(2,1)S(1)} %get-tuple-element.47.fix, bf16[128,32]{1,0:T(8,128)(2,1)S(1)} %get-tuple-element.48.colm, f32[40,768]{1,0:T(8,128)S(1)} %corner.1.a, ...), custom_call_target="tpu_custom_call" | custom-call | flops 1000000000 | bytes 13000000 | tf_op jit(solution)/shard_map/final/pallas_call | solution.py:680
Async XLA Ops:
  0.0 13.4 %copy-start.2 = (f32[3]{0:T(128)S(1)}, f32[3]{0:T(128)}, u32[]{:S(2)}) copy-start(f32[3]{0:T(128)} %cpl_far.1) | copy-start | bytes 40
  0.0 13.4 %copy-start.1 = (f32[4,128,128]{2,1,0:T(8,128)S(1)}, f32[4,128,128]{2,1,0:T(8,128)}, u32[]{:S(2)}) copy-start(f32[4,128,128]{2,1,0:T(8,128)} %di.1) | copy-start | bytes 786436
  0.0 13.4 %copy-start = (f32[6,128,128]{2,1,0:T(8,128)S(1)}, f32[6,128,128]{2,1,0:T(8,128)}, u32[]{:S(2)}) copy-start(f32[6,128,128]{2,1,0:T(8,128)} %wi.1) | copy-start | bytes 1179652
  5.2 9.0 %collective-permute-start.1 = (f32[40,768]{1,0:T(8,128)S(1)}, f32[40,768]{1,0:T(8,128)S(1)}, u32[]{:S(2)}, u32[]{:S(2)}) collective-permute-start(f32[40,768]{1,0:T(8,128)S(1)} %get-tuple-element.36.own), channel_id=1, source_target_pairs={{32,0},{64,32},{96,64},{33,1},{65,33},{97,65},{34,2},{66,34},{98,6... | collective-permute-start | bytes 368648 | tf_op jit(solution)/shard_map/ppermute | solution.py:561
  8.5 6.7 %collective-permute-start = (f32[40,768]{1,0:T(8,128)S(1)}, f32[40,768]{1,0:T(8,128)S(1)}, u32[]{:S(2)}, u32[]{:S(2)}) collective-permute-start(f32[40,768]{1,0:T(8,128)S(1)} %get-tuple-element.36.own), channel_id=1, source_target_pairs={{0,32},{32,64},{64,96},{1,33},{33,65},{65,97},{2,34},{34,66},{66,9... | collective-permute-start | bytes 368648 | tf_op jit(solution)/shard_map/ppermute | solution.py:560
  18.3 20.8 %all-to-all-start = ((f32[32,48,128]{2,1,0:T(8,128)}), f32[32,48,128]{2,1,0:T(8,128)S(1)}, u32[]{:S(2)}, u32[]{:S(2)}) async-start(f32[32,48,128]{2,1,0:T(8,128)} %edges.1), calls=%async_computation | async-start | bytes 1572864 | tf_op jit(solution)/shard_map/all_to_all | solution.py:597
  40.8 18.6 %all-to-all-start.1 = ((f32[32,48,128]{2,1,0:T(8,128)}), f32[32,48,128]{2,1,0:T(8,128)S(1)}, u32[]{:S(2)}, u32[]{:S(2)}) async-start(f32[32,48,128]{2,1,0:T(8,128)} %solver.1), calls=%async_computation.1 | async-start | bytes 1572864 | tf_op jit(solution)/shard_map/all_to_all | solution.py:630
  59.8 1.4 %collective-permute-start.2 = (f32[40,768]{1,0:T(8,128)S(1)}, f32[40,768]{1,0:T(8,128)S(1)}, u32[]{:S(2)}, u32[]{:S(2)}) collective-permute-start(f32[40,768]{1,0:T(8,128)S(1)} %corner.1.a), channel_id=1, source_target_pairs={{0,32},{32,0},{64,96},{96,64},{1,33},{33,1},{65,97},{97,65},{2,34}... | collective-permute-start | bytes 368648 | tf_op jit(solution)/shard_map/ppermute | solution.py:657
  61.9 7.3 %collective-permute-start.3 = (f32[24,768]{1,0:T(8,128)S(1)}, f32[24,768]{1,0:T(8,128)S(1)}, u32[]{:S(2)}, u32[]{:S(2)}) collective-permute-start(f32[24,768]{1,0:T(8,128)S(1)} %pair.1.v0), channel_id=1, source_target_pairs={{0,64},{32,96},{64,0},{96,32},{1,65},{33,97},{65,1},{97,33},{2,66}... | collective-permute-start | bytes 221192 | tf_op jit(solution)/shard_map/ppermute | solution.py:657

commit v4 on v3

--- a/solution.py
+++ b/solution.py
@@ -12,7 +12,7 @@
 NB = W // B
 NP = 32
 S = W // NP
-T = 16
+T = 32
 HALF = 3
 f32 = jnp.float32
 bf16 = jnp.bfloat16
@@ -80,7 +80,7 @@
     i1 = 1.0 / (1.0 - p * p)
     v = p + p * q * q * i1
     i2 = 1.0 / (1.0 - v * v)
-    heads += [i2, i2 * v]
+    heads += [i2, i2 * v, jnp.full(row, lax.bitwise_and(slab[0], 1), jnp.int32).astype(f32)]
     one, none = jnp.ones(row, f32), jnp.zeros(row, f32)
     by_slab = (
         ((none, q * i1, q * i1 * p, one, none), (none,) * 5, (none, p * i1, i1, none, q * i1)),
@@ -153,9 +153,11 @@
     hcol[...] = influence(jnp.broadcast_to(lh, (H, 128)), float(H), jnp.where(ln == 0, c, H - 1.0 - c))
 
 
-def sums_kernel(cpl_far, rho, sig, cr, cs, halo, rv, sv, coef, packed, cpl, sems, sem):
-    small = pltpu.make_async_copy(cpl_far, cpl, sem)
+def sums_kernel(cpl_far, slab_far, rho, sig, cr, cs, inner, outer, rv, sv, coef, packed, cpl, slab, sems, sem):
+    small = pltpu.make_async_copy(cpl_far, cpl, sem.at[0])
     small.start()
+    where = pltpu.make_async_copy(slab_far, slab, sem.at[1])
+    where.start()
     def parts(i):
         at = pl.ds(pl.multiple_of(i * B, B), B)
         return (
@@ -167,6 +169,8 @@
         for part in parts(i):
             part.start()
     small.wait()
+    where.wait()
+    odd = lax.bitwise_and(slab[0], 1) == 1
     sh = jnp.full((8, 128), cpl[1], f32)
     lh = log_decay(sh)
     for h in range(H):
@@ -194,9 +198,12 @@
             combs.append(jnp.where(lane < 2, pltpu.roll(fr, 1, 1), pltpu.roll(tr, 3, 1)))
         at = pl.ds(pl.multiple_of(i * B, B), B)
         packed[...] = jnp.concatenate(packs, axis=0).T[: 2 * H]
-        halo[:H, at] = packed[pl.ds(1, H, stride=2), :]
-        halo[H : 2 * H, at] = packed[pl.ds(0, H, stride=2), :]
-        halo[2 * H :, at] = jnp.concatenate(combs, axis=0).T[:8]
+        first, last = packed[pl.ds(1, H, stride=2), :], packed[pl.ds(0, H, stride=2), :]
+        inner[:H, at] = jnp.where(odd, first, last)
+        outer[:H, at] = jnp.where(odd, last, first)
+        comb = jnp.concatenate(combs, axis=0).T[:8]
+        inner[H:, at] = comb
+        outer[H:, at] = comb
         return 0
 
     lax.fori_loop(0, NB, block, 0)
@@ -231,15 +238,17 @@
     return y[:, :D] + y[:, D:]
 
 
-def edges_kernel(par, cr, cs, from_left, from_right, gw3, gd4, cols, out, e):
+def edges_kernel(par, cr, cs, from_inner, from_outer, gw3, gd4, cols, out, e):
     c0, c1, c2 = par[HEAD, 0], par[HEAD, 1], par[HEAD, 2]
     row = iota((B, D), 0)
     lane = iota((B, D), 1)
     blank = jnp.zeros((B - 8, B), f32)
+    odd = par[HEAD, 12] > 0.5
     for k in range(NB):
         spot = slice(k * B, (k + 1) * B)
-        lc = jnp.concatenate([from_left[2 * H :, spot], blank], axis=0).T
-        rc = jnp.concatenate([from_right[2 * H :, spot], blank], axis=0).T
+        a, b = from_inner[H:, spot], from_outer[H:, spot]
+        lc = jnp.concatenate([jnp.where(odd, a, b), blank], axis=0).T
+        rc = jnp.concatenate([jnp.where(odd, b, a), blank], axis=0).T
         xs = []
         for j in range(2):
             x = cr[j, spot]
@@ -367,7 +376,7 @@
         send(i).wait()
 
 
-def planes_kernel(par, ew0, ew1, qp0, qp1, own, from_left, from_right, hmat, rows, gwf, planes, u, fix, flat):
+def planes_kernel(par, ew0, ew1, qp0, qp1, inner, outer, from_inner, from_outer, hmat, rows, gwf, planes, u, fix, flat):
     ew = [ew0[k] for k in range(HALF)] + [ew1[k] for k in range(NB - HALF)]
     ls, rs = chain_w([a[0] for a in ew], [a[1] for a in ew], par)
     flat[...] = jnp.zeros((8, H * D), f32)
@@ -378,7 +387,9 @@
         x = flat[...]
         hi = x.astype(bf16).astype(f32)
         fix[k] = jnp.concatenate([hi, x - hi, hi, jnp.zeros_like(x)], axis=0).astype(bf16)
-    v = jnp.concatenate([from_left[H : 2 * H] - own[H : 2 * H], from_right[:H] - own[:H]], axis=0)
+    odd = par[HEAD, 12] > 0.5
+    a, b = from_inner[:H] - outer[:H], from_outer[:H] - inner[:H]
+    v = jnp.concatenate([jnp.where(odd, a, b), jnp.where(odd, b, a)], axis=0)
     v = jnp.dot(hmat[:, : 2 * H], v, precision=HIGHEST, preferred_element_type=f32)
     parts = []
     for k in range(NB):
@@ -536,29 +547,32 @@
 def per_device(density, source, coupling, width_inverse, height_inverse, depth_inverse):
     slab = lax.axis_index("slab")
     slabs = lax.axis_size("slab")
-    up = [(k, k + 1) for k in range(slabs - 1)]
-    down = [(k + 1, k) for k in range(slabs - 1)]
+
+    def across(value, pairs):
+        return lax.ppermute(value, "slab", pairs)
+
     grid = [pltpu.VMEM((H, W + 8, D), f32)]
 
-    cr, cs, halo = pl.pallas_call(
+    cr, cs, inner, outer = pl.pallas_call(
         sums_kernel,
-        in_specs=[HBM, HBM, HBM],
-        out_specs=[VMEM] * 3,
-        out_shape=[held(2, W, D), held(2, W, D), held(2 * H + 8, W)],
+        in_specs=[HBM] * 4,
+        out_specs=[VMEM] * 4,
+        out_shape=[held(2, W, D), held(2, W, D), held(H + 8, W), held(H + 8, W)],
         scratch_shapes=grid * 2
         + [
             pltpu.VMEM((H, 8, 128), f32),
             pltpu.VMEM((2 * H, B), f32),
             pltpu.SMEM((3,), f32),
+            pltpu.SMEM((1,), jnp.int32),
             pltpu.SemaphoreType.DMA((2, NB)),
-            pltpu.SemaphoreType.DMA(()),
+            pltpu.SemaphoreType.DMA((2,)),
         ],
         compiler_params=limit(24),
         name="sums",
         cost_estimate=cost(10**7, 14 * 10**6),
-    )(far(coupling), far(density), far(source))
-    halo_left = lax.ppermute(halo, "slab", up)
-    halo_right = lax.ppermute(halo, "slab", down)
+    )(far(coupling), far(slab.reshape(1)), far(density), far(source))
+    from_inner = across(inner, [(k, k ^ 1) for k in range(slabs)])
+    from_outer = across(outer, [(1, 2), (2, 1)])
 
     first = pl.BlockSpec((1, B, B), lambda *_: (0, 0, 0))
     shapes = [
@@ -593,7 +607,7 @@
         compiler_params=limit(8),
         name="edges",
         cost_estimate=cost(10**8, 3 * 10**6),
-    )(par, near(cr), near(cs), near(halo_left), near(halo_right), near(gw3), near(gd4), near(cols))
+    )(par, near(cr), near(cs), near(from_inner), near(from_outer), near(gw3), near(gd4), near(cols))
     arrived = lax.all_to_all(edges, "pencil", 0, 0, tiled=True)
 
     def field(start, count):
@@ -632,14 +646,14 @@
     raw1, ew1, qp1 = field(HALF, NB - HALF)
     planes, u, fix = pl.pallas_call(
         planes_kernel,
-        in_specs=[SMEM] + [VMEM] * 10,
+        in_specs=[SMEM] + [VMEM] * 11,
         out_specs=[VMEM] * 3,
         out_shape=[held(2 * H, W), held(2 * H, W), held(NB, 32, H * D, dtype=bf16)],
         scratch_shapes=[pltpu.VMEM((8, H * D), f32)],
         compiler_params=limit(8),
         name="planes",
         cost_estimate=cost(10**8, 10**6),
-    )(par, *[near(v) for v in (ew0, ew1, qp0, qp1)], near(halo), near(halo_left), near(halo_right), near(hmat), near(rows), near(gwf))
+    )(par, *[near(v) for v in (ew0, ew1, qp0, qp1)], near(inner), near(outer), near(from_inner), near(from_outer), near(hmat), near(rows), near(gwf))
 
     outside = near(outside)
     corners = pl.pallas_call(
@@ -652,11 +666,7 @@
         name="corner",
         cost_estimate=cost(10**6, 10**6),
     )(outside, near(planes))
-
-    def across(value, d):
-        return lax.ppermute(value, "slab", [(k, k ^ d) for k in range(slabs)])
-
-    beside = across(corners, 1)
+    beside = across(corners, [(k, k ^ 1) for k in range(slabs)])
     rim = pl.pallas_call(
         pair_kernel,
         in_specs=[SMEM] + [VMEM] * 2,
@@ -666,7 +676,7 @@
         name="pair",
         cost_estimate=cost(10**5, 10**5),
     )(par, near(corners), near(beside))
-    far_rim = across(rim, 2)
+    far_rim = across(rim, [(k, k ^ 2) for k in range(slabs)])
     base = pl.pallas_call(
         nearly_kernel,
         in_specs=[SMEM, HBM, HBM, VMEM],

time: 73.7 us -> 70.1 us (0.951)
  waiting for transfers between devices: 6.34 us -> 3.78 us
    ppermute x4, starting transfers between devices: 11.9 us -> 9.59 us  [across(): return lax.ppermute(value, 'slab', pairs)]
    all_to_all x1, waiting for transfers between devices: 1.56 us -> 0.01 us  [per_device(): outside = lax.all_to_all(solved, 'pencil', 0, 0, tiled=True)]
    all_to_all x1, starting transfers between devices: 5.32 us -> 6.79 us  [per_device(): outside = lax.all_to_all(solved, 'pencil', 0, 0, tiled=True)]
    all_to_all x1, waiting for transfers between devices: 2.45 us -> 0.98 us  [per_device(): arrived = lax.all_to_all(edges, 'pencil', 0, 0, tiled=True)]
  transfers between devices with their start and end apart: 6 -> 6, of which waited for: 4 -> 3; matrix products, arithmetic and copies ran while one was open for 0% -> 0% of each run, Pallas kernels for 35% -> 36%
where the time goes in v4:
time: 70.1 us; the launch traced here: 69.8 us
  Pallas kernels  40.5 us (58%)
  starting transfers between devices  25.4 us (36%)
  waiting for transfers between devices  3.78 us (5%)
    pallas_call x2, Pallas kernels, field(): pl.pallas_call(partial(field_kernel, start, count), in_specs=[SMEM, HBM,...  18.8 us
    ppermute x4, starting transfers between devices, across(): return lax.ppermute(value, 'slab', pairs)  9.59 us
    all_to_all x1, starting transfers between devices, per_device(): arrived = lax.all_to_all(edges, 'pencil', 0, 0, tiled=True)  9.01 us
    all_to_all x1, starting transfers between devices, per_device(): outside = lax.all_to_all(solved, 'pencil', 0, 0, tiled=True)  6.79 us
    pallas_call x1, Pallas kernels, per_device(): pl.pallas_call(sums_kernel, in_specs=[HBM] * 4, out_specs=[VMEM] * 4, out...  5.22 us
    pallas_call x1, Pallas kernels, per_device(): pl.pallas_call(final_kernel, in_specs=[SMEM] + [VMEM] * 10, out_specs=HBM...  4.06 us
    pallas_call x1, Pallas kernels, per_device(): pl.pallas_call(nearly_kernel, in_specs=[SMEM, HBM, HBM, VMEM], out_specs=...  3.66 us
    pallas_call x1, Pallas kernels, per_device(): pl.pallas_call(edges_kernel, in_specs=[SMEM] + [VMEM] * 7, out_specs=VMEM...  3.09 us
  transfers between devices with their start and end apart: 6, of which 3 were waited for; matrix products, arithmetic and copies ran while one was open for 0% of the time, Pallas kernels for 36%

profile of v4, /device:TPU:1, one launch (start us, length us, event | category | flops | bytes accessed | tf_op | source)
XLA Modules:
  0.0 69.8 jit_solution(1817390437675194030)
XLA Ops:
  0.0 0.0 copy-start
  0.0 0.0 copy-start.1
  0.0 0.0 copy-start.2
  0.0 5.2 %sums.1 = (f32[2,768,128]{2,1,0:T(8,128)S(1)}, f32[2,768,128]{2,1,0:T(8,128)S(1)}, f32[24,768]{1,0:T(8,128)S(1)}, f32[24,768]{1,0:T(8,128)S(1)}) custom-call(f32[3]{0:T(128)} %cpl_far.1, s32[1]{0:T(128)} %bitcast.slab.slab_far, f32[16,768,128]{2,1,0:T(8,128)} %rho.5, f32[16,768,128]{2,1,0:T(8,128)} %sig.5), custom_call_target="tpu_custom_call" | custom-call | flops 10000000 | bytes 14000000 | tf_op jit(solution)/shard_map/sums/pallas_call | solution.py:556
  5.2 1.5 %collective-permute-start = (f32[24,768]{1,0:T(8,128)S(1)}, f32[24,768]{1,0:T(8,128)S(1)}, u32[]{:S(2)}, u32[]{:S(2)}) collective-permute-start(f32[24,768]{1,0:T(8,128)S(1)} %get-tuple-element.37.inner), channel_id=1, source_target_pairs={{0,32},{32,0},{64,96},{96,64},{1,33},{33,1},{65,97},{97,65},{2,34}... | collective-permute-start | bytes 221192 | tf_op jit(solution)/shard_map/ppermute | solution.py:552
  6.7 4.8 %collective-permute-start.1 = (f32[24,768]{1,0:T(8,128)S(1)}, f32[24,768]{1,0:T(8,128)S(1)}, u32[]{:S(2)}, u32[]{:S(2)}) collective-permute-start(f32[24,768]{1,0:T(8,128)S(1)} %get-tuple-element.38.outer), channel_id=1, source_target_pairs={{32,64},{64,32},{33,65},{65,33},{34,66},{66,34},{35,67},{67,35},{3... | collective-permute-start | bytes 221192 | tf_op jit(solution)/shard_map/ppermute | solution.py:552
  11.5 0.0 copy-done
  11.5 0.0 copy-done.1
  11.6 0.0 copy-done.2
  11.6 0.8 %tables.1 = (f32[16,128]{1,0:T(8,128)S(1)}, f32[2,128,128]{2,1,0:T(8,128)S(1)}, f32[8,128]{1,0:T(8,128)S(1)}, bf16[128,384]{1,0:T(8,128)(2,1)S(1)}, bf16[256,256...) custom-call(f32[3]{0:T(128)S(1)} %copy-done.2, ...), custom_call_target="tpu_custom_call" | custom-call | flops 10000000 | bytes 1000000 | tf_op jit(solution)/shard_map/tables/pallas_call | solution.py:590
  12.4 0.0 collective-permute-done.from_inner
  12.4 1.5 %collective-permute-done.1.from_outer = f32[24,768]{1,0:T(8,128)S(1)} collective-permute-done((f32[24,768]{1,0:T(8,128)S(1)}, f32[24,768]{1,0:T(8,128)S(1)}, u32[]{:S(2)}, u32[]{:S(2)}) %collective-permute-start.1) | collective-permute-done | bytes 73760 | tf_op jit(solution)/shard_map/ppermute | solution.py:552
  13.9 3.1 %edges.1 = f32[32,48,128]{2,1,0:T(8,128)} custom-call(f32[16,128]{1,0:T(8,128)S(1)} %get-tuple-element.30.par, f32[2,768,128]{2,1,0:T(8,128)S(1)} %get-tuple-element.35.cr, f32[2,768,128]{2,1,0:T(8,128)S(1)} %get-tuple-element.36.cs, f32[24,768]{1,0:T(8,128)S(1)} %collective-permute-done.from_inner, f32[24,768]{1,0:T(8,128)S(1)} %collective-permute-done.1.from_outer, ...), custom_call_target="tpu_custom_call" | custom-call | flops 100000000 | bytes 3000000 | tf_op jit(solution)/shard_map/edges/pallas_call | solution.py:601
  16.9 9.0 %all-to-all-start = ((f32[32,48,128]{2,1,0:T(8,128)}), f32[32,48,128]{2,1,0:T(8,128)S(1)}, u32[]{:S(2)}, u32[]{:S(2)}) async-start(f32[32,48,128]{2,1,0:T(8,128)} %edges.1), calls=%async_computation | async-start | bytes 1572864 | tf_op jit(solution)/shard_map/all_to_all | solution.py:611
  26.0 9.4 %field0.1 = (f32[16,384,128]{2,1,0:T(8,128)}, f32[3,2,16,128]{3,2,1,0:T(8,128)S(1)}, f32[32,384]{1,0:T(8,128)S(1)}) custom-call(f32[16,128]{1,0:T(8,128)S(1)} %get-tuple-element.30.par, f32[16,768,128]{2,1,0:T(8,128)} %rho.5, f32[16,768,128]{2,1,0:T(8,128)} %sig.5, bf16[128,384]{1,0:T(8,128)(2,1)S(1)} %get-tuple-element.31.gw3, ...), custom_call_target="tpu_custom_call" | custom-call | flops 2000000000 | bytes 10000000 | tf_op jit(solution)/shard_map/field0/pallas_call | solution.py:615
  35.3 1.0 %all-to-all-done.y = f32[32,48,128]{2,1,0:T(8,128)S(1)} async-done(((f32[32,48,128]{2,1,0:T(8,128)}), f32[32,48,128]{2,1,0:T(8,128)S(1)}, u32[]{:S(2)}, u32[]{:S(2)}) %all-to-all-start) | async-done | bytes 786464 | tf_op jit(solution)/shard_map/all_to_all | solution.py:611
  36.3 1.8 %solver.1 = f32[32,48,128]{2,1,0:T(8,128)} custom-call(f32[16,128]{1,0:T(8,128)S(1)} %get-tuple-element.30.par, f32[32,48,128]{2,1,0:T(8,128)S(1)} %all-to-all-done.y), custom_call_target="tpu_custom_call" | custom-call | flops 1000000 | bytes 2000000 | tf_op jit(solution)/shard_map/solver/pallas_call | solution.py:634
  38.1 6.8 %all-to-all-start.1 = ((f32[32,48,128]{2,1,0:T(8,128)}), f32[32,48,128]{2,1,0:T(8,128)S(1)}, u32[]{:S(2)}, u32[]{:S(2)}) async-start(f32[32,48,128]{2,1,0:T(8,128)} %solver.1), calls=%async_computation.1 | async-start | bytes 1572864 | tf_op jit(solution)/shard_map/all_to_all | solution.py:644
  44.9 9.4 %field3.1 = (f32[16,384,128]{2,1,0:T(8,128)}, f32[3,2,16,128]{3,2,1,0:T(8,128)S(1)}, f32[32,384]{1,0:T(8,128)S(1)}) custom-call(f32[16,128]{1,0:T(8,128)S(1)} %get-tuple-element.30.par, f32[16,768,128]{2,1,0:T(8,128)} %rho.5, f32[16,768,128]{2,1,0:T(8,128)} %sig.5, bf16[128,384]{1,0:T(8,128)(2,1)S(1)} %get-tuple-element.31.gw3, ...), custom_call_target="tpu_custom_call" | custom-call | flops 2000000000 | bytes 10000000 | tf_op jit(solution)/shard_map/field3/pallas_call | solution.py:615
  54.3 2.1 %planes.1 = (f32[32,768]{1,0:T(8,128)S(1)}, f32[32,768]{1,0:T(8,128)S(1)}, bf16[6,32,2048]{2,1,0:T(8,128)(2,1)S(1)}) custom-call(f32[16,128]{1,0:T(8,128)S(1)} %get-tuple-element.30.par, f32[3,2,16,128]{3,2,1,0:T(8,128)S(1)} %get-tuple-element.42.ew0, f32[3,2,16,128]{3,2,1,0:T(8,128)S(1)} %get-tuple-element.43.ew1, f32[32,384]{1,0:T(8,128)S(1)} %get-tuple-element.44.qp0, ...), custom_call_target="tpu_custom_call" | custom-call | flops 100000000 | bytes 1000000 | tf_op jit(solution)/shard_map/planes/pallas_call | solution.py:647
  56.4 0.0 all-to-all-done.1.a
  56.4 0.3 corner.1.a
  56.7 0.1 collective-permute-start.2
  56.8 1.3 %collective-permute-done.2.b = f32[40,768]{1,0:T(8,128)S(1)} collective-permute-done((f32[40,768]{1,0:T(8,128)S(1)}, f32[40,768]{1,0:T(8,128)S(1)}, u32[]{:S(2)}, u32[]{:S(2)}) %collective-permute-start.2) | collective-permute-done | bytes 122912 | tf_op jit(solution)/shard_map/ppermute | solution.py:552
  58.1 0.7 pair.1.v0
  58.8 3.2 %collective-permute-start.3 = (f32[24,768]{1,0:T(8,128)S(1)}, f32[24,768]{1,0:T(8,128)S(1)}, u32[]{:S(2)}, u32[]{:S(2)}) collective-permute-start(f32[24,768]{1,0:T(8,128)S(1)} %pair.1.v0), channel_id=1, source_target_pairs={{0,64},{32,96},{64,0},{96,32},{1,65},{33,97},{65,1},{97,33},{2,66}... | collective-permute-start | bytes 221192 | tf_op jit(solution)/shard_map/ppermute | solution.py:552
  62.0 3.7 %nearly.1.base = f32[16,768,128]{2,1,0:T(8,128)S(1)} custom-call(f32[16,128]{1,0:T(8,128)S(1)} %get-tuple-element.30.par, f32[16,384,128]{2,1,0:T(8,128)} %get-tuple-element.33.raw0, f32[16,384,128]{2,1,0:T(8,128)} %get-tuple-element.34.raw1, f32[32,48,128]{2,1,0:T(8,128)S(1)} %all-to-all-done.1.a), custom_call_target="tpu_custom_call" | custom-call | flops 100000000 | bytes 7000000 | tf_op jit(solution)/shard_map/nearly/pallas_call | solution.py:680
  65.7 0.0 collective-permute-done.3.v1
  65.7 4.1 %final.1 = f32[16,768,128]{2,1,0:T(8,128)} custom-call(f32[16,128]{1,0:T(8,128)S(1)} %get-tuple-element.30.par, f32[16,768,128]{2,1,0:T(8,128)S(1)} %nearly.1.base, bf16[6,32,2048]{2,1,0:T(8,128)(2,1)S(1)} %get-tuple-element.49.fix, bf16[128,32]{1,0:T(8,128)(2,1)S(1)} %get-tuple-element.50.colm, f32[40,768]{1,0:T(8,128)S(1)} %corner.1.a, ...), custom_call_target="tpu_custom_call" | custom-call | flops 1000000000 | bytes 13000000 | tf_op jit(solution)/shard_map/final/pallas_call | solution.py:690
Async XLA Ops:
  0.0 11.5 %copy-start = (f32[6,128,128]{2,1,0:T(8,128)S(1)}, f32[6,128,128]{2,1,0:T(8,128)}, u32[]{:S(2)}) copy-start(f32[6,128,128]{2,1,0:T(8,128)} %wi.1) | copy-start | bytes 1179652
  0.0 11.5 %copy-start.1 = (f32[4,128,128]{2,1,0:T(8,128)S(1)}, f32[4,128,128]{2,1,0:T(8,128)}, u32[]{:S(2)}) copy-start(f32[4,128,128]{2,1,0:T(8,128)} %di.1) | copy-start | bytes 786436
  0.0 11.6 %copy-start.2 = (f32[3]{0:T(128)S(1)}, f32[3]{0:T(128)}, u32[]{:S(2)}) copy-start(f32[3]{0:T(128)} %cpl_far.1) | copy-start | bytes 40
  5.2 7.1 %collective-permute-start = (f32[24,768]{1,0:T(8,128)S(1)}, f32[24,768]{1,0:T(8,128)S(1)}, u32[]{:S(2)}, u32[]{:S(2)}) collective-permute-start(f32[24,768]{1,0:T(8,128)S(1)} %get-tuple-element.37.inner), channel_id=1, source_target_pairs={{0,32},{32,0},{64,96},{96,64},{1,33},{33,1},{65,97},{97,65},{2,34}... | collective-permute-start | bytes 221192 | tf_op jit(solution)/shard_map/ppermute | solution.py:552
  6.7 7.2 %collective-permute-start.1 = (f32[24,768]{1,0:T(8,128)S(1)}, f32[24,768]{1,0:T(8,128)S(1)}, u32[]{:S(2)}, u32[]{:S(2)}) collective-permute-start(f32[24,768]{1,0:T(8,128)S(1)} %get-tuple-element.38.outer), channel_id=1, source_target_pairs={{32,64},{64,32},{33,65},{65,33},{34,66},{66,34},{35,67},{67,35},{3... | collective-permute-start | bytes 221192 | tf_op jit(solution)/shard_map/ppermute | solution.py:552
  16.9 19.4 %all-to-all-start = ((f32[32,48,128]{2,1,0:T(8,128)}), f32[32,48,128]{2,1,0:T(8,128)S(1)}, u32[]{:S(2)}, u32[]{:S(2)}) async-start(f32[32,48,128]{2,1,0:T(8,128)} %edges.1), calls=%async_computation | async-start | bytes 1572864 | tf_op jit(solution)/shard_map/all_to_all | solution.py:611
  38.1 18.3 %all-to-all-start.1 = ((f32[32,48,128]{2,1,0:T(8,128)}), f32[32,48,128]{2,1,0:T(8,128)S(1)}, u32[]{:S(2)}, u32[]{:S(2)}) async-start(f32[32,48,128]{2,1,0:T(8,128)} %solver.1), calls=%async_computation.1 | async-start | bytes 1572864 | tf_op jit(solution)/shard_map/all_to_all | solution.py:644
  56.7 1.4 %collective-permute-start.2 = (f32[40,768]{1,0:T(8,128)S(1)}, f32[40,768]{1,0:T(8,128)S(1)}, u32[]{:S(2)}, u32[]{:S(2)}) collective-permute-start(f32[40,768]{1,0:T(8,128)S(1)} %corner.1.a), channel_id=1, source_target_pairs={{0,32},{32,0},{64,96},{96,64},{1,33},{33,1},{65,97},{97,65},{2,34}... | collective-permute-start | bytes 368648 | tf_op jit(solution)/shard_map/ppermute | solution.py:552
  58.8 6.9 %collective-permute-start.3 = (f32[24,768]{1,0:T(8,128)S(1)}, f32[24,768]{1,0:T(8,128)S(1)}, u32[]{:S(2)}, u32[]{:S(2)}) collective-permute-start(f32[24,768]{1,0:T(8,128)S(1)} %pair.1.v0), channel_id=1, source_target_pairs={{0,64},{32,96},{64,0},{96,32},{1,65},{33,97},{65,1},{97,33},{2,66}... | collective-permute-start | bytes 221192 | tf_op jit(solution)/shard_map/ppermute | solution.py:552

commit v5 on v3

--- a/solution.py
+++ b/solution.py
@@ -12,8 +12,9 @@
 NB = W // B
 NP = 32
 S = W // NP
-T = 16
+T = 32
 HALF = 3
+R = H + 8
 f32 = jnp.float32
 bf16 = jnp.bfloat16
 HIGHEST = lax.Precision.HIGHEST
@@ -80,13 +81,13 @@
     i1 = 1.0 / (1.0 - p * p)
     v = p + p * q * q * i1
     i2 = 1.0 / (1.0 - v * v)
-    heads += [i2, i2 * v]
-    one, none = jnp.ones(row, f32), jnp.zeros(row, f32)
+    heads += [i2, i2 * v, jnp.full(row, lax.bitwise_and(slab[0], 1), jnp.int32).astype(f32)]
+    one, none, two = jnp.ones(row, f32), jnp.zeros(row, f32), jnp.full(row, 2.0, f32)
     by_slab = (
-        ((none, q * i1, q * i1 * p, one, none), (none,) * 5, (none, p * i1, i1, none, q * i1)),
-        ((q * i1 * p, one, none, q * i1, none), (p * i1, none, none, i1, p * q * i1), (none,) * 4 + (one,)),
-        ((one, q * i1 * p, q * i1, none, none), (none,) * 4 + (one,), (none, p * i1, i1, none, p * q * i1)),
-        ((q * i1, none, one, q * i1 * p, none), (p * i1, none, none, i1, q * i1), (none,) * 5),
+        ((none, q * i1, q * i1 * p, one, none, none, none, none, two), (none,) * 5, (none, p * i1, i1, none, q * i1)),
+        ((q * i1 * p, one, none, q * i1, none, none, two, none, none), (p * i1, none, none, i1, p * q * i1), (none,) * 4 + (one,)),
+        ((one, q * i1 * p, q * i1, none, none, two, none, none, none), (none,) * 4 + (one,), (none, p * i1, i1, none, p * q * i1)),
+        ((q * i1, none, one, q * i1 * p, none, none, none, two, none), (p * i1, none, none, i1, q * i1), (none,) * 5),
     )
     mine = jnp.full(row, slab[0], jnp.int32)
     for line in range(3):
@@ -153,7 +154,7 @@
     hcol[...] = influence(jnp.broadcast_to(lh, (H, 128)), float(H), jnp.where(ln == 0, c, H - 1.0 - c))
 
 
-def sums_kernel(cpl_far, rho, sig, cr, cs, halo, rv, sv, coef, packed, cpl, sems, sem):
+def sums_kernel(cpl_far, rho, sig, cr, cs, own, comb, rv, sv, coef, packed, cpl, sems, sem):
     small = pltpu.make_async_copy(cpl_far, cpl, sem)
     small.start()
     def parts(i):
@@ -194,9 +195,9 @@
             combs.append(jnp.where(lane < 2, pltpu.roll(fr, 1, 1), pltpu.roll(tr, 3, 1)))
         at = pl.ds(pl.multiple_of(i * B, B), B)
         packed[...] = jnp.concatenate(packs, axis=0).T[: 2 * H]
-        halo[:H, at] = packed[pl.ds(1, H, stride=2), :]
-        halo[H : 2 * H, at] = packed[pl.ds(0, H, stride=2), :]
-        halo[2 * H :, at] = jnp.concatenate(combs, axis=0).T[:8]
+        own[:H, at] = packed[pl.ds(1, H, stride=2), :]
+        own[H:, at] = packed[pl.ds(0, H, stride=2), :]
+        comb[:, at] = jnp.concatenate(combs, axis=0).T[:8]
         return 0
 
     lax.fori_loop(0, NB, block, 0)
@@ -231,15 +232,12 @@
     return y[:, :D] + y[:, D:]
 
 
-def edges_kernel(par, cr, cs, from_left, from_right, gw3, gd4, cols, out, e):
+def edges_kernel(par, cr, cs, comb, gwf, rows, gw3, gd4, cols, out, e, wc):
     c0, c1, c2 = par[HEAD, 0], par[HEAD, 1], par[HEAD, 2]
     row = iota((B, D), 0)
-    lane = iota((B, D), 1)
-    blank = jnp.zeros((B - 8, B), f32)
+    parts = []
     for k in range(NB):
         spot = slice(k * B, (k + 1) * B)
-        lc = jnp.concatenate([from_left[2 * H :, spot], blank], axis=0).T
-        rc = jnp.concatenate([from_right[2 * H :, spot], blank], axis=0).T
         xs = []
         for j in range(2):
             x = cr[j, spot]
@@ -247,13 +245,21 @@
             up = jnp.where(row == 0, cr[j, k * B - 1 : k * B] if k > 0 else 0.0, up)
             down = pltpu.roll(x, B - 1, 0)
             down = jnp.where(row == B - 1, cr[j, (k + 1) * B : (k + 1) * B + 1] if k < NB - 1 else 0.0, down)
-            lcol = lc if j == 0 else pltpu.roll(lc, D - 2, 1)
-            left = jnp.where(lane == 0, lcol, pltpu.roll(x, 1, 1))
-            right = jnp.where(lane == D - 1, pltpu.roll(rc, D - 2 if j == 0 else D - 4, 1), pltpu.roll(x, D - 1, 1))
-            xs.append(cs[j, spot] + c0 * x + c1 * (up + down) + c2 * (left + right))
+            xs.append(cs[j, spot] + c0 * x + c1 * (up + down) + c2 * (pltpu.roll(x, 1, 1) + pltpu.roll(x, D - 1, 1)))
         y = solve_wd(jnp.concatenate(xs, axis=1), gw3, gd4)
         e[0, spot] = y[:B]
         e[1, spot] = y[B:]
+        parts.append(
+            lax.dot_general(
+                comb[:, spot], gwf[...], (((1,), (1,)), ((), ())), precision=HIGHEST, preferred_element_type=f32
+            )
+        )
+    ls, rs = chain_w([a[:, 0:1] for a in parts], [a[:, B - 1 : B] for a in parts], par)
+    for k in range(NB):
+        wc[:, k * B : (k + 1) * B] = parts[k] + ls[k] * rows[0:1] + rs[k] * rows[1:2]
+    line = wc[...]
+    for p in range(NP):
+        out[p, 2 * S :] = pltpu.roll(line, (W - S * p) % W, 1)[:, :D]
     for j in range(2):
         ls, rs = chain_w(
             [e[j, k * B : k * B + 1] for k in range(NB)], [e[j, k * B + B - 1 : k * B + B] for k in range(NB)], par
@@ -367,7 +373,7 @@
         send(i).wait()
 
 
-def planes_kernel(par, ew0, ew1, qp0, qp1, own, from_left, from_right, hmat, rows, gwf, planes, u, fix, flat):
+def planes_kernel(par, ew0, ew1, qp0, qp1, own, hmat, rows, gwf, planes, fix, flat):
     ew = [ew0[k] for k in range(HALF)] + [ew1[k] for k in range(NB - HALF)]
     ls, rs = chain_w([a[0] for a in ew], [a[1] for a in ew], par)
     flat[...] = jnp.zeros((8, H * D), f32)
@@ -378,8 +384,7 @@
         x = flat[...]
         hi = x.astype(bf16).astype(f32)
         fix[k] = jnp.concatenate([hi, x - hi, hi, jnp.zeros_like(x)], axis=0).astype(bf16)
-    v = jnp.concatenate([from_left[H : 2 * H] - own[H : 2 * H], from_right[:H] - own[:H]], axis=0)
-    v = jnp.dot(hmat[:, : 2 * H], v, precision=HIGHEST, preferred_element_type=f32)
+    v = jnp.dot(hmat[:, : 2 * H], own[...], precision=HIGHEST, preferred_element_type=f32)
     parts = []
     for k in range(NB):
         spot = slice(k * B, (k + 1) * B)
@@ -387,60 +392,90 @@
             v[:, spot], gwf[...], (((1,), (1,)), ((), ())), precision=HIGHEST, preferred_element_type=f32
         )
         seen = qp0[:, spot] if k < HALF else qp1[:, (k - HALF) * B : (k - HALF + 1) * B]
-        parts.append(jnp.concatenate([2.0 * solved, seen], axis=0))
+        parts.append(jnp.concatenate([seen, solved], axis=0))
     ls, rs = chain_w([a[:, 0:1] for a in parts], [a[:, B - 1 : B] for a in parts], par)
-    p, q = par[HEAD, 7], par[HEAD, 8]
+    for k in range(NB):
+        planes[:, k * B : (k + 1) * B] = parts[k] + ls[k] * rows[0:1] + rs[k] * rows[1:2]
+
+
+def groups(ref):
+    return [ref[R * k : R * (k + 1)] for k in range(4)]
+
+
+def pair_kernel(par, a, b, known, rim):
+    p, q = 2.0 * par[HEAD, 7], 2.0 * par[HEAD, 8]
+    odd = par[HEAD, 12]
+    even = 1.0 - odd
+    f, t, h0, h1 = groups(a)
+    f2, t2, g0, g1 = groups(b)
+    f = f - p * h1 - q * h0 + (even * q) * g0 + (odd * p) * g1
+    t = t - q * h1 - p * h0 + (even * p) * g0 + (odd * q) * g1
+    f2 = f2 - p * g1 - q * g0 + (odd * q) * h0 + (even * p) * h1
+    t2 = t2 - q * g1 - p * g0 + (odd * p) * h0 + (even * q) * h1
+    total = par[PAIR, 5] * h0 + par[PAIR, 6] * h1 + par[PAIR, 7] * g0 + par[PAIR, 8] * g1
+    for k, v in enumerate((f, t, f2, t2)):
+        known[R * k : R * (k + 1)] = v
+        total = total + par[PAIR, k] * v
+    rim[...] = total
+
+
+def solver_kernel(par, y, out, us, uc):
+    p, q = par[HEAD, 5], par[HEAD, 6]
+    before, inv, w, qw = (BEFORE_H + k for k in range(4))
+    row = iota((8, D), 0)
+
+    def lines(k):
+        c = y[k, 2 * S :]
+        return (y[k, :S], y[k, S : 2 * S]), (c, pltpu.roll(c, 6, 0))
+
+    u = [None, None]
+    for k in range(NP):
+        for n, (first, last) in enumerate(lines(k)):
+            v = last + par[w, k] * first
+            u[n] = v if k == 0 else v + par[qw, k] * u[n]
+        us[k] = u[0]
+        uc[k] = u[1]
+    f = [jnp.zeros((S, D), f32), jnp.zeros((8, D), f32)]
+    for k in reversed(range(NP)):
+        beyond = list(f)
+        inside = [None, None]
+        for n, (first, _) in enumerate(lines(k)):
+            g = first
+            held_u = (us, uc)[n][k - 1] if k > 0 else None
+            if k > 0:
+                g = g + p * held_u
+            f[n] = (g + q * f[n]) * par[inv, k]
+            inside[n] = held_u + par[before, k] * f[n] if k > 0 else jnp.zeros_like(f[n])
+        out[k, :S] = inside[0]
+        out[k, S : 2 * S] = beyond[0]
+        out[k, 2 * S :] = jnp.where(row < 2, inside[1], pltpu.roll(beyond[1], 2, 0))
+
+
+def corner_kernel(a, planes, out, wide):
+    for k in range(4):
+        out[R * k : R * k + H] = planes[H * k : H * (k + 1)]
+    lane = iota((S, D), 1)
+    narrow = iota((8, D), 1)
+    line = jnp.zeros((8, W), f32)
+    blank = jnp.zeros((8, W - D), f32)
+    for p in range(NP):
+        l, r = a[p, :S], a[p, S : 2 * S]
+        v = jnp.where(lane == 0, l, jnp.where(lane == 1, pltpu.roll(r, 1, 1), 0.0))
+        wide[S * p : S * (p + 1)] = jnp.where(
+            lane == 8, pltpu.roll(l, 9, 1), jnp.where(lane == 9, pltpu.roll(r, 10, 1), v)
+        )
+        piece = jnp.concatenate([jnp.where(narrow < S, a[p, 2 * S :], 0.0), blank], axis=1)
+        line = line + pltpu.roll(piece, S * p, 1)
+    row = iota((8, W), 0)
+    out[2 * R + H : 3 * R] = jnp.where(
+        row == 0, pltpu.roll(line, 7, 0), jnp.where(row == 1, pltpu.roll(line, 6, 0), 0.0)
+    )
+    out[3 * R + H :] = jnp.where(row == 0, line, jnp.where(row == 1, pltpu.roll(line, 7, 0), 0.0))
     for k in range(NB):
         spot = slice(k * B, (k + 1) * B)
-        both = parts[k] + ls[k] * rows[0:1] + rs[k] * rows[1:2]
-        ul, ur = both[:H], both[H : 2 * H]
-        u[:, spot] = both[: 2 * H]
-        planes[:H, spot] = both[2 * H : 3 * H] + p * ul + q * ur
-        planes[H:, spot] = both[3 * H :] + q * ul + p * ur
-
-
-def pair_kernel(par, a, b, out):
-    def joined(first, last):
-        return (
-            par[PAIR, 0] * a[first, :] + par[PAIR, 1] * a[last, :] + par[PAIR, 2] * b[first, :] + par[PAIR, 3] * b[last, :]
-        )
-
-    out[:H] = joined(pl.ds(0, H), pl.ds(H, H))
-    out[H:] = jnp.zeros((8, W), f32)
-    for plane in range(2):
-        at = 2 * H + 2 * plane
-        out[H + plane : H + plane + 1] = joined(pl.ds(at + 1, 1), pl.ds(at, 1))
-
-
-def solver_kernel(par, y, out, us):
-    p, q = par[HEAD, 5], par[HEAD, 6]
-    before, inv, w, qw = (BEFORE_H + k for k in range(4))
-    u = y[0, S:] + par[w, 0] * y[0, :S]
-    us[0] = u
-    for k in range(1, NP):
-        u = y[k, S:] + par[w, k] * y[k, :S] + par[qw, k] * u
-        us[k] = u
-    zero = jnp.zeros_like(u)
-    out[NP - 1, S:] = zero
-    f = zero
-    for k in reversed(range(NP)):
-        g = y[k, :S]
-        if k > 0:
-            g = g + p * us[k - 1]
-        f = (g + q * f) * par[inv, k]
-        if k > 0:
-            out[k, :S] = us[k - 1] + par[before, k] * f
-            out[k - 1, S:] = f
-    out[0, :S] = zero
-
-
-def corner_kernel(a, planes, out, wide):
-    out[: 2 * H] = planes[...]
-    lane = iota((S, D), 1)
-    for p in range(NP):
-        wide[S * p : S * (p + 1)] = jnp.where(lane < 2, pltpu.roll(a[p, :S], 1, 1), pltpu.roll(a[p, S:], 3, 1))
-    for k in range(NB):
-        out[2 * H :, k * B : (k + 1) * B] = wide[k * B : (k + 1) * B].T[:8]
+        both = wide[spot].T[:16]
+        out[H:R, spot] = both[:8]
+        out[R + H : 2 * R, spot] = both[8:]
 
 
 def nearly_kernel(par, raw0, raw1, a, out, lr, sems):
@@ -463,27 +498,18 @@
     lax.fori_loop(0, NB, block, 0)
 
 
-def final_kernel(par, base, fix, colm, a, b, v0, v1, u, hcol, spread, out, tall, buf, sems):
+def final_kernel(par, base, fix, colm, a, b, parts, v0, v1, hcol, spread, out, tall, buf, sems):
     beyond = par[HEAD, 10] * v1[...] + par[HEAD, 11] * v0[...]
-
-    def known(first, last, far_row):
-        return (a[first, :], a[last, :], b[first, :], b[last, :], far_row)
-
+    odd = par[HEAD, 12]
+    even = 1.0 - odd
+    _, _, h0, h1 = groups(a)
+    _, _, g0, g1 = groups(b)
     sides = []
-    for side in range(2):
-
-        def mixed(parts):
-            total = 0.0
-            for k, part in enumerate(parts):
-                total = total + par[PAIR + 1 + side, k] * part
-            return total
-
-        own = u[H * side : H * (side + 1)] + mixed(known(pl.ds(0, H), pl.ds(H, H), beyond[:H]))
-        for plane in range(2):
-            at = 2 * H + 2 * plane
-            row = beyond[H + plane : H + plane + 1]
-            own = own + hcol[:, plane : plane + 1] * mixed(known(pl.ds(at + 1, 1), pl.ds(at, 1), row))
-        sides.append(own)
+    for side, start in enumerate(((2.0 * odd) * g1 - 2.0 * h1, (2.0 * even) * g0 - 2.0 * h0)):
+        total = start + par[PAIR + 1 + side, 4] * beyond
+        for k, part in enumerate(groups(parts)):
+            total = total + par[PAIR + 1 + side, k] * part
+        sides.append(total[:H] + hcol[:, 0:1] * total[H : H + 1] + hcol[:, 1:2] * total[H + 1 : H + 2])
     both = jnp.concatenate(sides + [jnp.zeros((D - 2 * H, W), f32)], axis=0)
     for k in range(NB):
         tall[k * B : (k + 1) * B] = both[:, k * B : (k + 1) * B].T
@@ -536,15 +562,17 @@
 def per_device(density, source, coupling, width_inverse, height_inverse, depth_inverse):
     slab = lax.axis_index("slab")
     slabs = lax.axis_size("slab")
-    up = [(k, k + 1) for k in range(slabs - 1)]
-    down = [(k + 1, k) for k in range(slabs - 1)]
+
+    def across(value, pairs):
+        return lax.ppermute(value, "slab", pairs)
+
     grid = [pltpu.VMEM((H, W + 8, D), f32)]
 
-    cr, cs, halo = pl.pallas_call(
+    cr, cs, own, comb = pl.pallas_call(
         sums_kernel,
-        in_specs=[HBM, HBM, HBM],
-        out_specs=[VMEM] * 3,
-        out_shape=[held(2, W, D), held(2, W, D), held(2 * H + 8, W)],
+        in_specs=[HBM] * 3,
+        out_specs=[VMEM] * 4,
+        out_shape=[held(2, W, D), held(2, W, D), held(2 * H, W), held(8, W)],
         scratch_shapes=grid * 2
         + [
             pltpu.VMEM((H, 8, 128), f32),
@@ -557,9 +585,6 @@
         name="sums",
         cost_estimate=cost(10**7, 14 * 10**6),
     )(far(coupling), far(density), far(source))
-    halo_left = lax.ppermute(halo, "slab", up)
-    halo_right = lax.ppermute(halo, "slab", down)
-
     first = pl.BlockSpec((1, B, B), lambda *_: (0, 0, 0))
     shapes = [
         ((16, 128), f32),
@@ -586,14 +611,14 @@
 
     edges = pl.pallas_call(
         edges_kernel,
-        in_specs=[SMEM] + [VMEM] * 7,
+        in_specs=[SMEM] + [VMEM] * 8,
         out_specs=VMEM,
-        out_shape=held(NP, 2 * S, D),
-        scratch_shapes=[pltpu.VMEM((2, W, D), f32)],
+        out_shape=held(NP, 2 * S + 8, D),
+        scratch_shapes=[pltpu.VMEM((2, W, D), f32), pltpu.VMEM((8, W), f32)],
         compiler_params=limit(8),
         name="edges",
         cost_estimate=cost(10**8, 3 * 10**6),
-    )(par, near(cr), near(cs), near(halo_left), near(halo_right), near(gw3), near(gd4), near(cols))
+    )(par, near(cr), near(cs), near(comb), near(gwf), near(rows), near(gw3), near(gd4), near(cols))
     arrived = lax.all_to_all(edges, "pencil", 0, 0, tiled=True)
 
     def field(start, count):
@@ -621,8 +646,8 @@
         solver_kernel,
         in_specs=[SMEM, VMEM],
         out_specs=VMEM,
-        out_shape=held(NP, 2 * S, D),
-        scratch_shapes=[pltpu.VMEM((NP, S, D), f32)],
+        out_shape=held(NP, 2 * S + 8, D),
+        scratch_shapes=[pltpu.VMEM((NP, S, D), f32), pltpu.VMEM((NP, 8, D), f32)],
         compiler_params=limit(8),
         name="solver",
         cost_estimate=cost(10**6, 2 * 10**6),
@@ -630,43 +655,39 @@
     outside = lax.all_to_all(solved, "pencil", 0, 0, tiled=True)
 
     raw1, ew1, qp1 = field(HALF, NB - HALF)
-    planes, u, fix = pl.pallas_call(
+    planes, fix = pl.pallas_call(
         planes_kernel,
-        in_specs=[SMEM] + [VMEM] * 10,
-        out_specs=[VMEM] * 3,
-        out_shape=[held(2 * H, W), held(2 * H, W), held(NB, 32, H * D, dtype=bf16)],
+        in_specs=[SMEM] + [VMEM] * 8,
+        out_specs=[VMEM] * 2,
+        out_shape=[held(4 * H, W), held(NB, 32, H * D, dtype=bf16)],
         scratch_shapes=[pltpu.VMEM((8, H * D), f32)],
         compiler_params=limit(8),
         name="planes",
         cost_estimate=cost(10**8, 10**6),
-    )(par, *[near(v) for v in (ew0, ew1, qp0, qp1)], near(halo), near(halo_left), near(halo_right), near(hmat), near(rows), near(gwf))
+    )(par, *[near(v) for v in (ew0, ew1, qp0, qp1)], near(own), near(hmat), near(rows), near(gwf))
 
     outside = near(outside)
     corners = pl.pallas_call(
         corner_kernel,
         in_specs=[VMEM] * 2,
         out_specs=VMEM,
-        out_shape=held(2 * H + 8, W),
+        out_shape=held(4 * R, W),
         scratch_shapes=[pltpu.VMEM((W, D), f32)],
         compiler_params=limit(8),
         name="corner",
         cost_estimate=cost(10**6, 10**6),
     )(outside, near(planes))
-
-    def across(value, d):
-        return lax.ppermute(value, "slab", [(k, k ^ d) for k in range(slabs)])
-
-    beside = across(corners, 1)
-    rim = pl.pallas_call(
+    beside = across(corners, [(k, k ^ 1) for k in range(slabs)])
+    parts, rim = pl.pallas_call(
         pair_kernel,
         in_specs=[SMEM] + [VMEM] * 2,
-        out_specs=VMEM,
-        out_shape=held(H + 8, W),
+        out_specs=[VMEM] * 2,
+        out_shape=[held(4 * R, W), held(R, W)],
         compiler_params=limit(8),
         name="pair",
         cost_estimate=cost(10**5, 10**5),
     )(par, near(corners), near(beside))
-    far_rim = across(rim, 2)
+    far_rim = across(rim, [(k, k ^ 2) for k in range(slabs)])
     base = pl.pallas_call(
         nearly_kernel,
         in_specs=[SMEM, HBM, HBM, VMEM],
@@ -693,9 +714,9 @@
         near(colm),
         near(corners),
         near(beside),
+        near(parts),
         near(rim),
         near(far_rim),
-        near(u),
         near(hcol),
         near(spread),
     )

time: 73.7 us -> 69.7 us (0.946)
  starting transfers between devices: 25.8 us -> 20.2 us
  waiting for transfers between devices: 6.34 us -> 7.83 us
    ppermute x4 -> x2, starting transfers between devices: 11.9 us -> 5.76 us  [across(): return lax.ppermute(value, 'slab', pairs)]
    all_to_all x1, waiting for transfers between devices: 2.45 us -> 4.6 us  [per_device(): arrived = lax.all_to_all(edges, 'pencil', 0, 0, tiled=True)]
    ppermute x4 -> x2, waiting for transfers between devices: 2.33 us -> 1.21 us  [across(): return lax.ppermute(value, 'slab', pairs)]
    all_to_all x1, starting transfers between devices: 8.66 us -> 9.71 us  [per_device(): arrived = lax.all_to_all(edges, 'pencil', 0, 0, tiled=True)]
  transfers between devices with their start and end apart: 6 -> 4, of which waited for: 4 -> 3; matrix products, arithmetic and copies ran while one was open for 0% -> 0% of each run, Pallas kernels for 35% -> 35%
where the time goes in v5:
time: 69.7 us; the launch traced here: 69.4 us
  Pallas kernels  41.3 us (59%)
  starting transfers between devices  20.2 us (29%)
  waiting for transfers between devices  7.83 us (11%)
    pallas_call x2, Pallas kernels, field(): pl.pallas_call(partial(field_kernel, start, count), in_specs=[SMEM, HBM,...  18.8 us
    all_to_all x1, starting transfers between devices, per_device(): arrived = lax.all_to_all(edges, 'pencil', 0, 0, tiled=True)  9.71 us
    ppermute x2, starting transfers between devices, across(): return lax.ppermute(value, 'slab', pairs)  5.76 us
    pallas_call x1, Pallas kernels, per_device(): pl.pallas_call(sums_kernel, in_specs=[HBM] * 3, out_specs=[VMEM] * 4, out...  5.21 us
    all_to_all x1, starting transfers between devices, per_device(): outside = lax.all_to_all(solved, 'pencil', 0, 0, tiled=True)  4.72 us
    all_to_all x1, waiting for transfers between devices, per_device(): arrived = lax.all_to_all(edges, 'pencil', 0, 0, tiled=True)  4.6 us
    pallas_call x1, Pallas kernels, per_device(): pl.pallas_call(final_kernel, in_specs=[SMEM] + [VMEM] * 10, out_specs=HBM...  4.06 us
    pallas_call x1, Pallas kernels, per_device(): pl.pallas_call(nearly_kernel, in_specs=[SMEM, HBM, HBM, VMEM], out_specs=...  3.66 us
  transfers between devices with their start and end apart: 4, of which 3 were waited for; matrix products, arithmetic and copies ran while one was open for 0% of the time, Pallas kernels for 35%

profile of v5, /device:TPU:1, one launch (start us, length us, event | category | flops | bytes accessed | tf_op | source)
XLA Modules:
  0.0 69.4 jit_solution(15300162119792609298)
XLA Ops:
  0.0 0.0 copy-start
  0.0 0.0 copy-start.1
  0.0 0.0 copy-start.2
  0.0 5.2 %sums.1 = (f32[2,768,128]{2,1,0:T(8,128)S(1)}, f32[2,768,128]{2,1,0:T(8,128)S(1)}, f32[32,768]{1,0:T(8,128)S(1)}, f32[8,768]{1,0:T(8,128)S(1)}) custom-call(f32[3]{0:T(128)} %cpl_far.1, f32[16,768,128]{2,1,0:T(8,128)} %rho.5, f32[16,768,128]{2,1,0:T(8,128)} %sig.5), custom_call_target="tpu_custom_call" | custom-call | flops 10000000 | bytes 14000000 | tf_op jit(solution)/shard_map/sums/pallas_call | solution.py:571
  5.2 0.0 copy-done
  5.2 0.0 copy-done.1
  5.2 0.0 copy-done.2
  5.3 0.8 %tables.1 = (f32[16,128]{1,0:T(8,128)S(1)}, f32[2,128,128]{2,1,0:T(8,128)S(1)}, f32[8,128]{1,0:T(8,128)S(1)}, bf16[128,384]{1,0:T(8,128)(2,1)S(1)}, bf16[256,256...) custom-call(f32[3]{0:T(128)S(1)} %copy-done.2, ...), custom_call_target="tpu_custom_call" | custom-call | flops 10000000 | bytes 1000000 | tf_op jit(solution)/shard_map/tables/pallas_call | solution.py:601
  6.1 3.6 %edges.1 = f32[32,56,128]{2,1,0:T(8,128)} custom-call(f32[16,128]{1,0:T(8,128)S(1)} %get-tuple-element.31.par, f32[2,768,128]{2,1,0:T(8,128)S(1)} %get-tuple-element.36.cr, f32[2,768,128]{2,1,0:T(8,128)S(1)} %get-tuple-element.37.cs, f32[8,768]{1,0:T(8,128)S(1)} %get-tuple-element.38.comb, f32[128,128]{1,0:T(8,128)S(1)} %get-tuple-element.39.gwf, ...), custom_call_target="tpu_custom_call" | custom-call | flops 100000000 | bytes 3000000 | tf_op jit(solution)/shard_map/edges/pallas_call | solution.py:612
  9.6 9.7 %all-to-all-start = ((f32[32,56,128]{2,1,0:T(8,128)}), f32[32,56,128]{2,1,0:T(8,128)S(1)}, u32[]{:S(2)}, u32[]{:S(2)}) async-start(f32[32,56,128]{2,1,0:T(8,128)} %edges.1), calls=%async_computation | async-start | bytes 1835008 | tf_op jit(solution)/shard_map/all_to_all | solution.py:622
  19.4 9.4 %field0.1 = (f32[16,384,128]{2,1,0:T(8,128)}, f32[3,2,16,128]{3,2,1,0:T(8,128)S(1)}, f32[32,384]{1,0:T(8,128)S(1)}) custom-call(f32[16,128]{1,0:T(8,128)S(1)} %get-tuple-element.31.par, f32[16,768,128]{2,1,0:T(8,128)} %rho.5, f32[16,768,128]{2,1,0:T(8,128)} %sig.5, bf16[128,384]{1,0:T(8,128)(2,1)S(1)} %get-tuple-element.32.gw3, ...), custom_call_target="tpu_custom_call" | custom-call | flops 2000000000 | bytes 10000000 | tf_op jit(solution)/shard_map/field0/pallas_call | solution.py:626
  28.7 4.6 %all-to-all-done.y = f32[32,56,128]{2,1,0:T(8,128)S(1)} async-done(((f32[32,56,128]{2,1,0:T(8,128)}), f32[32,56,128]{2,1,0:T(8,128)S(1)}, u32[]{:S(2)}, u32[]{:S(2)}) %all-to-all-start) | async-done | bytes 917536 | tf_op jit(solution)/shard_map/all_to_all | solution.py:622
  33.3 1.8 %solver.1 = f32[32,56,128]{2,1,0:T(8,128)} custom-call(f32[16,128]{1,0:T(8,128)S(1)} %get-tuple-element.31.par, f32[32,56,128]{2,1,0:T(8,128)S(1)} %all-to-all-done.y), custom_call_target="tpu_custom_call" | custom-call | flops 1000000 | bytes 2000000 | tf_op jit(solution)/shard_map/solver/pallas_call | solution.py:645
  35.2 4.7 %all-to-all-start.1 = ((f32[32,56,128]{2,1,0:T(8,128)}), f32[32,56,128]{2,1,0:T(8,128)S(1)}, u32[]{:S(2)}, u32[]{:S(2)}) async-start(f32[32,56,128]{2,1,0:T(8,128)} %solver.1), calls=%async_computation.1 | async-start | bytes 1835008 | tf_op jit(solution)/shard_map/all_to_all | solution.py:655
  39.9 9.4 %field3.1 = (f32[16,384,128]{2,1,0:T(8,128)}, f32[3,2,16,128]{3,2,1,0:T(8,128)S(1)}, f32[32,384]{1,0:T(8,128)S(1)}) custom-call(f32[16,128]{1,0:T(8,128)S(1)} %get-tuple-element.31.par, f32[16,768,128]{2,1,0:T(8,128)} %rho.5, f32[16,768,128]{2,1,0:T(8,128)} %sig.5, bf16[128,384]{1,0:T(8,128)(2,1)S(1)} %get-tuple-element.32.gw3, ...), custom_call_target="tpu_custom_call" | custom-call | flops 2000000000 | bytes 10000000 | tf_op jit(solution)/shard_map/field3/pallas_call | solution.py:626
  49.3 2.0 %planes.1 = (f32[64,768]{1,0:T(8,128)S(1)}, bf16[6,32,2048]{2,1,0:T(8,128)(2,1)S(1)}) custom-call(f32[16,128]{1,0:T(8,128)S(1)} %get-tuple-element.31.par, f32[3,2,16,128]{3,2,1,0:T(8,128)S(1)} %get-tuple-element.44.ew0, f32[3,2,16,128]{3,2,1,0:T(8,128)S(1)} %get-tuple-element.45.ew1, f32[32,384]{1,0:T(8,128)S(1)} %get-tuple-element.46.qp0, ...), custom_call_target="tpu_custom_call" | custom-call | flops 100000000 | bytes 1000000 | tf_op jit(solution)/shard_map/planes/pallas_call | solution.py:658
  51.4 2.0 %all-to-all-done.1.a = f32[32,56,128]{2,1,0:T(8,128)S(1)} async-done(((f32[32,56,128]{2,1,0:T(8,128)}), f32[32,56,128]{2,1,0:T(8,128)S(1)}, u32[]{:S(2)}, u32[]{:S(2)}) %all-to-all-start.1) | async-done | bytes 917536 | tf_op jit(solution)/shard_map/all_to_all | solution.py:655
  53.4 0.5 corner.1.a
  53.9 3.1 %collective-permute-start = (f32[96,768]{1,0:T(8,128)S(1)}, f32[96,768]{1,0:T(8,128)S(1)}, u32[]{:S(2)}, u32[]{:S(2)}) collective-permute-start(f32[96,768]{1,0:T(8,128)S(1)} %corner.1.a), channel_id=1, source_target_pairs={{0,32},{32,0},{64,96},{96,64},{1,33},{33,1},{65,97},{97,65},{2,34}... | collective-permute-start | bytes 884744 | tf_op jit(solution)/shard_map/ppermute | solution.py:567
  57.0 1.2 %collective-permute-done.b = f32[96,768]{1,0:T(8,128)S(1)} collective-permute-done((f32[96,768]{1,0:T(8,128)S(1)}, f32[96,768]{1,0:T(8,128)S(1)}, u32[]{:S(2)}, u32[]{:S(2)}) %collective-permute-start) | collective-permute-done | bytes 294944 | tf_op jit(solution)/shard_map/ppermute | solution.py:567
  58.2 0.8 %pair.1 = (f32[96,768]{1,0:T(8,128)S(1)}, f32[24,768]{1,0:T(8,128)S(1)}) custom-call(f32[16,128]{1,0:T(8,128)S(1)} %get-tuple-element.31.par, f32[96,768]{1,0:T(8,128)S(1)} %corner.1.a, f32[96,768]{1,0:T(8,128)S(1)} %collective-permute-done.b), custom_call_target="tpu_custom_call" | custom-call | flops 100000 | bytes 100000 | tf_op jit(solution)/shard_map/pair/pallas_call | solution.py:681
  59.0 2.7 %collective-permute-start.1 = (f32[24,768]{1,0:T(8,128)S(1)}, f32[24,768]{1,0:T(8,128)S(1)}, u32[]{:S(2)}, u32[]{:S(2)}) collective-permute-start(f32[24,768]{1,0:T(8,128)S(1)} %get-tuple-element.54.v0), channel_id=1, source_target_pairs={{0,64},{32,96},{64,0},{96,32},{1,65},{33,97},{65,1},{97,33},{2,66}... | collective-permute-start | bytes 221192 | tf_op jit(solution)/shard_map/ppermute | solution.py:567
  61.7 3.7 %nearly.1.base = f32[16,768,128]{2,1,0:T(8,128)S(1)} custom-call(f32[16,128]{1,0:T(8,128)S(1)} %get-tuple-element.31.par, f32[16,384,128]{2,1,0:T(8,128)} %get-tuple-element.34.raw0, f32[16,384,128]{2,1,0:T(8,128)} %get-tuple-element.35.raw1, f32[32,56,128]{2,1,0:T(8,128)S(1)} %all-to-all-done.1.a), custom_call_target="tpu_custom_call" | custom-call | flops 100000000 | bytes 7000000 | tf_op jit(solution)/shard_map/nearly/pallas_call | solution.py:691
  65.4 0.0 collective-permute-done.1.v1
  65.4 4.1 %final.1 = f32[16,768,128]{2,1,0:T(8,128)} custom-call(f32[16,128]{1,0:T(8,128)S(1)} %get-tuple-element.31.par, f32[16,768,128]{2,1,0:T(8,128)S(1)} %nearly.1.base, bf16[6,32,2048]{2,1,0:T(8,128)(2,1)S(1)} %get-tuple-element.50.fix, bf16[128,32]{1,0:T(8,128)(2,1)S(1)} %get-tuple-element.51.colm, f32[96,768]{1,0:T(8,128)S(1)} %corner.1.a, ...), custom_call_target="tpu_custom_call" | custom-call | flops 1000000000 | bytes 13000000 | tf_op jit(solution)/shard_map/final/pallas_call | solution.py:701
Async XLA Ops:
  0.0 5.2 %copy-start = (f32[6,128,128]{2,1,0:T(8,128)S(1)}, f32[6,128,128]{2,1,0:T(8,128)}, u32[]{:S(2)}) copy-start(f32[6,128,128]{2,1,0:T(8,128)} %wi.1) | copy-start | bytes 1179652
  0.0 5.2 %copy-start.1 = (f32[4,128,128]{2,1,0:T(8,128)S(1)}, f32[4,128,128]{2,1,0:T(8,128)}, u32[]{:S(2)}) copy-start(f32[4,128,128]{2,1,0:T(8,128)} %di.1) | copy-start | bytes 786436
  0.0 5.2 %copy-start.2 = (f32[3]{0:T(128)S(1)}, f32[3]{0:T(128)}, u32[]{:S(2)}) copy-start(f32[3]{0:T(128)} %cpl_far.1) | copy-start | bytes 40
  9.6 23.7 %all-to-all-start = ((f32[32,56,128]{2,1,0:T(8,128)}), f32[32,56,128]{2,1,0:T(8,128)S(1)}, u32[]{:S(2)}, u32[]{:S(2)}) async-start(f32[32,56,128]{2,1,0:T(8,128)} %edges.1), calls=%async_computation | async-start | bytes 1835008 | tf_op jit(solution)/shard_map/all_to_all | solution.py:622
  35.2 18.2 %all-to-all-start.1 = ((f32[32,56,128]{2,1,0:T(8,128)}), f32[32,56,128]{2,1,0:T(8,128)S(1)}, u32[]{:S(2)}, u32[]{:S(2)}) async-start(f32[32,56,128]{2,1,0:T(8,128)} %solver.1), calls=%async_computation.1 | async-start | bytes 1835008 | tf_op jit(solution)/shard_map/all_to_all | solution.py:655
  53.9 4.3 %collective-permute-start = (f32[96,768]{1,0:T(8,128)S(1)}, f32[96,768]{1,0:T(8,128)S(1)}, u32[]{:S(2)}, u32[]{:S(2)}) collective-permute-start(f32[96,768]{1,0:T(8,128)S(1)} %corner.1.a), channel_id=1, source_target_pairs={{0,32},{32,0},{64,96},{96,64},{1,33},{33,1},{65,97},{97,65},{2,34}... | collective-permute-start | bytes 884744 | tf_op jit(solution)/shard_map/ppermute | solution.py:567
  59.0 6.4 %collective-permute-start.1 = (f32[24,768]{1,0:T(8,128)S(1)}, f32[24,768]{1,0:T(8,128)S(1)}, u32[]{:S(2)}, u32[]{:S(2)}) collective-permute-start(f32[24,768]{1,0:T(8,128)S(1)} %get-tuple-element.54.v0), channel_id=1, source_target_pairs={{0,64},{32,96},{64,0},{96,32},{1,65},{33,97},{65,1},{97,33},{2,66}... | collective-permute-start | bytes 221192 | tf_op jit(solution)/shard_map/ppermute | solution.py:567
